TPU v7x, 32 devices: a whole 2x2x4 slice. The times are simulated.
32 devices in a mesh: genome: 16 (over z, x, core), samples: 2 (over y).
Axes of the slice: x: 2, y: 2, z: 4, core: 2. Of those that a mesh axis runs over, the one named last changes fastest.
Arguments:
- haplotypes: bfloat16 [4096, 16384], P('samples', 'genome'), may hold values from 0 to 1
- window_ends: int32 [16384], P(('genome', 'samples')), may hold values from 1 to 16384, as said below
Outputs:
- ld_score: float32 [16384], P(('genome', 'samples'))
- profile: float32 [2, 16384], P(None, ('genome', 'samples'))
Inputs may be any that keep to these rules, and one draw needn't show every extreme that they name: window_ends[v] - v lies between 1 and 1024 for every variant v, and equals 1024 at v = 0.
All inputs are finite; a program needn't handle non-finite values.
Results may differ from a plain program's by a relative error of at most 0.0013.
Values may be sent and summed in bfloat16 or wider, within the bound.
No kernel may reach another device: no remote copies, remote signals or barrier semaphores. Data moves between devices by JAX's collectives and lax.ppermute only.
A program may use at most 64 MiB of HBM per device.

v0:
```python
import math

import jax
import jax.numpy as jnp
from jax import lax
from jax.sharding import PartitionSpec as P

WIN = 1024
TILE = 128


variance_floor = 0.01


def from_behind(block, axis, distance):
    devices = range(lax.axis_size(axis))
    route = [(i - distance, i) for i in devices if i - distance in devices]
    return lax.ppermute(block, axis, route)


def carried_in(x, axis, combine, identity):
    peers, position = (lax.axis_size(axis), lax.axis_index(axis))
    everything = jax.tree.map(lambda part: lax.all_gather(part, axis), x)
    start = jax.tree.map(
        lambda part, zero: jnp.broadcast_to(jnp.asarray(zero, part.dtype), part.shape), x, identity
    )

    def lap(k, before):
        reached = k < position
        new = combine(before, jax.tree.map(lambda part: part[k], everything))
        return jax.tree.map(lambda a, b: jnp.where(reached, a, b), new, before)

    return lax.fori_loop(0, peers, lap, start)


def standardize(alleles, frequency, inverse_sd):
    return ((alleles.astype(jnp.float32) - frequency) * inverse_sd).astype(jnp.bfloat16)


def transpose_product(left_side, right_side):
    return lax.dot_general(
        left_side, right_side, (((0,), (0,)), ((), ())), preferred_element_type=jnp.float32
    )


def window_mean(cross_sum, haplo_total, row_position, column_position, window_end):
    correlation = cross_sum / haplo_total
    inside = (column_position > row_position[:, None]) & (column_position < window_end[:, None])
    squares = jnp.sum(
        jnp.where(inside, correlation * correlation, jnp.zeros_like(correlation)), axis=1
    )
    counted = jnp.maximum(window_end - row_position - 1, 1).astype(jnp.float32)
    return squares / counted


def per_device(haplotypes, window_ends):
    sample_count = lax.axis_size("samples")
    genome_count = lax.axis_size("genome")
    block_width = haplotypes.shape[1]
    share_rows = block_width // sample_count
    haplo_total = float(haplotypes.shape[0] * sample_count)
    counts = lax.psum(jnp.sum(haplotypes, axis=0, dtype=jnp.float32), "samples")
    frequency = counts / haplo_total
    inverse_sd = lax.rsqrt(jnp.maximum(frequency * (1.0 - frequency), variance_floor))
    standard = standardize(haplotypes, frequency, inverse_sd)
    next_edge = from_behind(standard, "genome", -1)
    extended = jnp.concatenate([standard, next_edge], axis=1)
    sample_index = lax.axis_index("samples")
    genome_index = lax.axis_index("genome")
    row_position = sample_index * share_rows + jnp.arange(share_rows, dtype=jnp.int32)

    def single(tile_index):
        tile_start = tile_index * TILE
        row_block = lax.dynamic_slice_in_dim(standard, tile_start, TILE, 1)
        column_block = lax.dynamic_slice_in_dim(extended, tile_start, TILE + WIN, 1)
        return transpose_product(row_block, column_block)

    tiles = lax.map(
        single, jnp.arange(share_rows * lax.axis_size("samples") // TILE, dtype=jnp.int32)
    )
    cross_sum = lax.psum_scatter(
        tiles.reshape(share_rows * lax.axis_size("samples"), TILE + WIN),
        "samples",
        scatter_dimension=0,
        tiled=True,
    )
    column_position = (
        row_position[:, None] // TILE * TILE + jnp.arange(TILE + WIN, dtype=jnp.int32)[None, :]
    )
    window_end = window_ends - genome_index * block_width
    ld_score = window_mean(cross_sum, haplo_total, row_position, column_position, window_end)
    log_rates = jnp.array(
        [math.log(0.5) / (4 * share_rows), math.log(0.1) / (block_width * genome_count)],
        jnp.float32,
    )
    steps_index = jnp.arange(share_rows, dtype=jnp.float32)
    lag_steps = steps_index[:, None] - steps_index[None, :]
    decay_matrix = jnp.where(
        lag_steps[None] >= 0.0,
        jnp.exp(jnp.maximum(lag_steps, 0.0)[None] * log_rates[:, None, None]),
        0.0,
    )
    local_sums = jnp.einsum("ktu,u->kt", decay_matrix, ld_score, precision=lax.Precision.HIGHEST)

    def combine(earlier, later):
        return (earlier[0] * jnp.exp(later[1] * log_rates) + later[0], earlier[1] + later[1])

    identity = (jnp.zeros(2, jnp.float32), jnp.zeros((), jnp.float32))
    element = (local_sums[:, -1], jnp.full((), share_rows, jnp.float32))
    group_prefix = carried_in(element, "samples", combine, identity)
    remaining = ((sample_count - 1 - sample_index) * share_rows).astype(jnp.float32)
    group_total = lax.psum(local_sums[:, -1] * jnp.exp(remaining * log_rates), "samples")
    outer_prefix = carried_in(
        (group_total, jnp.full((), share_rows * sample_count, jnp.float32)),
        "genome",
        combine,
        identity,
    )
    incoming = combine(outer_prefix, group_prefix)
    smoothed = local_sums + incoming[0][:, None] * jnp.exp(
        (steps_index[None, :] + 1.0) * log_rates[:, None]
    )
    position = (genome_index * block_width + row_position).astype(jnp.float32) + 1.0
    profile = (
        smoothed
        * (-jnp.expm1(log_rates))[:, None]
        / -jnp.expm1(position[None, :] * log_rates[:, None])
    )
    return (ld_score, profile)


def solution(mesh):
    placed = (P("samples", "genome"), P(("genome", "samples")))
    return jax.shard_map(
        per_device,
        mesh=mesh,
        in_specs=placed,
        out_specs=(P(("genome", "samples")), P(None, ("genome", "samples"))),
        check_vma=False,
    )
```

profile of v0, /device:TPU:0, one launch (start us, length us, event | category | flops | bytes accessed | tf_op | source)
XLA Modules:
  0.0 249.5 jit_solution(747514324755722235)
XLA Ops:
  7.2 2.9 %convert_reduce_fusion = f32[1024]{0:T(1024)S(1)} fusion(bf16[2048,1024]{1,0:T(8,128)(2,1)} %param.9), kind=kLoop, calls=%fused_computation.13 | loop fusion | flops 4193280 | bytes 4198400 | tf_op jit(solution)/shard_map/reduce_sum | solution.py:62
  10.1 5.9 %psum.14 = f32[1024]{0:T(1024)S(1)} all-reduce(f32[1024]{0:T(1024)S(1)} %convert_reduce_fusion), channel_id=1, replica_groups=mesh['genome'=16,'samples'=2] {'samples'}, use_global_device_ids=true, to_apply=%region_1.0 | all-reduce | flops 1024 | bytes 8192 | tf_op jit(solution)/shard_map/psum | solution.py:62
  16.0 5.4 %fusion.11 = bf16[2048,1024]{1,0:T(8,128)(2,1)} fusion(bf16[2048,1024]{1,0:T(8,128)(2,1)} %param.9, f32[1024]{0:T(1024)S(1)} %get-tuple-element.391, f32[1024]{0:T(1024)S(1)} %get-tuple-element.390), kind=kLoop, calls=%fused_computation.15 | loop fusion | flops 8388608 | bytes 8396800 | tf_op jit(solution)/shard_map/convert_element_type | solution.py:37
  21.4 1.3 collective-permute-start
  22.7 8.1 %collective-permute-done = bf16[2048,1024]{1,0:T(8,128)(2,1)} collective-permute-done((bf16[2048,1024]{1,0:T(8,128)(2,1)}, bf16[2048,1024]{1,0:T(8,128)(2,1)}, u32[]{:S(2)}, u32[]{:S(2)}) %collective-permute-start) | collective-permute-done | bytes 4194336 | tf_op jit(solution)/shard_map/ppermute | solution.py:18
  30.8 8.1 %pad_maximum_fusion = bf16[2048,2048]{1,0:T(8,128)(2,1)} fusion(bf16[2048,1024]{1,0:T(8,128)(2,1)} %collective-permute-done, bf16[2048,1024]{1,0:T(8,128)(2,1)} %fusion.11), kind=kLoop, calls=%fused_computation.16 | loop fusion | flops 16777216 | bytes 16777216 | tf_op jit(solution)/shard_map/concatenate | solution.py:67
  38.9 44.0 %while.42 = (s32[]{:T(128)}, f32[8,128,1152]{2,1,0:T(8,128)}, s32[8]{0:T(128)S(1)}, bf16[2048,1024]{1,0:T(8,128)(2,1)}, bf16[2048,2048]{1,0:T(8,128)(2,1)}, /*in...) while((s32[]{:T(128)}, f32[8,128,1152]{2,1,0:T(8,128)}, s32[8]{0:T(128)S(1)}, ...), condition=%wide.region_3.4_spmd, body=%wide.region_2.3_spmd.sunk | while | flops 603979776 | bytes 5833408 | solution.py:78
  40.2 4.3 %fusion.38 = f32[8,128,1152]{2,1,0:T(8,128)} fusion(f32[8,128,1152]{2,1,0:T(8,128)} %get-tuple-element.506, s32[]{:T(128)} %get-tuple-element.505, bf16[2048,2048]{1,0:T(8,128)(2,1)} %get-tuple-element.519, s32[]{:T(128)S(6)} %select_n.109, bf16[2048,1024]{1,0:T(8,128)(2,1)} %get-tuple-element.518, s32[]{:T(128)S(6)} %select_n.110), kind=kOutput, calls=%fused_computation.3.clone.1 | convolution fusion | flops 603979776 | bytes 5833224 | tf_op jit(solution)/shard_map/while/body/eval_jaxpr/dot_general | solution.py:41
  45.7 4.3 %fusion.38 = f32[8,128,1152]{2,1,0:T(8,128)} fusion(f32[8,128,1152]{2,1,0:T(8,128)} %get-tuple-element.506, s32[]{:T(128)} %get-tuple-element.505, bf16[2048,2048]{1,0:T(8,128)(2,1)} %get-tuple-element.519, s32[]{:T(128)S(6)} %select_n.109, bf16[2048,1024]{1,0:T(8,128)(2,1)} %get-tuple-element.518, s32[]{:T(128)S(6)} %select_n.110), kind=kOutput, calls=%fused_computation.3.clone.1 | convolution fusion | flops 603979776 | bytes 5833224 | tf_op jit(solution)/shard_map/while/body/eval_jaxpr/dot_general | solution.py:41
  51.2 4.2 %fusion.38 = f32[8,128,1152]{2,1,0:T(8,128)} fusion(f32[8,128,1152]{2,1,0:T(8,128)} %get-tuple-element.506, s32[]{:T(128)} %get-tuple-element.505, bf16[2048,2048]{1,0:T(8,128)(2,1)} %get-tuple-element.519, s32[]{:T(128)S(6)} %select_n.109, bf16[2048,1024]{1,0:T(8,128)(2,1)} %get-tuple-element.518, s32[]{:T(128)S(6)} %select_n.110), kind=kOutput, calls=%fused_computation.3.clone.1 | convolution fusion | flops 603979776 | bytes 5833224 | tf_op jit(solution)/shard_map/while/body/eval_jaxpr/dot_general | solution.py:41
  56.7 4.3 %fusion.38 = f32[8,128,1152]{2,1,0:T(8,128)} fusion(f32[8,128,1152]{2,1,0:T(8,128)} %get-tuple-element.506, s32[]{:T(128)} %get-tuple-element.505, bf16[2048,2048]{1,0:T(8,128)(2,1)} %get-tuple-element.519, s32[]{:T(128)S(6)} %select_n.109, bf16[2048,1024]{1,0:T(8,128)(2,1)} %get-tuple-element.518, s32[]{:T(128)S(6)} %select_n.110), kind=kOutput, calls=%fused_computation.3.clone.1 | convolution fusion | flops 603979776 | bytes 5833224 | tf_op jit(solution)/shard_map/while/body/eval_jaxpr/dot_general | solution.py:41
  62.2 4.2 %fusion.38 = f32[8,128,1152]{2,1,0:T(8,128)} fusion(f32[8,128,1152]{2,1,0:T(8,128)} %get-tuple-element.506, s32[]{:T(128)} %get-tuple-element.505, bf16[2048,2048]{1,0:T(8,128)(2,1)} %get-tuple-element.519, s32[]{:T(128)S(6)} %select_n.109, bf16[2048,1024]{1,0:T(8,128)(2,1)} %get-tuple-element.518, s32[]{:T(128)S(6)} %select_n.110), kind=kOutput, calls=%fused_computation.3.clone.1 | convolution fusion | flops 603979776 | bytes 5833224 | tf_op jit(solution)/shard_map/while/body/eval_jaxpr/dot_general | solution.py:41
  67.7 4.2 %fusion.38 = f32[8,128,1152]{2,1,0:T(8,128)} fusion(f32[8,128,1152]{2,1,0:T(8,128)} %get-tuple-element.506, s32[]{:T(128)} %get-tuple-element.505, bf16[2048,2048]{1,0:T(8,128)(2,1)} %get-tuple-element.519, s32[]{:T(128)S(6)} %select_n.109, bf16[2048,1024]{1,0:T(8,128)(2,1)} %get-tuple-element.518, s32[]{:T(128)S(6)} %select_n.110), kind=kOutput, calls=%fused_computation.3.clone.1 | convolution fusion | flops 603979776 | bytes 5833224 | tf_op jit(solution)/shard_map/while/body/eval_jaxpr/dot_general | solution.py:41
  73.1 4.2 %fusion.38 = f32[8,128,1152]{2,1,0:T(8,128)} fusion(f32[8,128,1152]{2,1,0:T(8,128)} %get-tuple-element.506, s32[]{:T(128)} %get-tuple-element.505, bf16[2048,2048]{1,0:T(8,128)(2,1)} %get-tuple-element.519, s32[]{:T(128)S(6)} %select_n.109, bf16[2048,1024]{1,0:T(8,128)(2,1)} %get-tuple-element.518, s32[]{:T(128)S(6)} %select_n.110), kind=kOutput, calls=%fused_computation.3.clone.1 | convolution fusion | flops 603979776 | bytes 5833224 | tf_op jit(solution)/shard_map/while/body/eval_jaxpr/dot_general | solution.py:41
  78.6 4.3 %fusion.38 = f32[8,128,1152]{2,1,0:T(8,128)} fusion(f32[8,128,1152]{2,1,0:T(8,128)} %get-tuple-element.506, s32[]{:T(128)} %get-tuple-element.505, bf16[2048,2048]{1,0:T(8,128)(2,1)} %get-tuple-element.519, s32[]{:T(128)S(6)} %select_n.109, bf16[2048,1024]{1,0:T(8,128)(2,1)} %get-tuple-element.518, s32[]{:T(128)S(6)} %select_n.110), kind=kOutput, calls=%fused_computation.3.clone.1 | convolution fusion | flops 603979776 | bytes 5833224 | tf_op jit(solution)/shard_map/while/body/eval_jaxpr/dot_general | solution.py:41
  84.1 0.8 dynamic-update-slice
  84.9 70.6 %all-reduce = f32[16]{0:T(128)S(1)} all-reduce(f32[16]{0:T(128)S(1)} %dynamic-update-slice), channel_id=1, replica_groups=mesh['genome'=16,'samples'=2] {'genome'}, use_global_device_ids=true, to_apply=%add | all-reduce | flops 16 | bytes 128
  156.7 0.8 dynamic-update-slice.1
  158.0 26.3 %reduce-scatter.2.cloned.1.call-done = f32[512,1152]{1,0:T(8,128)} async-done(((f32[1024,1152]{1,0:T(8,128)}), f32[512,1152]{1,0:T(8,128)}) %reduce-scatter.2.cloned.1.call-update) | async-done | bytes 2359312 | tf_op jit(solution)/shard_map/reduce_scatter | solution.py:81
  184.2 2.5 select_reduce_fusion
  186.7 2.3 fusion.15
  189.6 4.9 %all-reduce.3 = (f32[2]{0:T(128)S(1)}, f32[4]{0:T(128)S(1)}, f32[1,2]{1,0:T(1,128)S(1)}) all-reduce(f32[2]{0:T(128)S(1)} %dynamic-update-slice.1, f32[4]{0:T(128)S(1)} %dynamic-update-slice.2, f32[1,2]{1,0:T(1,128)S(1)} %multiply_bitcast_fusion), channel_id=1, replica_groups=mesh['genome'=16,'samples'=2] {'samples'}, use_global_device_ids=true, to_apply=%add.1 | all-reduce | flops 8 | bytes 64
  194.5 21.3 %all-gather.1 = f32[16,1,2]{2,1,0:T(1,128)S(1)} all-gather(f32[1,1,2]{2,1,0:T(1,128)S(1)} %bitcast.46), channel_id=1, replica_groups=mesh['genome'=16,'samples'=2] {'genome'}, dimensions={0}, use_global_device_ids=true | all-gather | bytes 136 | tf_op jit(solution)/shard_map/all_gather | solution.py:23
  215.8 22.2 %while.43 = (s32[]{:T(128)}, f32[2]{0:T(128)S(1)}, s32[]{:T(128)}, f32[16]{0:T(128)S(1)}, f32[16,2]{1,0:T(8,128)S(1)}, /*index=5*/s32[]{:T(128)}, s32[]{:T(128)}, f32[2]{0:T(128)S(1)}) while((s32[]{:T(128)}, f32[2]{0:T(128)S(1)}, s32[]{:T(128)}, f32[16]{0:T(128)S(1)}, f32[16,2]{1,0:T(8,128)S(1)}, ...), condition=%wide.region_8.9_spmd.clone.clone, body=%wide.region_7.8_spmd.sunk.clone.clone.sunk | while | flops 14 | bytes 157 | solution.py:33
  216.5 0.7 broadcast_select_fusion.6
  217.8 0.7 broadcast_select_fusion.6
  219.2 0.7 broadcast_select_fusion.6
  220.6 0.7 broadcast_select_fusion.6
  221.3 0.7 dynamic_slice.71
  222.0 0.7 broadcast_select_fusion.6
  222.7 0.7 dynamic_slice.71
  223.4 0.7 broadcast_select_fusion.6
  224.1 0.7 dynamic_slice.71
  224.8 0.7 broadcast_select_fusion.6
  225.5 0.7 dynamic_slice.71
  226.2 0.7 broadcast_select_fusion.6
  226.9 0.7 dynamic_slice.71
  227.6 0.7 broadcast_select_fusion.6
  228.3 0.7 dynamic_slice.71
  228.9 0.7 broadcast_select_fusion.6
  230.3 0.7 broadcast_select_fusion.6
  231.7 0.7 broadcast_select_fusion.6
  233.1 0.7 broadcast_select_fusion.6
  234.5 0.7 broadcast_select_fusion.6
  235.9 0.7 broadcast_select_fusion.6
  237.3 0.7 broadcast_select_fusion.6
  238.1 3.8 %while.44 = (s32[]{:T(128)}, f32[2]{0:T(128)S(1)}, f32[]{:T(128)}, s32[]{:T(128)}, f32[2]{0:T(128)S(1)}, /*index=5*/f32[2,2]{1,0:T(2,128)S(1)}, s32[]{:T(128)}, s32[]{:T(128)}, f32[2]{0:T(128)S(1)}) while((s32[]{:T(128)}, f32[2]{0:T(128)S(1)}, f32[]{:T(128)}, s32[]{:T(128)}, f32[2]{0:T(128)S(1)}, ...), condition=%wide.region_10.11_spmd.clone.clone, body=%wide.region_9.10_spmd.sunk.clone.clone.sunk | while | flops 16 | bytes 190 | solution.py:33
  241.9 0.7 negate_divide_fusion
  (58 shorter events, 16.7 us)
Async XLA Ops:
  7.2 177.1 %reduce-scatter.2.cloned.1.call-start = ((), (), s32[]{:S(2)}) async-start(), calls=%async_computation.1 | async-start | bytes 7077888 | tf_op jit(solution)/shard_map/reduce_scatter | solution.py:81
  21.4 9.4 %collective-permute-start = (bf16[2048,1024]{1,0:T(8,128)(2,1)}, bf16[2048,1024]{1,0:T(8,128)(2,1)}, u32[]{:S(2)}, u32[]{:S(2)}) collective-permute-start(bf16[2048,1024]{1,0:T(8,128)(2,1)} %fusion.11), channel_id=1, source_target_pairs={{2,0},{4,2},{6,4},{8,6},{10,8},{12,10},{14,12},{16,14},{18,16},{20... | collective-permute-start | bytes 12582920 | tf_op jit(solution)/shard_map/ppermute | solution.py:18
  82.9 0.7 copy-start.5
  82.9 72.6 %copy-start.4 = (u32[32]{0:T(128)S(1)}, u32[32]{0:T(128)}, u32[]{:S(2)}) copy-start(u32[32]{0:T(128)} %constant.127) | copy-start | bytes 388
  82.9 75.1 %copy-start.1 = (s32[512]{0:T(512)S(1)}, s32[512]{0:T(512)}, u32[]{:S(2)}) copy-start(s32[512]{0:T(512)} %param.10) | copy-start | bytes 6148
  82.9 103.8 %copy-start = (f32[2]{0:T(128)S(1)}, f32[2]{0:T(128)}, u32[]{:S(2)}) copy-start(f32[2]{0:T(128)} %constant.117.clone) | copy-start | bytes 28
  82.9 159.0 %copy-start.3 = (f32[2]{0:T(128)S(1)}, f32[2]{0:T(128)}, u32[]{:S(2)}) copy-start(f32[2]{0:T(128)} %constant.119) | copy-start | bytes 28
  186.7 55.9 %copy-start.2 = (f32[512]{0:T(512)}, f32[512]{0:T(512)S(1)}, u32[]{:S(2)}) copy-start(f32[512]{0:T(512)S(1)} %convert_divide_fusion) | copy-start | bytes 6148
Sparse Core Ops, SparseCore 0:
  83.0 101.1 reduce-scatter.1
where the time goes:
time: 250 us; the launch traced here: 249 us
  blocking collectives  103 us (41%)
  matrix products  36.4 us (15%)
  waiting for transfers between devices  34.4 us (14%)
  other arithmetic  32.6 us (13%)
  local copies, waits for them, and re-layouts  20.3 us (8%)
  between operations  14.9 us (6%)
  loops' own time  6.88 us (3%)
    unnamed x2, blocking collectives  75.5 us
    dot_general x8, matrix products, transpose_product(): lax.dot_general(left_side, right_side, (((0,), (0,)), ((), ())), preferre...  34 us
    reduce_scatter x1, waiting for transfers between devices, per_device(): lax.psum_scatter(tiles.reshape(share_rows * lax.axis_size('samples'), TIL...  26.3 us
    all_gather x1, blocking collectives, carried_in(): everything = jax.tree.map(lambda part: lax.all_gather(part, axis), x)  21.3 us
    select_n x18, other arithmetic, lap(): return jax.tree.map(lambda a, b: jnp.where(reached, a, b), new, before)  12.6 us
    dynamic_slice x18, local copies, waits for them, and re-layouts, lap(): new = combine(before, jax.tree.map(lambda part: part[k], everything))  11.8 us
    concatenate x1, other arithmetic, per_device(): extended = jnp.concatenate([standard, next_edge], axis=1)  8.15 us
    ppermute x1, waiting for transfers between devices, from_behind(): return lax.ppermute(block, axis, route)  8.09 us
  transfers between devices with their start and end apart: 2, of which 2 were waited for; matrix products, arithmetic and copies ran while one was open for 1% of the time, Pallas kernels for 0%

commit v1 on v0

v1 whole, which is shorter than its diff:
```python
import functools
import math

import jax
import jax.numpy as jnp
from jax import lax
from jax.experimental import pallas as pl
from jax.experimental.pallas import tpu as pltpu
from jax.sharding import PartitionSpec as P


LANES = 128
EIGHTHS = (2, 3, 2, 1)
VMEM_LIMIT = 20 * 2**20
variance_floor = 0.01


def standardize(alleles, frequency, inverse_sd):
    return ((alleles.astype(jnp.float32) - frequency) * inverse_sd).astype(jnp.bfloat16)


def product(left, right):
    return lax.dot_general(
        left, right, (((0,), (0,)), ((), ())), preferred_element_type=jnp.float32
    )


def moments(counts, haplo_total):
    frequency = counts / haplo_total
    return frequency, lax.rsqrt(jnp.maximum(frequency * (1.0 - frequency), variance_floor))


def call(kernel, shapes, *arrays):
    return pl.pallas_call(
        kernel,
        in_specs=[pl.BlockSpec(memory_space=pltpu.VMEM)] * len(arrays),
        out_specs=[pl.BlockSpec(memory_space=pltpu.VMEM)] * len(shapes),
        out_shape=[jax.ShapeDtypeStruct(s, t) for s, t in shapes],
        compiler_params=pltpu.CompilerParams(vmem_limit_bytes=VMEM_LIMIT),
    )(*arrays)


def columns(index, width):
    return pl.ds(pl.multiple_of(index * width, LANES), width)


def expm1(x):
    series = jnp.ones_like(x)
    for n in range(9, 1, -1):
        series = 1.0 + series * (x * (1.0 / n))
    return jnp.where(x > -0.35, x * series, jnp.exp(x) - 1.0)


def own_kernel(share, haplo_total, rates, hap_ref, counts_ref, std_ref, low_ref, high_ref, low_send, high_send, norm_ref, token_ref):
    token_ref[...] = jnp.zeros_like(token_ref)
    me = lax.axis_index("genome") * lax.axis_size("samples") + lax.axis_index("samples")
    position = (me * share + lax.broadcasted_iota(jnp.int32, (1, share), 1)).astype(jnp.float32) + 1.0
    for k, rate in enumerate(rates):
        norm_ref[k : k + 1, :] = math.expm1(rate) / expm1(position * rate)
    frequency, inverse_sd = moments(counts_ref[...], haplo_total)
    std_ref[...] = standardize(hap_ref[...], frequency, inverse_sd)
    mine = lax.axis_index("samples")
    other = 1 - mine
    later = std_ref[:, share:]
    high_send[...] = product(later, std_ref[:, columns(other, share)]).astype(jnp.bfloat16)
    low = product(std_ref[:, :share], std_ref[:, :share])
    low_ref[...] = low
    low_send[...] = low.astype(jnp.bfloat16)
    high_ref[...] = product(later, std_ref[:, columns(mine, share)])


def both_kernel(first, share, haplo_total, raw_ref, counts_ref, std_ref, before_ref, keep_ref, send_ref, token_ref):
    token_ref[...] = before_ref[...]
    frequency, inverse_sd = moments(counts_ref[:, first : first + raw_ref.shape[1]], haplo_total)
    later = standardize(raw_ref[...], frequency, inverse_sd)
    mine = lax.axis_index("samples")
    other = 1 - mine
    send_ref[...] = product(later, std_ref[:, columns(other, share)]).astype(jnp.bfloat16)
    keep_ref[...] = product(later, std_ref[:, columns(mine, share)])


def last_kernel(first, haplo_total, raw_ref, counts_ref, std_ref, before_ref, keep_ref, send_ref, token_ref):
    token_ref[...] = before_ref[...]
    frequency, inverse_sd = moments(counts_ref[:, first : first + raw_ref.shape[1]], haplo_total)
    later = standardize(raw_ref[...], frequency, inverse_sd)
    keep = product(later, std_ref[:, first:])
    keep_ref[...] = keep
    send_ref[...] = keep.astype(jnp.bfloat16)


def window_sums(total, haplo_total, first_column, first_row, ends):
    correlation = total / haplo_total
    column = first_column + lax.broadcasted_iota(jnp.int32, total.shape, 0)
    row = first_row + lax.broadcasted_iota(jnp.int32, total.shape, 1)
    inside = (column > row) & (column < ends)
    return jnp.sum(jnp.where(inside, correlation * correlation, 0.0), axis=0, keepdims=True)


def local_ends(ends_ref, share):
    start = lax.axis_index("genome") * (lax.axis_size("samples") * share)
    return ends_ref[...] - start


def early_kernel(share, haplo_total, pieces, ends_ref, *refs):
    out_ref = refs[-1]
    mine = lax.axis_index("samples")
    ends = local_ends(ends_ref, share)
    out_ref[...] = jnp.zeros_like(out_ref)
    for k, (first_column, owner) in enumerate(pieces):
        keep, got = refs[2 * k], refs[2 * k + 1]

        def add(keep=keep, got=got, first_column=first_column):
            total = keep[...] + got[...].astype(jnp.float32)
            out_ref[...] += window_sums(total, haplo_total, first_column, mine * share, ends)

        if owner is None:
            add()
        else:
            pl.when(mine == owner)(add)


def rates_of(share, variants):
    return (math.log(0.5) / (4 * share), math.log(0.1) / variants)


def tail_kernel(share, haplo_total, pieces, rates, ends_ref, sums_ref, *refs):
    n = len(pieces)
    score_ref, local_ref, last_ref, total_ref = refs[2 * n :]
    mine = lax.axis_index("samples")
    ends = local_ends(ends_ref, share)
    total_ref[...] = sums_ref[...]
    for k, (first_column, first_row, owner) in enumerate(pieces):
        keep, got = refs[2 * k], refs[2 * k + 1]

        @pl.when(mine == owner)
        def _(keep=keep, got=got, first_column=first_column, first_row=first_row, owner=owner):
            inner = slice(first_row - owner * share, None)
            total = keep[...] + got[...].astype(jnp.float32)
            total_ref[:, inner] += window_sums(
                total, haplo_total, first_column, first_row, ends[:, inner]
            )

    row = mine * share + lax.broadcasted_iota(jnp.int32, (1, share), 1)
    counted = jnp.maximum(ends - row - 1, 1).astype(jnp.float32)
    score = total_ref[...] / counted
    score_ref[...] = score
    blocks = share // LANES
    stacked = jnp.concatenate(
        [score[:, b * LANES : (b + 1) * LANES] for b in range(blocks)]
        + ([jnp.zeros(((-blocks) % 8, LANES), jnp.float32)] if blocks % 8 else []),
        axis=0,
    )
    source = lax.broadcasted_iota(jnp.int32, (LANES, LANES), 0)
    target = lax.broadcasted_iota(jnp.int32, (LANES, LANES), 1)
    lag = (target - source).astype(jnp.float32)
    lane = lax.broadcasted_iota(jnp.int32, (1, LANES), 1).astype(jnp.float32)
    lasts = []
    for k, rate in enumerate(rates):
        weight = jnp.where(lag >= 0.0, jnp.exp(jnp.maximum(lag, 0.0) * rate), 0.0)
        inner = lax.dot_general(
            stacked,
            weight,
            (((1,), (0,)), ((), ())),
            precision=lax.Precision.HIGHEST,
            preferred_element_type=jnp.float32,
        )
        fall = jnp.exp((lane + 1.0) * rate)
        carry = jnp.zeros((1, 1), jnp.float32)
        for b in range(blocks):
            here = inner[b : b + 1, :] + carry * fall
            local_ref[k : k + 1, b * LANES : (b + 1) * LANES] = here
            carry = here[:, LANES - 1 :]
        lasts.append(carry)
    tile_lane = lax.broadcasted_iota(jnp.int32, last_ref.shape, 1)
    last_ref[...] = jnp.where(tile_lane == 0, lasts[0], jnp.where(tile_lane == 1, lasts[1], 0.0))


def finish_kernel(rates, local_ref, table_ref, norm_ref, profile_ref):
    share = local_ref.shape[1]
    peers = table_ref.shape[0]
    me = lax.axis_index("genome") * lax.axis_size("samples") + lax.axis_index("samples")
    peer = lax.broadcasted_iota(jnp.int32, (peers, LANES), 0)
    gap = ((me - 1 - peer) * share).astype(jnp.float32)
    step = lax.broadcasted_iota(jnp.int32, (1, share), 1).astype(jnp.float32)
    for k, rate in enumerate(rates):
        weight = jnp.where(peer < me, jnp.exp(jnp.maximum(gap, 0.0) * rate), 0.0)
        incoming = jnp.sum(weight * table_ref[...], axis=0, keepdims=True)[:, k : k + 1]
        smoothed = local_ref[k : k + 1, :] + incoming * jnp.exp((step + 1.0) * rate)
        profile_ref[k : k + 1, :] = smoothed * norm_ref[k : k + 1, :]


def per_device(haplotypes, window_ends):
    samples = lax.axis_size("samples")
    genome = lax.axis_size("genome")
    depth, width = haplotypes.shape
    share = width // samples
    haplo_total = float(depth * samples)
    rates = rates_of(share, width * genome)
    back = [(i + 1, i) for i in range(genome - 1)]
    ends = window_ends[None]
    f32, bf16 = jnp.float32, jnp.bfloat16
    unit = width // 8
    firsts = [unit * sum(EIGHTHS[:c]) for c in range(len(EIGHTHS))]
    sizes = [unit * e for e in EIGHTHS]

    raws, counts = [], None
    for first, size in zip(firsts, sizes):
        raws.append(lax.ppermute(haplotypes[:, first : first + size], "genome", back))
    counts = jnp.sum(haplotypes, axis=0, dtype=f32)[None]
    if samples == 2:
        counts = counts + lax.ppermute(counts, "samples", [(0, 1), (1, 0)])
    else:
        counts = lax.psum(counts, "samples")
    next_counts = lax.ppermute(counts, "genome", back)

    def swap(send, pairs):
        return lax.ppermute(send, "samples", pairs)

    both, up, down = [(0, 1), (1, 0)], [(0, 1)], [(1, 0)]
    tails, tail_pieces = [], []
    token_type = ((8, LANES), f32)
    if samples == 2:
        standard, low, high, low_send, high_send, norm, token = call(
            functools.partial(own_kernel, share, haplo_total, rates),
            [((depth, width), bf16)]
            + [((share, share), f32)] * 2
            + [((share, share), bf16)] * 2
            + [((2, share), f32), token_type],
            haplotypes,
            counts,
        )
        arrays = [high, swap(high_send, both), low, swap(low_send, down)]
        pieces = [(share, None), (0, 0)]
        for c, (first, size) in enumerate(zip(firsts, sizes)):
            straddles = first < share
            rows = share if straddles else width - first
            kernel = (
                functools.partial(both_kernel, first, share, haplo_total)
                if straddles
                else functools.partial(last_kernel, first, haplo_total)
            )
            keep, send, token = call(
                kernel,
                [((size, rows), f32), ((size, rows), bf16), token_type],
                raws[c],
                next_counts,
                standard,
                token,
            )
            got = swap(send, both if straddles else up)
            if straddles:
                arrays += [keep, got]
                pieces.append((width + first, None))
            else:
                tails += [keep, got]
                tail_pieces.append((width + first, first, 1))
        (sums,) = call(
            functools.partial(early_kernel, share, haplo_total, pieces),
            [((1, share), f32)],
            ends,
            *arrays,
        )
    else:
        frequency, inverse_sd = moments(counts, haplo_total)
        standard = standardize(haplotypes, frequency, inverse_sd)
        frequency, inverse_sd = moments(next_counts, haplo_total)
        later = standardize(jnp.concatenate(raws, axis=1), frequency, inverse_sd)
        total = lax.psum_scatter(
            product(jnp.concatenate([standard, later], axis=1), standard),
            "samples",
            scatter_dimension=1,
            tiled=True,
        )
        me = lax.axis_index("genome") * samples + lax.axis_index("samples")
        position = (me * share + jnp.arange(share, dtype=jnp.int32)).astype(f32) + 1.0
        log_rates = jnp.array(rates, f32)[:, None]
        norm = jnp.expm1(log_rates) / jnp.expm1(position[None] * log_rates)
        sums = window_sums(
            total,
            haplo_total,
            0,
            lax.axis_index("samples") * share,
            ends - lax.axis_index("genome") * width,
        )

    score, local, last, _ = call(
        functools.partial(tail_kernel, share, haplo_total, tail_pieces, rates),
        [((1, share), f32), ((2, share), f32), ((genome * samples, LANES), f32), ((1, share), f32)],
        ends,
        sums,
        *tails,
    )
    table = lax.all_to_all(last[:, None], ("genome", "samples"), 0, 0, tiled=True)[:, 0]
    (profile,) = call(
        functools.partial(finish_kernel, rates), [((2, share), f32)], local, table, norm
    )
    return score[0], profile


def solution(mesh):
    return jax.shard_map(
        per_device,
        mesh=mesh,
        in_specs=(P("samples", "genome"), P(("genome", "samples"))),
        out_specs=(P(("genome", "samples")), P(None, ("genome", "samples"))),
        check_vma=False,
    )
```

time: 250 us -> 107 us (0.43)
  blocking collectives: 103 us -> 61.2 us
  matrix products: 36.4 us -> 0 us
  other arithmetic: 32.6 us -> 0.72 us
  waiting for transfers between devices: 34.4 us -> 7.39 us
  starting transfers between devices: 1.32 us -> 20.8 us
  local copies, waits for them, and re-layouts: 20.3 us -> 3.56 us
  between operations: 14.9 us -> 0.81 us
  Pallas kernels: 0 us -> 12.4 us
  loops' own time: 6.88 us -> 0 us
    unnamed x2 -> x0, blocking collectives: 75.5 us -> none
    all_to_all x0 -> x1, blocking collectives: none -> 61.2 us  [per_device(): lax.all_to_all(last[:, None], ('genome', 'samples'), 0, 0, tiled=True)[:, 0]]
    dot_general x9 -> x0, matrix products: 36.4 us -> none  [the longest x8 34 us: transpose_product(): lax.dot_general(left_side, right_side, (((0,), (0,)), ((), ())), preferre...]
    reduce_scatter x1 -> x0, waiting for transfers between devices: 26.3 us -> none  [per_device(): lax.psum_scatter(tiles.reshape(share_rows * lax.axis_size('samples'), TIL...]
    all_gather x1 -> x0, blocking collectives: 21.3 us -> none  [carried_in(): everything = jax.tree.map(lambda part: lax.all_gather(part, axis), x)]
    ppermute x1 -> x12, starting transfers between devices: 1.28 us -> 20.8 us  [the longest x6 11.2 us: swap(): return lax.ppermute(send, 'samples', pairs)]
    dynamic_slice x26 -> x0, local copies, waits for them, and re-layouts: 16.5 us -> none  [the longest x18 11.8 us: lap(): new = combine(before, jax.tree.map(lambda part: part[k], everything))]
    select_n x18 -> x0, other arithmetic: 12.6 us -> none  [lap(): return jax.tree.map(lambda a, b: jnp.where(reached, a, b), new, before)]
  transfers between devices with their start and end apart: 2 -> 12, of which waited for: 2 -> 2; matrix products, arithmetic and copies ran while one was open for 1% -> 2% of each run, Pallas kernels for 0% -> 10%
where the time goes in v1:
time: 107 us
  blocking collectives  61.2 us (57%)
  starting transfers between devices  20.8 us (19%)
  Pallas kernels  12.4 us (12%)
  waiting for transfers between devices  7.39 us (7%)
  local copies, waits for them, and re-layouts  3.56 us (3%)
    all_to_all x1, blocking collectives, per_device(): lax.all_to_all(last[:, None], ('genome', 'samples'), 0, 0, tiled=True)[:, 0]  61.2 us
    pallas_call x8, Pallas kernels, call(): pl.pallas_call(kernel, in_specs=[pl.BlockSpec(memory_space=pltpu.VMEM)] *...  12.4 us
    ppermute x6, starting transfers between devices, swap(): return lax.ppermute(send, 'samples', pairs)  11.2 us
    ppermute x6, waiting for transfers between devices, swap(): return lax.ppermute(send, 'samples', pairs)  5.79 us
    ppermute x4, starting transfers between devices, per_device(): raws.append(lax.ppermute(haplotypes[:, first:first + size], 'genome', back))  5.3 us
    slice x3, local copies, waits for them, and re-layouts, per_device(): raws.append(lax.ppermute(haplotypes[:, first:first + size], 'genome', back))  3.55 us
    ppermute x1, starting transfers between devices, per_device(): counts = counts + lax.ppermute(counts, 'samples', [(0, 1), (1, 0)])  3.05 us
  transfers between devices with their start and end apart: 12, of which 2 were waited for; matrix products, arithmetic and copies ran while one was open for 2% of the time, Pallas kernels for 10%

profile of v1, /device:TPU:0, one launch (start us, length us, event | category | flops | bytes accessed | tf_op | source)
XLA Modules:
  0.0 106.9 jit_solution(17659887495595621174)
XLA Ops:
  0.6 0.0 copy-start
  0.6 1.7 %slice.13 = bf16[2048,384]{1,0:T(8,128)(2,1)S(1)} slice(bf16[2048,1024]{1,0:T(8,128)(2,1)} %hap_ref.1), slice={[0:2048], [256:640]} | slice | bytes 3145728 | tf_op jit(solution)/shard_map/slice | solution.py:208
  2.4 1.4 %collective-permute-start.6 = (bf16[2048,384]{1,0:T(8,128)(2,1)S(1)}, bf16[2048,384]{1,0:T(8,128)(2,1)S(1)}, u32[]{:S(2)}, u32[]{:S(2)}) collective-permute-start(bf16[2048,384]{1,0:T(8,128)(2,1)S(1)} %slice.13), channel_id=1, source_target_pairs={{2,0},{4,2},{6,4},{8,6},{10,8},{12,10},{14,12},{16,14},{18,16},{20... | collective-permute-start | bytes 4718600 | tf_op jit(solution)/shard_map/ppermute | solution.py:208
  3.8 1.7 %fusion = (bf16[2048,256]{1,0:T(8,128)(2,1)S(1)}, bf16[2048,256]{1,0:T(8,128)(2,1)S(1)}) fusion(bf16[2048,1024]{1,0:T(8,128)(2,1)} %hap_ref.1), kind=kLoop, calls=%fused_computation.1 | loop fusion | bytes 4194304 | tf_op jit(solution)/shard_map/slice | solution.py:208
  5.5 1.3 %collective-permute-start.3 = (bf16[2048,256]{1,0:T(8,128)(2,1)S(1)}, bf16[2048,256]{1,0:T(8,128)(2,1)S(1)}, u32[]{:S(2)}, u32[]{:S(2)}) collective-permute-start(bf16[2048,256]{1,0:T(8,128)(2,1)S(1)} %get-tuple-element.45), channel_id=1, source_target_pairs={{2,0},{4,2},{6,4},{8,6},{10,8},{12,10},{14,12},{16,14},{18,16},{20... | collective-permute-start | bytes 3145736 | tf_op jit(solution)/shard_map/ppermute | solution.py:208
  6.8 1.3 %collective-permute-start.8 = (bf16[2048,256]{1,0:T(8,128)(2,1)S(1)}, bf16[2048,256]{1,0:T(8,128)(2,1)S(1)}, u32[]{:S(2)}, u32[]{:S(2)}) collective-permute-start(bf16[2048,256]{1,0:T(8,128)(2,1)S(1)} %get-tuple-element.44), channel_id=1, source_target_pairs={{2,0},{4,2},{6,4},{8,6},{10,8},{12,10},{14,12},{16,14},{18,16},{20... | collective-permute-start | bytes 3145736 | tf_op jit(solution)/shard_map/ppermute | solution.py:208
  8.1 0.0 copy-done
  8.1 0.1 slice.15
  8.2 1.3 %collective-permute-start.10 = (bf16[2048,128]{1,0:T(8,128)(2,1)S(1)}, bf16[2048,128]{1,0:T(8,128)(2,1)S(1)}, u32[]{:S(2)}, u32[]{:S(2)}) collective-permute-start(bf16[2048,128]{1,0:T(8,128)(2,1)S(1)} %slice.15), channel_id=1, source_target_pairs={{2,0},{4,2},{6,4},{8,6},{10,8},{12,10},{14,12},{16,14},{18,16},{20... | collective-permute-start | bytes 1572872 | tf_op jit(solution)/shard_map/ppermute | solution.py:208
  9.5 0.7 convert_reduce_fusion
  10.3 3.1 %collective-permute-start = (f32[1,1024]{1,0:T(1,128)S(1)}, f32[1,1024]{1,0:T(1,128)S(1)}, u32[]{:S(2)}, u32[]{:S(2)}) collective-permute-start(f32[1,1024]{1,0:T(1,128)S(1)} %bitcast.11), channel_id=1, source_target_pairs={{0,1},{1,0},{2,3},{3,2},{4,5},{5,4},{6,7},{7,6},{8,9},{9,8},{10,11... | collective-permute-start | bytes 12296 | tf_op jit(solution)/shard_map/ppermute | solution.py:211
  13.3 1.6 %collective-permute-done = f32[1,1024]{1,0:T(1,128)S(1)} collective-permute-done((f32[1,1024]{1,0:T(1,128)S(1)}, f32[1,1024]{1,0:T(1,128)S(1)}, u32[]{:S(2)}, u32[]{:S(2)}) %collective-permute-start) | collective-permute-done | bytes 4128 | tf_op jit(solution)/shard_map/ppermute | solution.py:211
  14.9 1.3 %collective-permute-start.4 = (f32[1,1024]{1,0:T(1,128)S(1)}, f32[1,1024]{1,0:T(1,128)S(1)}, u32[]{:S(2)}, u32[]{:S(2)}) collective-permute-start(f32[1,1024]{1,0:T(1,128)S(1)} %add.3.counts_ref), channel_id=1, source_target_pairs={{2,0},{4,2},{6,4},{8,6},{10,8},{12,10},{14,12},{16,14},{18,16},{20... | collective-permute-start | bytes 12296 | tf_op jit(solution)/shard_map/ppermute | solution.py:214
  16.2 4.5 %shard_map.41 = (bf16[2048,1024]{1,0:T(8,128)(2,1)S(1)}, f32[512,512]{1,0:T(8,128)S(1)}, f32[512,512]{1,0:T(8,128)S(1)}, bf16[512,512]{1,0:T(8,128)(2,1)S(1)}, b...) custom-call(bf16[2048,1024]{1,0:T(8,128)(2,1)S(1)} %copy-done, f32[1,1024]{1,0:T(1,128)S(1)} %add.3.counts_ref), custom_call_target="tpu_custom_call" | custom-call | tf_op jit(solution)/shard_map/pallas_call | solution.py:34
  20.7 0.0 collective-permute-done.4.counts_ref
  20.7 2.0 %collective-permute-start.1 = (bf16[512,512]{1,0:T(8,128)(2,1)S(1)}, bf16[512,512]{1,0:T(8,128)(2,1)S(1)}, u32[]{:S(2)}, u32[]{:S(2)}) collective-permute-start(bf16[512,512]{1,0:T(8,128)(2,1)S(1)} %get-tuple-element.24), channel_id=1, source_target_pairs={{0,1},{1,0},{2,3},{3,2},{4,5},{5,4},{6,7},{7,6},{8,9},{9,8},{10,11... | collective-permute-start | bytes 1572872 | tf_op jit(solution)/shard_map/ppermute | solution.py:217
  22.8 0.0 collective-permute-done.3.raw_ref
  22.8 1.3 %collective-permute-start.2 = (bf16[512,512]{1,0:T(8,128)(2,1)S(1)}, bf16[512,512]{1,0:T(8,128)(2,1)S(1)}, u32[]{:S(2)}, u32[]{:S(2)}) collective-permute-start(bf16[512,512]{1,0:T(8,128)(2,1)S(1)} %get-tuple-element.26), channel_id=1, source_target_pairs={{1,0},{3,2},{5,4},{7,6},{9,8},{11,10},{13,12},{15,14},{17,16},{19,... | collective-permute-start | bytes 1572872 | tf_op jit(solution)/shard_map/ppermute | solution.py:217
  24.0 1.3 %shard_map.42 = (f32[256,512]{1,0:T(8,128)S(1)}, bf16[256,512]{1,0:T(8,128)(2,1)S(1)}, f32[8,128]{1,0:T(8,128)S(1)}) custom-call(bf16[2048,256]{1,0:T(8,128)(2,1)S(1)} %collective-permute-done.3.raw_ref, f32[1,1024]{1,0:T(1,128)S(1)} %collective-permute-done.4.counts_ref, bf16[2048,1024]{1,0:T(8,128)(2,1)S(1)} %get-tuple-element.27.std_ref, ...), custom_call_target="tpu_custom_call" | custom-call | tf_op jit(solution)/shard_map/pallas_call | solution.py:34
  25.4 0.0 collective-permute-done.6.raw_ref
  25.4 1.9 %shard_map.43 = (f32[384,512]{1,0:T(8,128)S(1)}, bf16[384,512]{1,0:T(8,128)(2,1)S(1)}, f32[8,128]{1,0:T(8,128)S(1)}) custom-call(bf16[2048,384]{1,0:T(8,128)(2,1)S(1)} %collective-permute-done.6.raw_ref, f32[1,1024]{1,0:T(1,128)S(1)} %collective-permute-done.4.counts_ref, bf16[2048,1024]{1,0:T(8,128)(2,1)S(1)} %get-tuple-element.27.std_ref, ...), custom_call_target="tpu_custom_call" | custom-call | tf_op jit(solution)/shard_map/pallas_call | solution.py:34
  27.2 2.7 %collective-permute-start.7 = (bf16[384,512]{1,0:T(8,128)(2,1)S(1)}, bf16[384,512]{1,0:T(8,128)(2,1)S(1)}, u32[]{:S(2)}, u32[]{:S(2)}) collective-permute-start(bf16[384,512]{1,0:T(8,128)(2,1)S(1)} %get-tuple-element.33), channel_id=1, source_target_pairs={{0,1},{1,0},{2,3},{3,2},{4,5},{5,4},{6,7},{7,6},{8,9},{9,8},{10,11... | collective-permute-start | bytes 1179656 | tf_op jit(solution)/shard_map/ppermute | solution.py:217
  29.9 0.0 collective-permute-done.8.raw_ref
  29.9 0.1 collective-permute-start.5
  30.0 0.0 copy-start.1
  30.0 0.8 shard_map.45
  30.8 0.0 collective-permute-done.10.raw_ref
  30.8 3.9 %collective-permute-start.9 = (bf16[256,384]{1,0:T(8,128)(2,1)S(1)}, bf16[256,384]{1,0:T(8,128)(2,1)S(1)}, u32[]{:S(2)}, u32[]{:S(2)}) collective-permute-start(bf16[256,384]{1,0:T(8,128)(2,1)S(1)} %get-tuple-element.36), channel_id=1, source_target_pairs={{0,1},{2,3},{4,5},{6,7},{8,9},{10,11},{12,13},{14,15},{16,17},{18,... | collective-permute-start | bytes 589832 | tf_op jit(solution)/shard_map/ppermute | solution.py:217
  34.7 0.9 shard_map.46
  35.6 0.0 collective-permute-done.1.refs_1_
  35.6 1.3 %collective-permute-start.11 = (bf16[128,128]{1,0:T(8,128)(2,1)S(1)}, bf16[128,128]{1,0:T(8,128)(2,1)S(1)}, u32[]{:S(2)}, u32[]{:S(2)}) collective-permute-start(bf16[128,128]{1,0:T(8,128)(2,1)S(1)} %get-tuple-element.39), channel_id=1, source_target_pairs={{0,1},{2,3},{4,5},{6,7},{8,9},{10,11},{12,13},{14,15},{16,17},{18,... | collective-permute-start | bytes 98312 | tf_op jit(solution)/shard_map/ppermute | solution.py:217
  36.8 0.0 collective-permute-done.2.refs_3_
  36.9 5.8 %collective-permute-done.5.refs_5_ = bf16[256,512]{1,0:T(8,128)(2,1)S(1)} collective-permute-done((bf16[256,512]{1,0:T(8,128)(2,1)S(1)}, bf16[256,512]{1,0:T(8,128)(2,1)S(1)}, u32[]{:S(2)}, u32[]{:S(2)}) %collective-permute-start.5) | collective-permute-done | bytes 262176 | tf_op jit(solution)/shard_map/ppermute | solution.py:217
  42.6 0.0 collective-permute-done.7.refs_7_
  42.6 0.0 copy-done.1
  42.6 1.7 %shard_map.44.sums_ref = f32[1,512]{1,0:T(1,128)S(1)} custom-call(s32[1,512]{1,0:T(1,128)S(1)} %bitcast.9, f32[512,512]{1,0:T(8,128)S(1)} %get-tuple-element.23.refs_0_, bf16[512,512]{1,0:T(8,128)(2,1)S(1)} %collective-permute-done.1.refs_1_, f32[512,512]{1,0:T(8,128)S(1)} %get-tuple-element.25.refs_2_, bf16[512,512]{1,0:T(8,128)(2,1)S(1)} %collective-permute-done.2.refs_3_, ...), custom_call_target="tpu_custom_call" | custom-call | tf_op jit(solution)/shard_map/pallas_call | solution.py:34
  44.3 0.0 collective-permute-done.11.refs_3_
  44.3 0.0 collective-permute-done.9.refs_1_
  44.3 0.6 shard_map.47
  45.0 61.2 %all_to_all.5 = f32[32,1,128]{2,1,0:T(1,128)S(1)} all-to-all(f32[32,1,128]{2,1,0:T(1,128)S(1)} %bitcast.8), channel_id=1, replica_groups=mesh['genome'=16,'samples'=2] {'genome','samples'}, dimensions={0} | all-to-all | bytes 32768 | tf_op jit(solution)/shard_map/all_to_all | solution.py:293
  106.2 0.7 shard_map.48
  (1 shorter events, 0.0 us)
Async XLA Ops:
  0.6 7.5 %copy-start = (bf16[2048,1024]{1,0:T(8,128)(2,1)S(1)}, bf16[2048,1024]{1,0:T(8,128)(2,1)}, u32[]{:S(2)}) copy-start(bf16[2048,1024]{1,0:T(8,128)(2,1)} %hap_ref.1) | copy-start | bytes 12582916
  2.4 23.0 %collective-permute-start.6 = (bf16[2048,384]{1,0:T(8,128)(2,1)S(1)}, bf16[2048,384]{1,0:T(8,128)(2,1)S(1)}, u32[]{:S(2)}, u32[]{:S(2)}) collective-permute-start(bf16[2048,384]{1,0:T(8,128)(2,1)S(1)} %slice.13), channel_id=1, source_target_pairs={{2,0},{4,2},{6,4},{8,6},{10,8},{12,10},{14,12},{16,14},{18,16},{20... | collective-permute-start | bytes 4718600 | tf_op jit(solution)/shard_map/ppermute | solution.py:208
  5.5 17.3 %collective-permute-start.3 = (bf16[2048,256]{1,0:T(8,128)(2,1)S(1)}, bf16[2048,256]{1,0:T(8,128)(2,1)S(1)}, u32[]{:S(2)}, u32[]{:S(2)}) collective-permute-start(bf16[2048,256]{1,0:T(8,128)(2,1)S(1)} %get-tuple-element.45), channel_id=1, source_target_pairs={{2,0},{4,2},{6,4},{8,6},{10,8},{12,10},{14,12},{16,14},{18,16},{20... | collective-permute-start | bytes 3145736 | tf_op jit(solution)/shard_map/ppermute | solution.py:208
  6.8 23.1 %collective-permute-start.8 = (bf16[2048,256]{1,0:T(8,128)(2,1)S(1)}, bf16[2048,256]{1,0:T(8,128)(2,1)S(1)}, u32[]{:S(2)}, u32[]{:S(2)}) collective-permute-start(bf16[2048,256]{1,0:T(8,128)(2,1)S(1)} %get-tuple-element.44), channel_id=1, source_target_pairs={{2,0},{4,2},{6,4},{8,6},{10,8},{12,10},{14,12},{16,14},{18,16},{20... | collective-permute-start | bytes 3145736 | tf_op jit(solution)/shard_map/ppermute | solution.py:208
  8.2 22.6 %collective-permute-start.10 = (bf16[2048,128]{1,0:T(8,128)(2,1)S(1)}, bf16[2048,128]{1,0:T(8,128)(2,1)S(1)}, u32[]{:S(2)}, u32[]{:S(2)}) collective-permute-start(bf16[2048,128]{1,0:T(8,128)(2,1)S(1)} %slice.15), channel_id=1, source_target_pairs={{2,0},{4,2},{6,4},{8,6},{10,8},{12,10},{14,12},{16,14},{18,16},{20... | collective-permute-start | bytes 1572872 | tf_op jit(solution)/shard_map/ppermute | solution.py:208
  10.3 4.6 %collective-permute-start = (f32[1,1024]{1,0:T(1,128)S(1)}, f32[1,1024]{1,0:T(1,128)S(1)}, u32[]{:S(2)}, u32[]{:S(2)}) collective-permute-start(f32[1,1024]{1,0:T(1,128)S(1)} %bitcast.11), channel_id=1, source_target_pairs={{0,1},{1,0},{2,3},{3,2},{4,5},{5,4},{6,7},{7,6},{8,9},{9,8},{10,11... | collective-permute-start | bytes 12296 | tf_op jit(solution)/shard_map/ppermute | solution.py:211
  14.9 5.8 %collective-permute-start.4 = (f32[1,1024]{1,0:T(1,128)S(1)}, f32[1,1024]{1,0:T(1,128)S(1)}, u32[]{:S(2)}, u32[]{:S(2)}) collective-permute-start(f32[1,1024]{1,0:T(1,128)S(1)} %add.3.counts_ref), channel_id=1, source_target_pairs={{2,0},{4,2},{6,4},{8,6},{10,8},{12,10},{14,12},{16,14},{18,16},{20... | collective-permute-start | bytes 12296 | tf_op jit(solution)/shard_map/ppermute | solution.py:214
  20.7 14.8 %collective-permute-start.1 = (bf16[512,512]{1,0:T(8,128)(2,1)S(1)}, bf16[512,512]{1,0:T(8,128)(2,1)S(1)}, u32[]{:S(2)}, u32[]{:S(2)}) collective-permute-start(bf16[512,512]{1,0:T(8,128)(2,1)S(1)} %get-tuple-element.24), channel_id=1, source_target_pairs={{0,1},{1,0},{2,3},{3,2},{4,5},{5,4},{6,7},{7,6},{8,9},{9,8},{10,11... | collective-permute-start | bytes 1572872 | tf_op jit(solution)/shard_map/ppermute | solution.py:217
  22.8 14.1 %collective-permute-start.2 = (bf16[512,512]{1,0:T(8,128)(2,1)S(1)}, bf16[512,512]{1,0:T(8,128)(2,1)S(1)}, u32[]{:S(2)}, u32[]{:S(2)}) collective-permute-start(bf16[512,512]{1,0:T(8,128)(2,1)S(1)} %get-tuple-element.26), channel_id=1, source_target_pairs={{1,0},{3,2},{5,4},{7,6},{9,8},{11,10},{13,12},{15,14},{17,16},{19,... | collective-permute-start | bytes 1572872 | tf_op jit(solution)/shard_map/ppermute | solution.py:217
  27.2 15.4 %collective-permute-start.7 = (bf16[384,512]{1,0:T(8,128)(2,1)S(1)}, bf16[384,512]{1,0:T(8,128)(2,1)S(1)}, u32[]{:S(2)}, u32[]{:S(2)}) collective-permute-start(bf16[384,512]{1,0:T(8,128)(2,1)S(1)} %get-tuple-element.33), channel_id=1, source_target_pairs={{0,1},{1,0},{2,3},{3,2},{4,5},{5,4},{6,7},{7,6},{8,9},{9,8},{10,11... | collective-permute-start | bytes 1179656 | tf_op jit(solution)/shard_map/ppermute | solution.py:217
  29.9 12.7 %collective-permute-start.5 = (bf16[256,512]{1,0:T(8,128)(2,1)S(1)}, bf16[256,512]{1,0:T(8,128)(2,1)S(1)}, u32[]{:S(2)}, u32[]{:S(2)}) collective-permute-start(bf16[256,512]{1,0:T(8,128)(2,1)S(1)} %get-tuple-element.30), channel_id=1, source_target_pairs={{0,1},{1,0},{2,3},{3,2},{4,5},{5,4},{6,7},{7,6},{8,9},{9,8},{10,11... | collective-permute-start | bytes 786440 | tf_op jit(solution)/shard_map/ppermute | solution.py:217
  30.0 12.6 %copy-start.1 = (s32[512]{0:T(512)S(1)}, s32[512]{0:T(512)}, u32[]{:S(2)}) copy-start(s32[512]{0:T(512)} %param.3) | copy-start | bytes 6148
  30.8 13.5 %collective-permute-start.9 = (bf16[256,384]{1,0:T(8,128)(2,1)S(1)}, bf16[256,384]{1,0:T(8,128)(2,1)S(1)}, u32[]{:S(2)}, u32[]{:S(2)}) collective-permute-start(bf16[256,384]{1,0:T(8,128)(2,1)S(1)} %get-tuple-element.36), channel_id=1, source_target_pairs={{0,1},{2,3},{4,5},{6,7},{8,9},{10,11},{12,13},{14,15},{16,17},{18,... | collective-permute-start | bytes 589832 | tf_op jit(solution)/shard_map/ppermute | solution.py:217
  35.6 8.8 %collective-permute-start.11 = (bf16[128,128]{1,0:T(8,128)(2,1)S(1)}, bf16[128,128]{1,0:T(8,128)(2,1)S(1)}, u32[]{:S(2)}, u32[]{:S(2)}) collective-permute-start(bf16[128,128]{1,0:T(8,128)(2,1)S(1)} %get-tuple-element.39), channel_id=1, source_target_pairs={{0,1},{2,3},{4,5},{6,7},{8,9},{10,11},{12,13},{14,15},{16,17},{18,... | collective-permute-start | bytes 98312 | tf_op jit(solution)/shard_map/ppermute | solution.py:217

commit v2 on v1

--- a/solution.py
+++ b/solution.py
@@ -40,10 +40,6 @@
     )(*arrays)
 
 
-def columns(index, width):
-    return pl.ds(pl.multiple_of(index * width, LANES), width)
-
-
 def expm1(x):
     series = jnp.ones_like(x)
     for n in range(9, 1, -1):
@@ -51,41 +47,77 @@
     return jnp.where(x > -0.35, x * series, jnp.exp(x) - 1.0)
 
 
-def own_kernel(share, haplo_total, rates, hap_ref, counts_ref, std_ref, low_ref, high_ref, low_send, high_send, norm_ref, token_ref):
+def expm1(x):
+    series = jnp.ones_like(x)
+    for n in range(9, 1, -1):
+        series = 1.0 + series * (x * (1.0 / n))
+    return jnp.where(x > -0.35, x * series, jnp.exp(x) - 1.0)
+
+
+def band_blocks(columns, rows, block):
+    out = []
+    for column in range(columns[0], columns[1], block):
+        stop = min(columns[1], column + block)
+        last = min(rows[1], stop)
+        if out and out[-1][2] == rows[0] and last == rows[1] and out[-1][3] == rows[1] - rows[0]:
+            first, count, row, length = out[-1]
+            out[-1] = (first, count + stop - column, row, length)
+        elif last > rows[0]:
+            out.append((column, stop - column, rows[0], last - rows[0]))
+    return out
+
+
+def band_low(first, stop, share):
+    return [(first, stop - first, first, share - first)]
+
+
+def multiply_blocks(left_ref, left_first, right_ref, messages):
+    mine = lax.axis_index("samples")
+    for owner, blocks, keeps, sends in messages:
+        for (column, count, row, length), keep, send in zip(blocks, keeps, sends):
+            part = product(
+                left_ref[:, column - left_first : column - left_first + count],
+                right_ref[:, row : row + length],
+            )
+
+            @pl.when(mine == owner)
+            def _(keep=keep, part=part):
+                keep[...] = part
+
+            @pl.when(mine != owner)
+            def _(send=send, part=part):
+                send[...] = part.astype(jnp.bfloat16)
+
+
+def split_refs(groups, refs):
+    messages, at = [], 0
+    for owner, blocks in groups:
+        n = len(blocks)
+        messages.append((owner, blocks, refs[at : at + n], refs[at + n : at + 2 * n]))
+        at += 2 * n
+    return messages
+
+
+def counts_kernel(hap_ref, out_ref):
+    out_ref[...] = jnp.sum(hap_ref[...].astype(jnp.float32), axis=0, keepdims=True)
+
+
+def own_kernel(groups, share, haplo_total, rates, hap_ref, counts_ref, std_ref, norm_ref, token_ref, *refs):
     token_ref[...] = jnp.zeros_like(token_ref)
+    frequency, inverse_sd = moments(counts_ref[...], haplo_total)
+    std_ref[...] = standardize(hap_ref[...], frequency, inverse_sd)
+    multiply_blocks(std_ref, 0, std_ref, split_refs(groups, refs))
     me = lax.axis_index("genome") * lax.axis_size("samples") + lax.axis_index("samples")
     position = (me * share + lax.broadcasted_iota(jnp.int32, (1, share), 1)).astype(jnp.float32) + 1.0
     for k, rate in enumerate(rates):
         norm_ref[k : k + 1, :] = math.expm1(rate) / expm1(position * rate)
-    frequency, inverse_sd = moments(counts_ref[...], haplo_total)
-    std_ref[...] = standardize(hap_ref[...], frequency, inverse_sd)
-    mine = lax.axis_index("samples")
-    other = 1 - mine
-    later = std_ref[:, share:]
-    high_send[...] = product(later, std_ref[:, columns(other, share)]).astype(jnp.bfloat16)
-    low = product(std_ref[:, :share], std_ref[:, :share])
-    low_ref[...] = low
-    low_send[...] = low.astype(jnp.bfloat16)
-    high_ref[...] = product(later, std_ref[:, columns(mine, share)])
-
-
-def both_kernel(first, share, haplo_total, raw_ref, counts_ref, std_ref, before_ref, keep_ref, send_ref, token_ref):
+
+
+def chunk_kernel(groups, first, haplo_total, raw_ref, counts_ref, std_ref, before_ref, token_ref, later_ref, *refs):
     token_ref[...] = before_ref[...]
     frequency, inverse_sd = moments(counts_ref[:, first : first + raw_ref.shape[1]], haplo_total)
-    later = standardize(raw_ref[...], frequency, inverse_sd)
-    mine = lax.axis_index("samples")
-    other = 1 - mine
-    send_ref[...] = product(later, std_ref[:, columns(other, share)]).astype(jnp.bfloat16)
-    keep_ref[...] = product(later, std_ref[:, columns(mine, share)])
-
-
-def last_kernel(first, haplo_total, raw_ref, counts_ref, std_ref, before_ref, keep_ref, send_ref, token_ref):
-    token_ref[...] = before_ref[...]
-    frequency, inverse_sd = moments(counts_ref[:, first : first + raw_ref.shape[1]], haplo_total)
-    later = standardize(raw_ref[...], frequency, inverse_sd)
-    keep = product(later, std_ref[:, first:])
-    keep_ref[...] = keep
-    send_ref[...] = keep.astype(jnp.bfloat16)
+    later_ref[...] = standardize(raw_ref[...], frequency, inverse_sd)
+    multiply_blocks(later_ref, first, std_ref, split_refs(groups, refs))
 
 
 def window_sums(total, haplo_total, first_column, first_row, ends):
@@ -101,22 +133,23 @@
     return ends_ref[...] - start
 
 
+def add_blocks(pieces, refs, share, haplo_total, ends, out_ref):
+    mine = lax.axis_index("samples")
+    for k, (owner, first_column, first_row) in enumerate(pieces):
+        keep, got = refs[2 * k], refs[2 * k + 1]
+
+        @pl.when(mine == owner)
+        def _(keep=keep, got=got, owner=owner, first_column=first_column, first_row=first_row):
+            start = first_row - owner * share
+            inner = slice(start, start + keep.shape[1])
+            total = keep[...] + got[...].astype(jnp.float32)
+            out_ref[:, inner] += window_sums(total, haplo_total, first_column, first_row, ends[:, inner])
+
+
 def early_kernel(share, haplo_total, pieces, ends_ref, *refs):
     out_ref = refs[-1]
-    mine = lax.axis_index("samples")
-    ends = local_ends(ends_ref, share)
     out_ref[...] = jnp.zeros_like(out_ref)
-    for k, (first_column, owner) in enumerate(pieces):
-        keep, got = refs[2 * k], refs[2 * k + 1]
-
-        def add(keep=keep, got=got, first_column=first_column):
-            total = keep[...] + got[...].astype(jnp.float32)
-            out_ref[...] += window_sums(total, haplo_total, first_column, mine * share, ends)
-
-        if owner is None:
-            add()
-        else:
-            pl.when(mine == owner)(add)
+    add_blocks(pieces, refs, share, haplo_total, local_ends(ends_ref, share), out_ref)
 
 
 def rates_of(share, variants):
@@ -129,17 +162,7 @@
     mine = lax.axis_index("samples")
     ends = local_ends(ends_ref, share)
     total_ref[...] = sums_ref[...]
-    for k, (first_column, first_row, owner) in enumerate(pieces):
-        keep, got = refs[2 * k], refs[2 * k + 1]
-
-        @pl.when(mine == owner)
-        def _(keep=keep, got=got, first_column=first_column, first_row=first_row, owner=owner):
-            inner = slice(first_row - owner * share, None)
-            total = keep[...] + got[...].astype(jnp.float32)
-            total_ref[:, inner] += window_sums(
-                total, haplo_total, first_column, first_row, ends[:, inner]
-            )
-
+    add_blocks(pieces, refs, share, haplo_total, ends, total_ref)
     row = mine * share + lax.broadcasted_iota(jnp.int32, (1, share), 1)
     counted = jnp.maximum(ends - row - 1, 1).astype(jnp.float32)
     score = total_ref[...] / counted
@@ -203,57 +226,78 @@
     firsts = [unit * sum(EIGHTHS[:c]) for c in range(len(EIGHTHS))]
     sizes = [unit * e for e in EIGHTHS]
 
-    raws, counts = [], None
-    for first, size in zip(firsts, sizes):
-        raws.append(lax.ppermute(haplotypes[:, first : first + size], "genome", back))
-    counts = jnp.sum(haplotypes, axis=0, dtype=f32)[None]
+    def shifted(array, c):
+        return lax.ppermute(array[:, firsts[c] : firsts[c] + sizes[c]], "genome", back)
+
+    raws = [shifted(haplotypes, 0)]
+    (counts,) = call(counts_kernel, [((1, width), f32)], haplotypes)
+    behind, counts = lax.optimization_barrier((haplotypes, counts))
+    raws += [shifted(behind, c) for c in range(1, len(EIGHTHS))]
     if samples == 2:
         counts = counts + lax.ppermute(counts, "samples", [(0, 1), (1, 0)])
     else:
         counts = lax.psum(counts, "samples")
     next_counts = lax.ppermute(counts, "genome", back)
 
-    def swap(send, pairs):
-        return lax.ppermute(send, "samples", pairs)
-
-    both, up, down = [(0, 1), (1, 0)], [(0, 1)], [(1, 0)]
+    def swap(owner, sends):
+        return [lax.ppermute(send, "samples", [(1 - owner, owner)]) for send in sends]
+
+    def shapes_of(groups):
+        shapes = []
+        for _, blocks in groups:
+            for kind in (f32, bf16):
+                shapes += [((count, length), kind) for _, count, _, length in blocks]
+        return shapes
+
     tails, tail_pieces = [], []
     token_type = ((8, LANES), f32)
     if samples == 2:
-        standard, low, high, low_send, high_send, norm, token = call(
-            functools.partial(own_kernel, share, haplo_total, rates),
-            [((depth, width), bf16)]
-            + [((share, share), f32)] * 2
-            + [((share, share), bf16)] * 2
-            + [((2, share), f32), token_type],
+        block = share // 2
+        groups = [
+            (1, band_blocks((share, width), (share, width), block)),
+            (0, [(share, width - share, 0, share)]),
+            (0, band_blocks((0, share), (0, share), block)),
+        ]
+        standard, norm, token, *outs = call(
+            functools.partial(own_kernel, groups, share, haplo_total, rates),
+            [((depth, width), bf16), ((2, share), f32), token_type] + shapes_of(groups),
             haplotypes,
             counts,
         )
-        arrays = [high, swap(high_send, both), low, swap(low_send, down)]
-        pieces = [(share, None), (0, 0)]
+        arrays, pieces = [], []
+
+        def exchange(groups, outs, shift):
+            added, where = [], []
+            for owner, blocks, keeps, sends in split_refs(groups, outs):
+                for keep, got, (column, _, row, _) in zip(keeps, swap(owner, sends), blocks):
+                    added += [keep, got]
+                    where.append((owner, column + shift, row))
+            return added, where
+
+        added, where = exchange(groups, outs, 0)
+        arrays += added
+        pieces += where
         for c, (first, size) in enumerate(zip(firsts, sizes)):
-            straddles = first < share
-            rows = share if straddles else width - first
-            kernel = (
-                functools.partial(both_kernel, first, share, haplo_total)
-                if straddles
-                else functools.partial(last_kernel, first, haplo_total)
-            )
-            keep, send, token = call(
-                kernel,
-                [((size, rows), f32), ((size, rows), bf16), token_type],
+            stop = first + size
+            groups = [(1, [(first, size, max(first, share), width - max(first, share))])]
+            if first < share:
+                low = min(stop, share)
+                groups.append((0, band_low(first, low, share)))
+            token, _, *outs = call(
+                functools.partial(chunk_kernel, groups, first, haplo_total),
+                [token_type, ((depth, size), bf16)] + shapes_of(groups),
                 raws[c],
                 next_counts,
                 standard,
                 token,
             )
-            got = swap(send, both if straddles else up)
-            if straddles:
-                arrays += [keep, got]
-                pieces.append((width + first, None))
+            added, where = exchange(groups, outs, width)
+            if first < share:
+                arrays += added
+                pieces += where
             else:
-                tails += [keep, got]
-                tail_pieces.append((width + first, first, 1))
+                tails += added
+                tail_pieces += where
         (sums,) = call(
             functools.partial(early_kernel, share, haplo_total, pieces),
             [((1, share), f32)],

time: 107 us -> 111 us (1.037)
  blocking collectives: 61.2 us -> 40.2 us
  starting transfers between devices: 20.8 us -> 39.6 us
  Pallas kernels: 12.4 us -> 17.9 us
  waiting for transfers between devices: 7.39 us -> 8.95 us
    all_to_all x1, blocking collectives: 61.2 us -> 40.2 us  [per_device(): lax.all_to_all(last[:, None], ('genome', 'samples'), 0, 0, tiled=True)[:, 0]]
    ppermute x10 -> x15, starting transfers between devices: 16.5 us -> 35.3 us  [the longest x11 30.1 us: swap(): lax.ppermute(send, 'samples', [(1 - owner, owner)])]
    pallas_call x8 -> x9, Pallas kernels: 12.4 us -> 17.9 us  [call(): pl.pallas_call(kernel, in_specs=[pl.BlockSpec(memory_space=pltpu.VMEM)] *...]
    slice x3 -> x4, local copies, waits for them, and re-layouts: 3.55 us -> 0.65 us  [shifted(): array[:, firsts[c]:firsts[c] + sizes[c]]]
    ppermute x1, waiting for transfers between devices: 0.01 us -> 2.22 us  [per_device(): next_counts = lax.ppermute(counts, 'genome', back)]
    unnamed x4, local copies, waits for them, and re-layouts: 0.01 us -> 2.19 us
    ppermute x10 -> x15, waiting for transfers between devices: 5.8 us -> 5.15 us  [the longest x11 5.14 us: swap(): lax.ppermute(send, 'samples', [(1 - owner, owner)])]
  transfers between devices with their start and end apart: 12 -> 17, of which waited for: 2 -> 4; matrix products, arithmetic and copies ran while one was open for 2% -> 0% of each run, Pallas kernels for 10% -> 14%
where the time goes in v2:
time: 111 us; the launch traced here: 110 us
  blocking collectives  40.2 us (36%)
  starting transfers between devices  39.6 us (36%)
  Pallas kernels  17.9 us (16%)
  waiting for transfers between devices  8.95 us (8%)
  local copies, waits for them, and re-layouts  2.84 us (3%)
    all_to_all x1, blocking collectives, per_device(): lax.all_to_all(last[:, None], ('genome', 'samples'), 0, 0, tiled=True)[:, 0]  40.2 us
    ppermute x11, starting transfers between devices, swap(): lax.ppermute(send, 'samples', [(1 - owner, owner)])  30.1 us
    pallas_call x9, Pallas kernels, call(): pl.pallas_call(kernel, in_specs=[pl.BlockSpec(memory_space=pltpu.VMEM)] *...  17.9 us
    ppermute x4, starting transfers between devices, shifted(): lax.ppermute(array[:, firsts[c]:firsts[c] + sizes[c]], 'genome', back)  5.17 us
    ppermute x11, waiting for transfers between devices, swap(): lax.ppermute(send, 'samples', [(1 - owner, owner)])  5.14 us
    ppermute x1, starting transfers between devices, per_device(): counts = counts + lax.ppermute(counts, 'samples', [(0, 1), (1, 0)])  3.06 us
  transfers between devices with their start and end apart: 17, of which 4 were waited for; matrix products, arithmetic and copies ran while one was open for 0% of the time, Pallas kernels for 14%

profile of v2, /device:TPU:0, one launch (start us, length us, event | category | flops | bytes accessed | tf_op | source)
XLA Modules:
  0.0 110.4 jit_solution(14540726653363889510)
XLA Ops:
  0.6 2.2 %copy-done = bf16[2048,1024]{1,0:T(8,128)(2,1)S(1)} copy-done((bf16[2048,1024]{1,0:T(8,128)(2,1)S(1)}, bf16[2048,1024]{1,0:T(8,128)(2,1)}, u32[]{:S(2)}) %copy-start) | copy-done | bytes 4194328
  2.8 0.8 shard_map.41
  3.6 0.2 slice.13
  3.9 1.3 %collective-permute-start.10 = (bf16[2048,384]{1,0:T(8,128)(2,1)S(1)}, bf16[2048,384]{1,0:T(8,128)(2,1)S(1)}, u32[]{:S(2)}, u32[]{:S(2)}) collective-permute-start(bf16[2048,384]{1,0:T(8,128)(2,1)S(1)} %slice.13), channel_id=1, source_target_pairs={{2,0},{4,2},{6,4},{8,6},{10,8},{12,10},{14,12},{16,14},{18,16},{20... | collective-permute-start | bytes 4718600 | tf_op jit(solution)/shard_map/ppermute | solution.py:230
  5.2 0.1 slice.12
  5.3 1.3 %collective-permute-start.6 = (bf16[2048,256]{1,0:T(8,128)(2,1)S(1)}, bf16[2048,256]{1,0:T(8,128)(2,1)S(1)}, u32[]{:S(2)}, u32[]{:S(2)}) collective-permute-start(bf16[2048,256]{1,0:T(8,128)(2,1)S(1)} %slice.12), channel_id=1, source_target_pairs={{2,0},{4,2},{6,4},{8,6},{10,8},{12,10},{14,12},{16,14},{18,16},{20... | collective-permute-start | bytes 3145736 | tf_op jit(solution)/shard_map/ppermute | solution.py:230
  6.6 0.1 slice.14
  6.8 1.3 %collective-permute-start.13 = (bf16[2048,256]{1,0:T(8,128)(2,1)S(1)}, bf16[2048,256]{1,0:T(8,128)(2,1)S(1)}, u32[]{:S(2)}, u32[]{:S(2)}) collective-permute-start(bf16[2048,256]{1,0:T(8,128)(2,1)S(1)} %slice.14), channel_id=1, source_target_pairs={{2,0},{4,2},{6,4},{8,6},{10,8},{12,10},{14,12},{16,14},{18,16},{20... | collective-permute-start | bytes 3145736 | tf_op jit(solution)/shard_map/ppermute | solution.py:230
  8.1 3.1 %collective-permute-start = (f32[1,1024]{1,0:T(1,128)S(1)}, f32[1,1024]{1,0:T(1,128)S(1)}, u32[]{:S(2)}, u32[]{:S(2)}) collective-permute-start(f32[1,1024]{1,0:T(1,128)S(1)} %shard_map.41), channel_id=1, source_target_pairs={{0,1},{1,0},{2,3},{3,2},{4,5},{5,4},{6,7},{7,6},{8,9},{9,8},{10,11... | collective-permute-start | bytes 12296 | tf_op jit(solution)/shard_map/ppermute | solution.py:237
  11.1 1.6 %collective-permute-done = f32[1,1024]{1,0:T(1,128)S(1)} collective-permute-done((f32[1,1024]{1,0:T(1,128)S(1)}, f32[1,1024]{1,0:T(1,128)S(1)}, u32[]{:S(2)}, u32[]{:S(2)}) %collective-permute-start) | collective-permute-done | bytes 4128 | tf_op jit(solution)/shard_map/ppermute | solution.py:237
  12.7 5.9 %shard_map.42 = (bf16[2048,1024]{1,0:T(8,128)(2,1)S(1)}, f32[2,512]{1,0:T(2,128)S(1)}, f32[8,128]{1,0:T(8,128)S(1)}, f32[256,256]{1,0:T(8,128)S(1)}, f32[256,512...) custom-call(bf16[2048,1024]{1,0:T(8,128)(2,1)S(1)} %copy-done, ...), custom_call_target="tpu_custom_call" | custom-call | tf_op jit(solution)/shard_map/pallas_call | solution.py:34
  18.6 3.9 %collective-permute-start.1 = (bf16[256,256]{1,0:T(8,128)(2,1)S(1)}, bf16[256,256]{1,0:T(8,128)(2,1)S(1)}, u32[]{:S(2)}, u32[]{:S(2)}) collective-permute-start(bf16[256,256]{1,0:T(8,128)(2,1)S(1)} %get-tuple-element.37), channel_id=1, source_target_pairs={{0,1},{2,3},{4,5},{6,7},{8,9},{10,11},{12,13},{14,15},{16,17},{18,... | collective-permute-start | bytes 393224 | tf_op jit(solution)/shard_map/ppermute | solution.py:243
  22.5 1.3 %collective-permute-start.7 = (f32[1,1024]{1,0:T(1,128)S(1)}, f32[1,1024]{1,0:T(1,128)S(1)}, u32[]{:S(2)}, u32[]{:S(2)}) collective-permute-start(f32[1,1024]{1,0:T(1,128)S(1)} %add.3.counts_ref), channel_id=1, source_target_pairs={{2,0},{4,2},{6,4},{8,6},{10,8},{12,10},{14,12},{16,14},{18,16},{20... | collective-permute-start | bytes 12296 | tf_op jit(solution)/shard_map/ppermute | solution.py:240
  23.8 2.2 %collective-permute-done.7.counts_ref = f32[1,1024]{1,0:T(1,128)S(1)} collective-permute-done((f32[1,1024]{1,0:T(1,128)S(1)}, f32[1,1024]{1,0:T(1,128)S(1)}, u32[]{:S(2)}, u32[]{:S(2)}) %collective-permute-start.7) | collective-permute-done | bytes 4128 | tf_op jit(solution)/shard_map/ppermute | solution.py:240
  26.1 1.3 %collective-permute-start.4 = (bf16[256,256]{1,0:T(8,128)(2,1)S(1)}, bf16[256,256]{1,0:T(8,128)(2,1)S(1)}, u32[]{:S(2)}, u32[]{:S(2)}) collective-permute-start(bf16[256,256]{1,0:T(8,128)(2,1)S(1)} %get-tuple-element.43), channel_id=1, source_target_pairs={{1,0},{3,2},{5,4},{7,6},{9,8},{11,10},{13,12},{15,14},{17,16},{19,... | collective-permute-start | bytes 393224 | tf_op jit(solution)/shard_map/ppermute | solution.py:243
  27.3 0.1 slice.15
  27.5 0.0 collective-permute-done.1.refs_1_
  27.5 1.3 %collective-permute-start.15 = (bf16[2048,128]{1,0:T(8,128)(2,1)S(1)}, bf16[2048,128]{1,0:T(8,128)(2,1)S(1)}, u32[]{:S(2)}, u32[]{:S(2)}) collective-permute-start(bf16[2048,128]{1,0:T(8,128)(2,1)S(1)} %slice.15), channel_id=1, source_target_pairs={{2,0},{4,2},{6,4},{8,6},{10,8},{12,10},{14,12},{16,14},{18,16},{20... | collective-permute-start | bytes 1572872 | tf_op jit(solution)/shard_map/ppermute | solution.py:230
  28.8 4.1 %collective-permute-done.4.refs_7_ = bf16[256,256]{1,0:T(8,128)(2,1)S(1)} collective-permute-done((bf16[256,256]{1,0:T(8,128)(2,1)S(1)}, bf16[256,256]{1,0:T(8,128)(2,1)S(1)}, u32[]{:S(2)}, u32[]{:S(2)}) %collective-permute-start.4) | collective-permute-done | bytes 131104 | tf_op jit(solution)/shard_map/ppermute | solution.py:243
  32.9 1.3 %collective-permute-start.3 = (bf16[512,512]{1,0:T(8,128)(2,1)S(1)}, bf16[512,512]{1,0:T(8,128)(2,1)S(1)}, u32[]{:S(2)}, u32[]{:S(2)}) collective-permute-start(bf16[512,512]{1,0:T(8,128)(2,1)S(1)} %get-tuple-element.41), channel_id=1, source_target_pairs={{1,0},{3,2},{5,4},{7,6},{9,8},{11,10},{13,12},{15,14},{17,16},{19,... | collective-permute-start | bytes 1572872 | tf_op jit(solution)/shard_map/ppermute | solution.py:243
  34.2 0.0 collective-permute-done.6.raw_ref
  34.2 4.6 %collective-permute-start.2 = (bf16[256,512]{1,0:T(8,128)(2,1)S(1)}, bf16[256,512]{1,0:T(8,128)(2,1)S(1)}, u32[]{:S(2)}, u32[]{:S(2)}) collective-permute-start(bf16[256,512]{1,0:T(8,128)(2,1)S(1)} %get-tuple-element.39), channel_id=1, source_target_pairs={{0,1},{2,3},{4,5},{6,7},{8,9},{10,11},{12,13},{14,15},{16,17},{18,... | collective-permute-start | bytes 786440 | tf_op jit(solution)/shard_map/ppermute | solution.py:243
  38.8 0.0 collective-permute-done.10.raw_ref
  38.8 1.3 %collective-permute-start.5 = (bf16[256,512]{1,0:T(8,128)(2,1)S(1)}, bf16[256,512]{1,0:T(8,128)(2,1)S(1)}, u32[]{:S(2)}, u32[]{:S(2)}) collective-permute-start(bf16[256,512]{1,0:T(8,128)(2,1)S(1)} %get-tuple-element.45), channel_id=1, source_target_pairs={{1,0},{3,2},{5,4},{7,6},{9,8},{11,10},{13,12},{15,14},{17,16},{19,... | collective-permute-start | bytes 786440 | tf_op jit(solution)/shard_map/ppermute | solution.py:243
  40.1 2.5 %shard_map.43 = (f32[8,128]{1,0:T(8,128)S(1)}, bf16[2048,256]{1,0:T(8,128)(2,1)}, f32[256,512]{1,0:T(8,128)S(1)}, bf16[256,512]{1,0:T(8,128)(2,1)S(1)}, f32[256,...) custom-call(bf16[2048,256]{1,0:T(8,128)(2,1)S(1)} %collective-permute-done.6.raw_ref, ...), custom_call_target="tpu_custom_call" | custom-call | tf_op jit(solution)/shard_map/pallas_call | solution.py:34
  42.7 3.3 %shard_map.44 = (f32[8,128]{1,0:T(8,128)S(1)}, bf16[2048,384]{1,0:T(8,128)(2,1)}, f32[384,512]{1,0:T(8,128)S(1)}, bf16[384,512]{1,0:T(8,128)(2,1)S(1)}, f32[256,...) custom-call(bf16[2048,384]{1,0:T(8,128)(2,1)S(1)} %collective-permute-done.10.raw_ref, ...), custom_call_target="tpu_custom_call" | custom-call | tf_op jit(solution)/shard_map/pallas_call | solution.py:34
  46.0 0.0 collective-permute-done.2.refs_3_
  46.0 4.6 %collective-permute-start.11 = (bf16[384,512]{1,0:T(8,128)(2,1)S(1)}, bf16[384,512]{1,0:T(8,128)(2,1)S(1)}, u32[]{:S(2)}, u32[]{:S(2)}) collective-permute-start(bf16[384,512]{1,0:T(8,128)(2,1)S(1)} %get-tuple-element.55), channel_id=1, source_target_pairs={{0,1},{2,3},{4,5},{6,7},{8,9},{10,11},{12,13},{14,15},{16,17},{18,... | collective-permute-start | bytes 1179656 | tf_op jit(solution)/shard_map/ppermute | solution.py:243
  50.5 0.0 collective-permute-done.5.refs_9_
  50.6 1.3 %collective-permute-start.8 = (bf16[256,512]{1,0:T(8,128)(2,1)S(1)}, bf16[256,512]{1,0:T(8,128)(2,1)S(1)}, u32[]{:S(2)}, u32[]{:S(2)}) collective-permute-start(bf16[256,512]{1,0:T(8,128)(2,1)S(1)} %get-tuple-element.49), channel_id=1, source_target_pairs={{0,1},{2,3},{4,5},{6,7},{8,9},{10,11},{12,13},{14,15},{16,17},{18,... | collective-permute-start | bytes 786440 | tf_op jit(solution)/shard_map/ppermute | solution.py:243
  51.9 0.0 collective-permute-done.13.raw_ref
  51.9 1.3 %collective-permute-start.9 = (bf16[256,512]{1,0:T(8,128)(2,1)S(1)}, bf16[256,512]{1,0:T(8,128)(2,1)S(1)}, u32[]{:S(2)}, u32[]{:S(2)}) collective-permute-start(bf16[256,512]{1,0:T(8,128)(2,1)S(1)} %get-tuple-element.51), channel_id=1, source_target_pairs={{1,0},{3,2},{5,4},{7,6},{9,8},{11,10},{13,12},{15,14},{17,16},{19,... | collective-permute-start | bytes 786440 | tf_op jit(solution)/shard_map/ppermute | solution.py:243
  53.2 1.8 %shard_map.46 = (f32[8,128]{1,0:T(8,128)S(1)}, bf16[2048,256]{1,0:T(8,128)(2,1)}, f32[256,384]{1,0:T(8,128)S(1)}, bf16[256,384]{1,0:T(8,128)(2,1)S(1)}) custom-call(bf16[2048,256]{1,0:T(8,128)(2,1)S(1)} %collective-permute-done.13.raw_ref, f32[1,1024]{1,0:T(1,128)S(1)} %collective-permute-done.7.counts_ref, ...), custom_call_target="tpu_custom_call" | custom-call | tf_op jit(solution)/shard_map/pallas_call | solution.py:34
  55.0 0.0 collective-permute-done.15.raw_ref
  55.0 4.6 %collective-permute-start.14 = (bf16[256,384]{1,0:T(8,128)(2,1)S(1)}, bf16[256,384]{1,0:T(8,128)(2,1)S(1)}, u32[]{:S(2)}, u32[]{:S(2)}) collective-permute-start(bf16[256,384]{1,0:T(8,128)(2,1)S(1)} %get-tuple-element.60), channel_id=1, source_target_pairs={{0,1},{2,3},{4,5},{6,7},{8,9},{10,11},{12,13},{14,15},{16,17},{18,... | collective-permute-start | bytes 589832 | tf_op jit(solution)/shard_map/ppermute | solution.py:243
  59.5 0.0 collective-permute-done.3.refs_5_
  59.5 1.5 %collective-permute-start.12 = (bf16[256,256]{1,0:T(8,128)(2,1)S(1)}, bf16[256,256]{1,0:T(8,128)(2,1)S(1)}, u32[]{:S(2)}, u32[]{:S(2)}) collective-permute-start(bf16[256,256]{1,0:T(8,128)(2,1)S(1)} %get-tuple-element.57), channel_id=1, source_target_pairs={{1,0},{3,2},{5,4},{7,6},{9,8},{11,10},{13,12},{15,14},{17,16},{19,... | collective-permute-start | bytes 393224 | tf_op jit(solution)/shard_map/ppermute | solution.py:243
  61.0 0.0 copy-start.1
  61.0 1.2 %shard_map.47 = (f32[8,128]{1,0:T(8,128)}, bf16[2048,128]{1,0:T(8,128)(2,1)}, f32[128,128]{1,0:T(8,128)S(1)}, bf16[128,128]{1,0:T(8,128)(2,1)S(1)}) custom-call(bf16[2048,128]{1,0:T(8,128)(2,1)S(1)} %collective-permute-done.15.raw_ref, f32[1,1024]{1,0:T(1,128)S(1)} %collective-permute-done.7.counts_ref, bf16[2048,1024]{1,0:T(8,128)(2,1)S(1)} %get-tuple-element.46.std_ref, ...), custom_call_target="tpu_custom_call" | custom-call | tf_op jit(solution)/shard_map/pallas_call | solution.py:34
  62.2 0.0 collective-permute-done.8.refs_11_
  62.2 4.5 %collective-permute-start.16 = (bf16[128,128]{1,0:T(8,128)(2,1)S(1)}, bf16[128,128]{1,0:T(8,128)(2,1)S(1)}, u32[]{:S(2)}, u32[]{:S(2)}) collective-permute-start(bf16[128,128]{1,0:T(8,128)(2,1)S(1)} %get-tuple-element.63), channel_id=1, source_target_pairs={{0,1},{2,3},{4,5},{6,7},{8,9},{10,11},{12,13},{14,15},{16,17},{18,... | collective-permute-start | bytes 98312 | tf_op jit(solution)/shard_map/ppermute | solution.py:243
  66.8 0.0 collective-permute-done.9.refs_13_
  66.8 1.0 collective-permute-done.12.refs_17_
  67.8 0.0 collective-permute-done.11.refs_15_
  67.8 1.0 shard_map.45.sums_ref
  68.9 0.6 shard_map.48
  69.5 40.2 %all_to_all.5 = f32[32,1,128]{2,1,0:T(1,128)S(1)} all-to-all(f32[32,1,128]{2,1,0:T(1,128)S(1)} %bitcast.7), channel_id=1, replica_groups=mesh['genome'=16,'samples'=2] {'genome','samples'}, dimensions={0} | all-to-all | bytes 32768 | tf_op jit(solution)/shard_map/all_to_all | solution.py:337
  109.7 0.7 shard_map.49
  (5 shorter events, 0.0 us)
Async XLA Ops:
  0.6 2.2 %copy-start = (bf16[2048,1024]{1,0:T(8,128)(2,1)S(1)}, bf16[2048,1024]{1,0:T(8,128)(2,1)}, u32[]{:S(2)}) copy-start(bf16[2048,1024]{1,0:T(8,128)(2,1)} %hap_ref.3) | copy-start | bytes 12582916
  3.9 34.9 %collective-permute-start.10 = (bf16[2048,384]{1,0:T(8,128)(2,1)S(1)}, bf16[2048,384]{1,0:T(8,128)(2,1)S(1)}, u32[]{:S(2)}, u32[]{:S(2)}) collective-permute-start(bf16[2048,384]{1,0:T(8,128)(2,1)S(1)} %slice.13), channel_id=1, source_target_pairs={{2,0},{4,2},{6,4},{8,6},{10,8},{12,10},{14,12},{16,14},{18,16},{20... | collective-permute-start | bytes 4718600 | tf_op jit(solution)/shard_map/ppermute | solution.py:230
  5.3 28.9 %collective-permute-start.6 = (bf16[2048,256]{1,0:T(8,128)(2,1)S(1)}, bf16[2048,256]{1,0:T(8,128)(2,1)S(1)}, u32[]{:S(2)}, u32[]{:S(2)}) collective-permute-start(bf16[2048,256]{1,0:T(8,128)(2,1)S(1)} %slice.12), channel_id=1, source_target_pairs={{2,0},{4,2},{6,4},{8,6},{10,8},{12,10},{14,12},{16,14},{18,16},{20... | collective-permute-start | bytes 3145736 | tf_op jit(solution)/shard_map/ppermute | solution.py:230
  6.8 45.1 %collective-permute-start.13 = (bf16[2048,256]{1,0:T(8,128)(2,1)S(1)}, bf16[2048,256]{1,0:T(8,128)(2,1)S(1)}, u32[]{:S(2)}, u32[]{:S(2)}) collective-permute-start(bf16[2048,256]{1,0:T(8,128)(2,1)S(1)} %slice.14), channel_id=1, source_target_pairs={{2,0},{4,2},{6,4},{8,6},{10,8},{12,10},{14,12},{16,14},{18,16},{20... | collective-permute-start | bytes 3145736 | tf_op jit(solution)/shard_map/ppermute | solution.py:230
  8.1 4.6 %collective-permute-start = (f32[1,1024]{1,0:T(1,128)S(1)}, f32[1,1024]{1,0:T(1,128)S(1)}, u32[]{:S(2)}, u32[]{:S(2)}) collective-permute-start(f32[1,1024]{1,0:T(1,128)S(1)} %shard_map.41), channel_id=1, source_target_pairs={{0,1},{1,0},{2,3},{3,2},{4,5},{5,4},{6,7},{7,6},{8,9},{9,8},{10,11... | collective-permute-start | bytes 12296 | tf_op jit(solution)/shard_map/ppermute | solution.py:237
  18.6 8.9 %collective-permute-start.1 = (bf16[256,256]{1,0:T(8,128)(2,1)S(1)}, bf16[256,256]{1,0:T(8,128)(2,1)S(1)}, u32[]{:S(2)}, u32[]{:S(2)}) collective-permute-start(bf16[256,256]{1,0:T(8,128)(2,1)S(1)} %get-tuple-element.37), channel_id=1, source_target_pairs={{0,1},{2,3},{4,5},{6,7},{8,9},{10,11},{12,13},{14,15},{16,17},{18,... | collective-permute-start | bytes 393224 | tf_op jit(solution)/shard_map/ppermute | solution.py:243
  22.5 3.5 %collective-permute-start.7 = (f32[1,1024]{1,0:T(1,128)S(1)}, f32[1,1024]{1,0:T(1,128)S(1)}, u32[]{:S(2)}, u32[]{:S(2)}) collective-permute-start(f32[1,1024]{1,0:T(1,128)S(1)} %add.3.counts_ref), channel_id=1, source_target_pairs={{2,0},{4,2},{6,4},{8,6},{10,8},{12,10},{14,12},{16,14},{18,16},{20... | collective-permute-start | bytes 12296 | tf_op jit(solution)/shard_map/ppermute | solution.py:240
  26.1 6.8 %collective-permute-start.4 = (bf16[256,256]{1,0:T(8,128)(2,1)S(1)}, bf16[256,256]{1,0:T(8,128)(2,1)S(1)}, u32[]{:S(2)}, u32[]{:S(2)}) collective-permute-start(bf16[256,256]{1,0:T(8,128)(2,1)S(1)} %get-tuple-element.43), channel_id=1, source_target_pairs={{1,0},{3,2},{5,4},{7,6},{9,8},{11,10},{13,12},{15,14},{17,16},{19,... | collective-permute-start | bytes 393224 | tf_op jit(solution)/shard_map/ppermute | solution.py:243
  27.5 27.5 %collective-permute-start.15 = (bf16[2048,128]{1,0:T(8,128)(2,1)S(1)}, bf16[2048,128]{1,0:T(8,128)(2,1)S(1)}, u32[]{:S(2)}, u32[]{:S(2)}) collective-permute-start(bf16[2048,128]{1,0:T(8,128)(2,1)S(1)} %slice.15), channel_id=1, source_target_pairs={{2,0},{4,2},{6,4},{8,6},{10,8},{12,10},{14,12},{16,14},{18,16},{20... | collective-permute-start | bytes 1572872 | tf_op jit(solution)/shard_map/ppermute | solution.py:230
  32.9 26.6 %collective-permute-start.3 = (bf16[512,512]{1,0:T(8,128)(2,1)S(1)}, bf16[512,512]{1,0:T(8,128)(2,1)S(1)}, u32[]{:S(2)}, u32[]{:S(2)}) collective-permute-start(bf16[512,512]{1,0:T(8,128)(2,1)S(1)} %get-tuple-element.41), channel_id=1, source_target_pairs={{1,0},{3,2},{5,4},{7,6},{9,8},{11,10},{13,12},{15,14},{17,16},{19,... | collective-permute-start | bytes 1572872 | tf_op jit(solution)/shard_map/ppermute | solution.py:243
  34.2 11.8 %collective-permute-start.2 = (bf16[256,512]{1,0:T(8,128)(2,1)S(1)}, bf16[256,512]{1,0:T(8,128)(2,1)S(1)}, u32[]{:S(2)}, u32[]{:S(2)}) collective-permute-start(bf16[256,512]{1,0:T(8,128)(2,1)S(1)} %get-tuple-element.39), channel_id=1, source_target_pairs={{0,1},{2,3},{4,5},{6,7},{8,9},{10,11},{12,13},{14,15},{16,17},{18,... | collective-permute-start | bytes 786440 | tf_op jit(solution)/shard_map/ppermute | solution.py:243
  38.8 11.7 %collective-permute-start.5 = (bf16[256,512]{1,0:T(8,128)(2,1)S(1)}, bf16[256,512]{1,0:T(8,128)(2,1)S(1)}, u32[]{:S(2)}, u32[]{:S(2)}) collective-permute-start(bf16[256,512]{1,0:T(8,128)(2,1)S(1)} %get-tuple-element.45), channel_id=1, source_target_pairs={{1,0},{3,2},{5,4},{7,6},{9,8},{11,10},{13,12},{15,14},{17,16},{19,... | collective-permute-start | bytes 786440 | tf_op jit(solution)/shard_map/ppermute | solution.py:243
  46.0 21.9 %collective-permute-start.11 = (bf16[384,512]{1,0:T(8,128)(2,1)S(1)}, bf16[384,512]{1,0:T(8,128)(2,1)S(1)}, u32[]{:S(2)}, u32[]{:S(2)}) collective-permute-start(bf16[384,512]{1,0:T(8,128)(2,1)S(1)} %get-tuple-element.55), channel_id=1, source_target_pairs={{0,1},{2,3},{4,5},{6,7},{8,9},{10,11},{12,13},{14,15},{16,17},{18,... | collective-permute-start | bytes 1179656 | tf_op jit(solution)/shard_map/ppermute | solution.py:243
  50.6 11.7 %collective-permute-start.8 = (bf16[256,512]{1,0:T(8,128)(2,1)S(1)}, bf16[256,512]{1,0:T(8,128)(2,1)S(1)}, u32[]{:S(2)}, u32[]{:S(2)}) collective-permute-start(bf16[256,512]{1,0:T(8,128)(2,1)S(1)} %get-tuple-element.49), channel_id=1, source_target_pairs={{0,1},{2,3},{4,5},{6,7},{8,9},{10,11},{12,13},{14,15},{16,17},{18,... | collective-permute-start | bytes 786440 | tf_op jit(solution)/shard_map/ppermute | solution.py:243
  51.9 14.9 %collective-permute-start.9 = (bf16[256,512]{1,0:T(8,128)(2,1)S(1)}, bf16[256,512]{1,0:T(8,128)(2,1)S(1)}, u32[]{:S(2)}, u32[]{:S(2)}) collective-permute-start(bf16[256,512]{1,0:T(8,128)(2,1)S(1)} %get-tuple-element.51), channel_id=1, source_target_pairs={{1,0},{3,2},{5,4},{7,6},{9,8},{11,10},{13,12},{15,14},{17,16},{19,... | collective-permute-start | bytes 786440 | tf_op jit(solution)/shard_map/ppermute | solution.py:243
  55.0 13.9 %collective-permute-start.14 = (bf16[256,384]{1,0:T(8,128)(2,1)S(1)}, bf16[256,384]{1,0:T(8,128)(2,1)S(1)}, u32[]{:S(2)}, u32[]{:S(2)}) collective-permute-start(bf16[256,384]{1,0:T(8,128)(2,1)S(1)} %get-tuple-element.60), channel_id=1, source_target_pairs={{0,1},{2,3},{4,5},{6,7},{8,9},{10,11},{12,13},{14,15},{16,17},{18,... | collective-permute-start | bytes 589832 | tf_op jit(solution)/shard_map/ppermute | solution.py:243
  59.5 8.3 %collective-permute-start.12 = (bf16[256,256]{1,0:T(8,128)(2,1)S(1)}, bf16[256,256]{1,0:T(8,128)(2,1)S(1)}, u32[]{:S(2)}, u32[]{:S(2)}) collective-permute-start(bf16[256,256]{1,0:T(8,128)(2,1)S(1)} %get-tuple-element.57), channel_id=1, source_target_pairs={{1,0},{3,2},{5,4},{7,6},{9,8},{11,10},{13,12},{15,14},{17,16},{19,... | collective-permute-start | bytes 393224 | tf_op jit(solution)/shard_map/ppermute | solution.py:243
  61.0 6.8 %copy-start.1 = (s32[512]{0:T(512)S(1)}, s32[512]{0:T(512)}, u32[]{:S(2)}) copy-start(s32[512]{0:T(512)} %param.3) | copy-start | bytes 6148
  62.2 6.6 %collective-permute-start.16 = (bf16[128,128]{1,0:T(8,128)(2,1)S(1)}, bf16[128,128]{1,0:T(8,128)(2,1)S(1)}, u32[]{:S(2)}, u32[]{:S(2)}) collective-permute-start(bf16[128,128]{1,0:T(8,128)(2,1)S(1)} %get-tuple-element.63), channel_id=1, source_target_pairs={{0,1},{2,3},{4,5},{6,7},{8,9},{10,11},{12,13},{14,15},{16,17},{18,... | collective-permute-start | bytes 98312 | tf_op jit(solution)/shard_map/ppermute | solution.py:243

commit v3 on v1

--- a/solution.py
+++ b/solution.py
@@ -10,7 +10,7 @@
 
 
 LANES = 128
-EIGHTHS = (2, 3, 2, 1)
+EIGHTHS = (1, 2, 2, 2, 1)
 VMEM_LIMIT = 20 * 2**20
 variance_floor = 0.01
 
@@ -51,38 +51,125 @@
     return jnp.where(x > -0.35, x * series, jnp.exp(x) - 1.0)
 
 
-def own_kernel(share, haplo_total, rates, hap_ref, counts_ref, std_ref, low_ref, high_ref, low_send, high_send, norm_ref, token_ref):
+def load_kernel(hap_hbm, hap_ref, out_ref, arrived):
+    parts = arrived.shape[0]
+    rows = hap_ref.shape[0] // parts
+    copies = [
+        pltpu.make_async_copy(
+            hap_hbm.at[pl.ds(k * rows, rows)], hap_ref.at[pl.ds(k * rows, rows)], arrived.at[k]
+        )
+        for k in range(parts)
+    ]
+    for copy in copies:
+        copy.start()
+    out_ref[...] = jnp.zeros_like(out_ref)
+    for k, copy in enumerate(copies):
+        copy.wait()
+        block = hap_ref[k * rows : (k + 1) * rows, :].astype(jnp.float32)
+        out_ref[...] += jnp.sum(block, axis=0, keepdims=True)
+
+
+def load(haplotypes):
+    return pl.pallas_call(
+        load_kernel,
+        in_specs=[pl.BlockSpec(memory_space=pl.ANY)],
+        out_specs=[pl.BlockSpec(memory_space=pltpu.VMEM)] * 2,
+        out_shape=[
+            jax.ShapeDtypeStruct(haplotypes.shape, haplotypes.dtype),
+            jax.ShapeDtypeStruct((1, haplotypes.shape[1]), jnp.float32),
+        ],
+        scratch_shapes=[pltpu.SemaphoreType.DMA((4,))],
+        compiler_params=pltpu.CompilerParams(vmem_limit_bytes=VMEM_LIMIT),
+        name="local_counts",
+    )(haplotypes)
+
+
+def standardize_part(raw_ref, counts_ref, first, haplo_total):
+    frequency, inverse_sd = moments(counts_ref[:, first : first + raw_ref.shape[1]], haplo_total)
+    return standardize(raw_ref[...], frequency, inverse_sd)
+
+
+def own_kernel(
+    share, haplo_total, rates, hap_ref, counts_ref,
+    std_ref, norm_ref, token_ref, high_ref, send_ref, low_ref, low_send_1, low_send_2,
+):
     token_ref[...] = jnp.zeros_like(token_ref)
-    me = lax.axis_index("genome") * lax.axis_size("samples") + lax.axis_index("samples")
+    std_ref[...] = standardize_part(hap_ref, counts_ref, 0, haplo_total)
+    mine = lax.axis_index("samples")
+    half = share // 2
+    later = std_ref[:, share:]
+    send_ref[...] = product(later, std_ref[:, columns(1 - mine, share)]).astype(jnp.bfloat16)
+    high_ref[...] = product(later, std_ref[:, columns(mine, share)])
+    low = product(std_ref[:, half:share], std_ref[:, :share])
+    low_ref[half:, :] = low
+    low_send_1[...] = low.astype(jnp.bfloat16)
+    low = product(std_ref[:, :half], std_ref[:, :half])
+    low_ref[:half, :half] = low
+    low_send_2[...] = low.astype(jnp.bfloat16)
+    me = lax.axis_index("genome") * lax.axis_size("samples") + mine
     position = (me * share + lax.broadcasted_iota(jnp.int32, (1, share), 1)).astype(jnp.float32) + 1.0
     for k, rate in enumerate(rates):
         norm_ref[k : k + 1, :] = math.expm1(rate) / expm1(position * rate)
-    frequency, inverse_sd = moments(counts_ref[...], haplo_total)
-    std_ref[...] = standardize(hap_ref[...], frequency, inverse_sd)
-    mine = lax.axis_index("samples")
-    other = 1 - mine
-    later = std_ref[:, share:]
-    high_send[...] = product(later, std_ref[:, columns(other, share)]).astype(jnp.bfloat16)
-    low = product(std_ref[:, :share], std_ref[:, :share])
-    low_ref[...] = low
-    low_send[...] = low.astype(jnp.bfloat16)
-    high_ref[...] = product(later, std_ref[:, columns(mine, share)])
-
-
-def both_kernel(first, share, haplo_total, raw_ref, counts_ref, std_ref, before_ref, keep_ref, send_ref, token_ref):
+
+
+def first_kernel(
+    share, haplo_total, raw_0, raw_1, counts_ref, std_ref, before_ref, token_ref, keep_ref, send_ref, later_ref
+):
     token_ref[...] = before_ref[...]
-    frequency, inverse_sd = moments(counts_ref[:, first : first + raw_ref.shape[1]], haplo_total)
-    later = standardize(raw_ref[...], frequency, inverse_sd)
-    mine = lax.axis_index("samples")
-    other = 1 - mine
-    send_ref[...] = product(later, std_ref[:, columns(other, share)]).astype(jnp.bfloat16)
-    keep_ref[...] = product(later, std_ref[:, columns(mine, share)])
-
-
-def last_kernel(first, haplo_total, raw_ref, counts_ref, std_ref, before_ref, keep_ref, send_ref, token_ref):
+    unit = raw_0.shape[1]
+    later_ref[:, :unit] = standardize_part(raw_0, counts_ref, 0, haplo_total)
+    later_ref[:, unit:] = standardize_part(raw_1, counts_ref, unit, haplo_total)
+    mine = lax.axis_index("samples")
+    send_ref[...] = product(later_ref[...], std_ref[:, columns(1 - mine, share)]).astype(jnp.bfloat16)
+    keep_ref[...] = product(later_ref[...], std_ref[:, columns(mine, share)])
+
+
+def middle_kernel(
+    first, share, haplo_total, raw_ref, counts_ref, std_ref, low_send_1, before_ref,
+    token_ref, keep_ref, send_ref, corner_ref, corner_send,
+):
     token_ref[...] = before_ref[...]
-    frequency, inverse_sd = moments(counts_ref[:, first : first + raw_ref.shape[1]], haplo_total)
-    later = standardize(raw_ref[...], frequency, inverse_sd)
+    later = standardize_part(raw_ref, counts_ref, first, haplo_total)
+    keep = product(later, std_ref[:, share:])
+    keep_ref[...] = keep
+    corner = product(later[:, : share - first], std_ref[:, first:share])
+    corner_ref[...] = corner
+    corner_send[...] = corner.astype(jnp.bfloat16)
+    mine = lax.axis_index("samples")
+
+    @pl.when(mine == 0)
+    def _():
+        send_ref[...] = keep.astype(jnp.bfloat16)
+
+    @pl.when(mine == 1)
+    def _():
+        send_ref[...] = low_send_1[...]
+
+
+def upper_kernel(
+    first, haplo_total, raw_ref, counts_ref, std_ref, low_send_2, corner_send, before_ref,
+    token_ref, keep_ref, send_ref,
+):
+    token_ref[...] = before_ref[...]
+    later = standardize_part(raw_ref, counts_ref, first, haplo_total)
+    keep = product(later, std_ref[:, first:])
+    keep_ref[...] = keep
+    mine = lax.axis_index("samples")
+
+    @pl.when(mine == 0)
+    def _():
+        send_ref[...] = keep.astype(jnp.bfloat16)
+
+    @pl.when(mine == 1)
+    def _():
+        half, corner = low_send_2.shape[1], corner_send.shape[0]
+        send_ref[:, :half] = low_send_2[...]
+        send_ref[:corner, half:] = corner_send[...]
+        send_ref[corner:, half:] = jnp.zeros_like(send_ref[corner:, half:])
+
+
+def last_kernel(first, haplo_total, raw_ref, counts_ref, std_ref, keep_ref, send_ref):
+    later = standardize_part(raw_ref, counts_ref, first, haplo_total)
     keep = product(later, std_ref[:, first:])
     keep_ref[...] = keep
     send_ref[...] = keep.astype(jnp.bfloat16)
@@ -101,17 +188,16 @@
     return ends_ref[...] - start
 
 
-def early_kernel(share, haplo_total, pieces, ends_ref, *refs):
-    out_ref = refs[-1]
-    mine = lax.axis_index("samples")
-    ends = local_ends(ends_ref, share)
-    out_ref[...] = jnp.zeros_like(out_ref)
-    for k, (first_column, owner) in enumerate(pieces):
-        keep, got = refs[2 * k], refs[2 * k + 1]
-
-        def add(keep=keep, got=got, first_column=first_column):
-            total = keep[...] + got[...].astype(jnp.float32)
-            out_ref[...] += window_sums(total, haplo_total, first_column, mine * share, ends)
+def add_blocks(pieces, refs, share, haplo_total, ends, out_ref):
+    mine = lax.axis_index("samples")
+    for owner, keep, keep_at, got, got_at, first_column, first_row in pieces:
+
+        def add(keep=keep, keep_at=keep_at, got=got, got_at=got_at, first_column=first_column, first_row=first_row):
+            total = refs[keep][keep_at] + refs[got][got_at].astype(jnp.float32)
+            start = first_row % share
+            inner = slice(start, start + total.shape[1])
+            row = mine * share + start
+            out_ref[:, inner] += window_sums(total, haplo_total, first_column, row, ends[:, inner])
 
         if owner is None:
             add()
@@ -119,27 +205,22 @@
             pl.when(mine == owner)(add)
 
 
+def early_kernel(share, haplo_total, pieces, ends_ref, *refs):
+    out_ref = refs[-1]
+    out_ref[...] = jnp.zeros_like(out_ref)
+    add_blocks(pieces, refs, share, haplo_total, local_ends(ends_ref, share), out_ref)
+
+
 def rates_of(share, variants):
     return (math.log(0.5) / (4 * share), math.log(0.1) / variants)
 
 
 def tail_kernel(share, haplo_total, pieces, rates, ends_ref, sums_ref, *refs):
-    n = len(pieces)
-    score_ref, local_ref, last_ref, total_ref = refs[2 * n :]
+    score_ref, local_ref, last_ref, total_ref = refs[-4:]
     mine = lax.axis_index("samples")
     ends = local_ends(ends_ref, share)
     total_ref[...] = sums_ref[...]
-    for k, (first_column, first_row, owner) in enumerate(pieces):
-        keep, got = refs[2 * k], refs[2 * k + 1]
-
-        @pl.when(mine == owner)
-        def _(keep=keep, got=got, first_column=first_column, first_row=first_row, owner=owner):
-            inner = slice(first_row - owner * share, None)
-            total = keep[...] + got[...].astype(jnp.float32)
-            total_ref[:, inner] += window_sums(
-                total, haplo_total, first_column, first_row, ends[:, inner]
-            )
-
+    add_blocks(pieces, refs, share, haplo_total, ends, total_ref)
     row = mine * share + lax.broadcasted_iota(jnp.int32, (1, share), 1)
     counted = jnp.maximum(ends - row - 1, 1).astype(jnp.float32)
     score = total_ref[...] / counted
@@ -203,63 +284,98 @@
     firsts = [unit * sum(EIGHTHS[:c]) for c in range(len(EIGHTHS))]
     sizes = [unit * e for e in EIGHTHS]
 
-    raws, counts = [], None
-    for first, size in zip(firsts, sizes):
-        raws.append(lax.ppermute(haplotypes[:, first : first + size], "genome", back))
-    counts = jnp.sum(haplotypes, axis=0, dtype=f32)[None]
+    def shifted(array, c):
+        return lax.ppermute(array[:, firsts[c] : firsts[c] + sizes[c]], "genome", back)
+
+    raws = [shifted(haplotypes, 0)]
+    haplotypes, counts = load(haplotypes)
+    raws += [shifted(haplotypes, c) for c in range(1, len(EIGHTHS))]
     if samples == 2:
         counts = counts + lax.ppermute(counts, "samples", [(0, 1), (1, 0)])
     else:
         counts = lax.psum(counts, "samples")
     next_counts = lax.ppermute(counts, "genome", back)
 
-    def swap(send, pairs):
+    def swap(send, pairs=((0, 1), (1, 0))):
         return lax.ppermute(send, "samples", pairs)
 
-    both, up, down = [(0, 1), (1, 0)], [(0, 1)], [(1, 0)]
     tails, tail_pieces = [], []
     token_type = ((8, LANES), f32)
     if samples == 2:
-        standard, low, high, low_send, high_send, norm, token = call(
+        half, u, whole = share // 2, unit, slice(None)
+        standard, norm, token, high, send, low, low_send_1, low_send_2 = call(
             functools.partial(own_kernel, share, haplo_total, rates),
-            [((depth, width), bf16)]
-            + [((share, share), f32)] * 2
-            + [((share, share), bf16)] * 2
-            + [((2, share), f32), token_type],
+            [((depth, width), bf16), ((2, share), f32), token_type]
+            + [((share, share), f32), ((share, share), bf16), ((share, share), f32)]
+            + [((half, share), bf16), ((half, half), bf16)],
             haplotypes,
             counts,
         )
-        arrays = [high, swap(high_send, both), low, swap(low_send, down)]
-        pieces = [(share, None), (0, 0)]
-        for c, (first, size) in enumerate(zip(firsts, sizes)):
-            straddles = first < share
-            rows = share if straddles else width - first
-            kernel = (
-                functools.partial(both_kernel, first, share, haplo_total)
-                if straddles
-                else functools.partial(last_kernel, first, haplo_total)
-            )
-            keep, send, token = call(
-                kernel,
-                [((size, rows), f32), ((size, rows), bf16), token_type],
-                raws[c],
-                next_counts,
-                standard,
-                token,
-            )
-            got = swap(send, both if straddles else up)
-            if straddles:
-                arrays += [keep, got]
-                pieces.append((width + first, None))
-            else:
-                tails += [keep, got]
-                tail_pieces.append((width + first, first, 1))
+        got_0 = swap(send)
+        token, keep_1, send, _ = call(
+            functools.partial(first_kernel, share, haplo_total),
+            [token_type, ((3 * u, share), f32), ((3 * u, share), bf16), ((depth, 3 * u), bf16)],
+            raws[0],
+            raws[1],
+            next_counts,
+            standard,
+            token,
+        )
+        got_1 = swap(send)
+        token, keep_2, send, corner, corner_send = call(
+            functools.partial(middle_kernel, firsts[2], share, haplo_total),
+            [token_type, ((2 * u, share), f32), ((2 * u, share), bf16), ((u, u), f32), ((u, u), bf16)],
+            raws[2],
+            next_counts,
+            standard,
+            low_send_1,
+            token,
+        )
+        got_2 = swap(send)
+        token, keep_3, send = call(
+            functools.partial(upper_kernel, firsts[3], haplo_total),
+            [token_type, ((2 * u, 3 * u), f32), ((2 * u, 3 * u), bf16)],
+            raws[3],
+            next_counts,
+            standard,
+            low_send_2,
+            corner_send,
+            token,
+        )
+        got_3 = swap(send)
+        pieces = [
+            (None, 0, (whole, whole), 1, (whole, whole), share, 0),
+            (None, 2, (whole, whole), 3, (whole, whole), width, 0),
+            (0, 4, (slice(half, None), whole), 6, (whole, whole), half, 0),
+            (1, 5, (whole, whole), 6, (whole, whole), width + firsts[2], share),
+        ]
         (sums,) = call(
             functools.partial(early_kernel, share, haplo_total, pieces),
             [((1, share), f32)],
             ends,
-            *arrays,
-        )
+            high,
+            got_0,
+            keep_1,
+            got_1,
+            low,
+            keep_2,
+            got_2,
+        )
+        keep_4, send = call(
+            functools.partial(last_kernel, firsts[4], haplo_total),
+            [((u, u), f32), ((u, u), bf16)],
+            raws[4],
+            next_counts,
+            standard,
+        )
+        got_4 = swap(send, [(0, 1)])
+        tails = [low, corner, keep_3, got_3, keep_4, got_4]
+        tail_pieces = [
+            (0, 0, (slice(0, half), slice(0, half)), 3, (whole, slice(0, half)), 0, 0),
+            (0, 1, (whole, whole), 3, (slice(0, u), slice(half, None)), width + firsts[2], firsts[2]),
+            (1, 2, (whole, whole), 3, (whole, whole), width + firsts[3], firsts[3]),
+            (1, 4, (whole, whole), 5, (whole, whole), width + firsts[4], firsts[4]),
+        ]
     else:
         frequency, inverse_sd = moments(counts, haplo_total)
         standard = standardize(haplotypes, frequency, inverse_sd)

time: 107 us -> 103 us (0.963)
  blocking collectives: 61.2 us -> 42.9 us
  waiting for transfers between devices: 7.39 us -> 25.6 us
  starting transfers between devices: 20.8 us -> 18.4 us
    ppermute x4 -> x5, waiting for transfers between devices: 0.01 us -> 20.1 us  [shifted(): lax.ppermute(array[:, firsts[c]:firsts[c] + sizes[c]], 'genome', back)]
    all_to_all x1, blocking collectives: 61.2 us -> 42.9 us  [per_device(): lax.all_to_all(last[:, None], ('genome', 'samples'), 0, 0, tiled=True)[:, 0]]
    ppermute x6 -> x5, waiting for transfers between devices: 5.79 us -> 0.67 us  [swap(): return lax.ppermute(send, 'samples', pairs)]
    ppermute x6 -> x5, starting transfers between devices: 11.2 us -> 7.64 us  [swap(): return lax.ppermute(send, 'samples', pairs)]
    ppermute x1, waiting for transfers between devices: 0.01 us -> 3.26 us  [per_device(): next_counts = lax.ppermute(counts, 'genome', back)]
    slice x3, local copies, waits for them, and re-layouts: 3.55 us -> 0.48 us  [shifted(): array[:, firsts[c]:firsts[c] + sizes[c]]]
    unnamed x4, local copies, waits for them, and re-layouts: 0.01 us -> 2.18 us
    pallas_call x0 -> x1, Pallas kernels: none -> 1.15 us  [load(): pl.pallas_call(load_kernel, in_specs=[pl.BlockSpec(memory_space=pl.ANY)],...]
  transfers between devices with their start and end apart: 12 -> 12, of which waited for: 2 -> 4; matrix products, arithmetic and copies ran while one was open for 2% -> 0% of each run, Pallas kernels for 10% -> 10%
where the time goes in v3:
time: 103 us
  blocking collectives  42.9 us (42%)
  waiting for transfers between devices  25.6 us (25%)
  starting transfers between devices  18.4 us (18%)
  Pallas kernels  12.7 us (12%)
  local copies, waits for them, and re-layouts  2.67 us (3%)
    all_to_all x1, blocking collectives, per_device(): lax.all_to_all(last[:, None], ('genome', 'samples'), 0, 0, tiled=True)[:, 0]  42.9 us
    ppermute x5, waiting for transfers between devices, shifted(): lax.ppermute(array[:, firsts[c]:firsts[c] + sizes[c]], 'genome', back)  20.1 us
    pallas_call x8, Pallas kernels, call(): pl.pallas_call(kernel, in_specs=[pl.BlockSpec(memory_space=pltpu.VMEM)] *...  11.5 us
    ppermute x5, starting transfers between devices, swap(): return lax.ppermute(send, 'samples', pairs)  7.64 us
    ppermute x5, starting transfers between devices, shifted(): lax.ppermute(array[:, firsts[c]:firsts[c] + sizes[c]], 'genome', back)  6.45 us
    ppermute x1, waiting for transfers between devices, per_device(): next_counts = lax.ppermute(counts, 'genome', back)  3.26 us
    ppermute x1, starting transfers between devices, per_device(): counts = counts + lax.ppermute(counts, 'samples', [(0, 1), (1, 0)])  3.06 us
    unnamed x4, local copies, waits for them, and re-layouts  2.18 us
  transfers between devices with their start and end apart: 12, of which 4 were waited for; matrix products, arithmetic and copies ran while one was open for 0% of the time, Pallas kernels for 10%

profile of v3, /device:TPU:0, one launch (start us, length us, event | category | flops | bytes accessed | tf_op | source)
XLA Modules:
  0.0 103.0 jit_solution(9969012289201696929)
XLA Ops:
  0.6 0.0 copy-start
  0.6 2.2 %copy-done = bf16[2048,1024]{1,0:T(8,128)(2,1)S(1)} copy-done((bf16[2048,1024]{1,0:T(8,128)(2,1)S(1)}, bf16[2048,1024]{1,0:T(8,128)(2,1)}, u32[]{:S(2)}) %copy-start) | copy-done | bytes 4194328
  2.8 1.2 %local_counts.1 = (bf16[2048,1024]{1,0:T(8,128)(2,1)S(1)}, f32[1,1024]{1,0:T(1,128)S(1)}) custom-call(bf16[2048,1024]{1,0:T(8,128)(2,1)S(1)} %copy-done), custom_call_target="tpu_custom_call" | custom-call | tf_op jit(solution)/shard_map/local_counts/pallas_call | solution.py:73
  4.0 0.2 fusion
  4.2 1.3 %collective-permute-start.3 = (bf16[2048,256]{1,0:T(8,128)(2,1)S(1)}, bf16[2048,256]{1,0:T(8,128)(2,1)S(1)}, u32[]{:S(2)}, u32[]{:S(2)}) collective-permute-start(bf16[2048,256]{1,0:T(8,128)(2,1)S(1)} %get-tuple-element.54), channel_id=1, source_target_pairs={{2,0},{4,2},{6,4},{8,6},{10,8},{12,10},{14,12},{16,14},{18,16},{20... | collective-permute-start | bytes 3145736 | tf_op jit(solution)/shard_map/ppermute | solution.py:288
  5.5 1.3 %collective-permute-start.6 = (bf16[2048,256]{1,0:T(8,128)(2,1)S(1)}, bf16[2048,256]{1,0:T(8,128)(2,1)S(1)}, u32[]{:S(2)}, u32[]{:S(2)}) collective-permute-start(bf16[2048,256]{1,0:T(8,128)(2,1)S(1)} %get-tuple-element.53), channel_id=1, source_target_pairs={{2,0},{4,2},{6,4},{8,6},{10,8},{12,10},{14,12},{16,14},{18,16},{20... | collective-permute-start | bytes 3145736 | tf_op jit(solution)/shard_map/ppermute | solution.py:288
  6.8 1.3 %collective-permute-start.8 = (bf16[2048,256]{1,0:T(8,128)(2,1)S(1)}, bf16[2048,256]{1,0:T(8,128)(2,1)S(1)}, u32[]{:S(2)}, u32[]{:S(2)}) collective-permute-start(bf16[2048,256]{1,0:T(8,128)(2,1)S(1)} %get-tuple-element.52), channel_id=1, source_target_pairs={{2,0},{4,2},{6,4},{8,6},{10,8},{12,10},{14,12},{16,14},{18,16},{20... | collective-permute-start | bytes 3145736 | tf_op jit(solution)/shard_map/ppermute | solution.py:288
  8.1 0.1 slice.15
  8.2 1.3 %collective-permute-start.2 = (bf16[2048,128]{1,0:T(8,128)(2,1)S(1)}, bf16[2048,128]{1,0:T(8,128)(2,1)S(1)}, u32[]{:S(2)}, u32[]{:S(2)}) collective-permute-start(bf16[2048,128]{1,0:T(8,128)(2,1)S(1)} %slice.15), channel_id=1, source_target_pairs={{2,0},{4,2},{6,4},{8,6},{10,8},{12,10},{14,12},{16,14},{18,16},{20... | collective-permute-start | bytes 1572872 | tf_op jit(solution)/shard_map/ppermute | solution.py:288
  9.5 3.1 %collective-permute-start = (f32[1,1024]{1,0:T(1,128)S(1)}, f32[1,1024]{1,0:T(1,128)S(1)}, u32[]{:S(2)}, u32[]{:S(2)}) collective-permute-start(f32[1,1024]{1,0:T(1,128)S(1)} %get-tuple-element.28), channel_id=1, source_target_pairs={{0,1},{1,0},{2,3},{3,2},{4,5},{5,4},{6,7},{7,6},{8,9},{9,8},{10,11... | collective-permute-start | bytes 12296 | tf_op jit(solution)/shard_map/ppermute | solution.py:294
  12.6 1.6 %collective-permute-done = f32[1,1024]{1,0:T(1,128)S(1)} collective-permute-done((f32[1,1024]{1,0:T(1,128)S(1)}, f32[1,1024]{1,0:T(1,128)S(1)}, u32[]{:S(2)}, u32[]{:S(2)}) %collective-permute-start) | collective-permute-done | bytes 4128 | tf_op jit(solution)/shard_map/ppermute | solution.py:294
  14.2 1.3 %collective-permute-start.4 = (f32[1,1024]{1,0:T(1,128)S(1)}, f32[1,1024]{1,0:T(1,128)S(1)}, u32[]{:S(2)}, u32[]{:S(2)}) collective-permute-start(f32[1,1024]{1,0:T(1,128)S(1)} %add.3.counts_ref), channel_id=1, source_target_pairs={{2,0},{4,2},{6,4},{8,6},{10,8},{12,10},{14,12},{16,14},{18,16},{20... | collective-permute-start | bytes 12296 | tf_op jit(solution)/shard_map/ppermute | solution.py:297
  15.5 0.1 slice.19
  15.6 3.3 %collective-permute-done.4.counts_ref = f32[1,1024]{1,0:T(1,128)S(1)} collective-permute-done((f32[1,1024]{1,0:T(1,128)S(1)}, f32[1,1024]{1,0:T(1,128)S(1)}, u32[]{:S(2)}, u32[]{:S(2)}) %collective-permute-start.4) | collective-permute-done | bytes 4128 | tf_op jit(solution)/shard_map/ppermute | solution.py:297
  18.9 1.3 %collective-permute-start.10 = (bf16[2048,128]{1,0:T(8,128)(2,1)S(1)}, bf16[2048,128]{1,0:T(8,128)(2,1)S(1)}, u32[]{:S(2)}, u32[]{:S(2)}) collective-permute-start(bf16[2048,128]{1,0:T(8,128)(2,1)S(1)} %slice.19), channel_id=1, source_target_pairs={{2,0},{4,2},{6,4},{8,6},{10,8},{12,10},{14,12},{16,14},{18,16},{20... | collective-permute-start | bytes 1572872 | tf_op jit(solution)/shard_map/ppermute | solution.py:288
  20.2 4.2 %shard_map.41 = (bf16[2048,1024]{1,0:T(8,128)(2,1)S(1)}, f32[2,512]{1,0:T(2,128)S(1)}, f32[8,128]{1,0:T(8,128)S(1)}, f32[512,512]{1,0:T(8,128)S(1)}, bf16[512,51...) custom-call(bf16[2048,1024]{1,0:T(8,128)(2,1)S(1)} %get-tuple-element.2, ...), custom_call_target="tpu_custom_call" | custom-call | tf_op jit(solution)/shard_map/pallas_call | solution.py:34
  24.4 0.0 collective-permute-done.2.raw_0
  24.4 1.8 %collective-permute-start.1 = (bf16[512,512]{1,0:T(8,128)(2,1)S(1)}, bf16[512,512]{1,0:T(8,128)(2,1)S(1)}, u32[]{:S(2)}, u32[]{:S(2)}) collective-permute-start(bf16[512,512]{1,0:T(8,128)(2,1)S(1)} %get-tuple-element.30), channel_id=1, source_target_pairs={{0,1},{1,0},{2,3},{3,2},{4,5},{5,4},{6,7},{7,6},{8,9},{9,8},{10,11... | collective-permute-start | bytes 1572872 | tf_op jit(solution)/shard_map/ppermute | solution.py:300
  26.2 0.0 collective-permute-done.3.raw_1
  26.2 2.1 %shard_map.42 = (f32[8,128]{1,0:T(8,128)S(1)}, f32[384,512]{1,0:T(8,128)S(1)}, bf16[384,512]{1,0:T(8,128)(2,1)S(1)}, bf16[2048,384]{1,0:T(8,128)(2,1)}) custom-call(bf16[2048,128]{1,0:T(8,128)(2,1)S(1)} %collective-permute-done.2.raw_0, bf16[2048,256]{1,0:T(8,128)(2,1)S(1)} %collective-permute-done.3.raw_1, f32[1,1024]{1,0:T(1,128)S(1)} %collective-permute-done.4.counts_ref, ...), custom_call_target="tpu_custom_call" | custom-call | tf_op jit(solution)/shard_map/pallas_call | solution.py:34
  28.3 0.3 collective-permute-start.5
  28.6 0.0 collective-permute-done.6.raw_ref
  28.6 1.0 shard_map.43
  29.6 1.8 %collective-permute-start.7 = (bf16[256,512]{1,0:T(8,128)(2,1)S(1)}, bf16[256,512]{1,0:T(8,128)(2,1)S(1)}, u32[]{:S(2)}, u32[]{:S(2)}) collective-permute-start(bf16[256,512]{1,0:T(8,128)(2,1)S(1)} %get-tuple-element.39), channel_id=1, source_target_pairs={{0,1},{1,0},{2,3},{3,2},{4,5},{5,4},{6,7},{7,6},{8,9},{9,8},{10,11... | collective-permute-start | bytes 786440 | tf_op jit(solution)/shard_map/ppermute | solution.py:300
  31.4 0.0 collective-permute-done.8.raw_ref
  31.4 0.0 copy-start.1
  31.4 1.4 %shard_map.45 = (f32[8,128]{1,0:T(8,128)}, f32[256,384]{1,0:T(8,128)S(1)}, bf16[256,384]{1,0:T(8,128)(2,1)S(1)}) custom-call(bf16[2048,256]{1,0:T(8,128)(2,1)S(1)} %collective-permute-done.8.raw_ref, f32[1,1024]{1,0:T(1,128)S(1)} %collective-permute-done.4.counts_ref, bf16[2048,1024]{1,0:T(8,128)(2,1)S(1)} %get-tuple-element.31.std_ref, ...), custom_call_target="tpu_custom_call" | custom-call | tf_op jit(solution)/shard_map/pallas_call | solution.py:34
  32.8 0.3 collective-permute-start.9
  33.0 20.0 %collective-permute-done.10.raw_ref = bf16[2048,128]{1,0:T(8,128)(2,1)S(1)} collective-permute-done((bf16[2048,128]{1,0:T(8,128)(2,1)S(1)}, bf16[2048,128]{1,0:T(8,128)(2,1)S(1)}, u32[]{:S(2)}, u32[]{:S(2)}) %collective-permute-start.10) | collective-permute-done | bytes 524320 | tf_op jit(solution)/shard_map/ppermute | solution.py:288
  53.1 0.4 shard_map.46
  53.5 3.4 %collective-permute-start.11 = (bf16[128,128]{1,0:T(8,128)(2,1)S(1)}, bf16[128,128]{1,0:T(8,128)(2,1)S(1)}, u32[]{:S(2)}, u32[]{:S(2)}) collective-permute-start(bf16[128,128]{1,0:T(8,128)(2,1)S(1)} %get-tuple-element.47), channel_id=1, source_target_pairs={{0,1},{2,3},{4,5},{6,7},{8,9},{10,11},{12,13},{14,15},{16,17},{18,... | collective-permute-start | bytes 98312 | tf_op jit(solution)/shard_map/ppermute | solution.py:300
  56.9 0.0 collective-permute-done.1.refs_1_
  56.9 0.0 collective-permute-done.7.refs_6_
  56.9 0.0 collective-permute-done.5.refs_3_
  56.9 0.0 copy-done.1
  56.9 1.1 %shard_map.44.sums_ref = f32[1,512]{1,0:T(1,128)S(1)} custom-call(s32[1,512]{1,0:T(1,128)S(1)} %bitcast.8, f32[512,512]{1,0:T(8,128)S(1)} %get-tuple-element.29.refs_0_, bf16[512,512]{1,0:T(8,128)(2,1)S(1)} %collective-permute-done.1.refs_1_, f32[384,512]{1,0:T(8,128)S(1)} %get-tuple-element.33.refs_2_, bf16[384,512]{1,0:T(8,128)(2,1)S(1)} %collective-permute-done.5.refs_3_, ...), custom_call_target="tpu_custom_call" | custom-call | tf_op jit(solution)/shard_map/pallas_call | solution.py:34
  58.0 0.7 collective-permute-done.11.refs_5_
  58.6 0.0 collective-permute-done.9.refs_3_
  58.6 0.8 shard_map.47
  59.5 42.9 %all_to_all.5 = f32[32,1,128]{2,1,0:T(1,128)S(1)} all-to-all(f32[32,1,128]{2,1,0:T(1,128)S(1)} %bitcast.7), channel_id=1, replica_groups=mesh['genome'=16,'samples'=2] {'genome','samples'}, dimensions={0} | all-to-all | bytes 32768 | tf_op jit(solution)/shard_map/all_to_all | solution.py:409
  102.3 0.7 shard_map.48
  (1 shorter events, 0.0 us)
Async XLA Ops:
  0.6 2.2 %copy-start = (bf16[2048,1024]{1,0:T(8,128)(2,1)S(1)}, bf16[2048,1024]{1,0:T(8,128)(2,1)}, u32[]{:S(2)}) copy-start(bf16[2048,1024]{1,0:T(8,128)(2,1)} %hap_hbm.1) | copy-start | bytes 12582916
  4.2 22.0 %collective-permute-start.3 = (bf16[2048,256]{1,0:T(8,128)(2,1)S(1)}, bf16[2048,256]{1,0:T(8,128)(2,1)S(1)}, u32[]{:S(2)}, u32[]{:S(2)}) collective-permute-start(bf16[2048,256]{1,0:T(8,128)(2,1)S(1)} %get-tuple-element.54), channel_id=1, source_target_pairs={{2,0},{4,2},{6,4},{8,6},{10,8},{12,10},{14,12},{16,14},{18,16},{20... | collective-permute-start | bytes 3145736 | tf_op jit(solution)/shard_map/ppermute | solution.py:288
  5.5 23.1 %collective-permute-start.6 = (bf16[2048,256]{1,0:T(8,128)(2,1)S(1)}, bf16[2048,256]{1,0:T(8,128)(2,1)S(1)}, u32[]{:S(2)}, u32[]{:S(2)}) collective-permute-start(bf16[2048,256]{1,0:T(8,128)(2,1)S(1)} %get-tuple-element.53), channel_id=1, source_target_pairs={{2,0},{4,2},{6,4},{8,6},{10,8},{12,10},{14,12},{16,14},{18,16},{20... | collective-permute-start | bytes 3145736 | tf_op jit(solution)/shard_map/ppermute | solution.py:288
  6.8 24.6 %collective-permute-start.8 = (bf16[2048,256]{1,0:T(8,128)(2,1)S(1)}, bf16[2048,256]{1,0:T(8,128)(2,1)S(1)}, u32[]{:S(2)}, u32[]{:S(2)}) collective-permute-start(bf16[2048,256]{1,0:T(8,128)(2,1)S(1)} %get-tuple-element.52), channel_id=1, source_target_pairs={{2,0},{4,2},{6,4},{8,6},{10,8},{12,10},{14,12},{16,14},{18,16},{20... | collective-permute-start | bytes 3145736 | tf_op jit(solution)/shard_map/ppermute | solution.py:288
  8.2 16.1 %collective-permute-start.2 = (bf16[2048,128]{1,0:T(8,128)(2,1)S(1)}, bf16[2048,128]{1,0:T(8,128)(2,1)S(1)}, u32[]{:S(2)}, u32[]{:S(2)}) collective-permute-start(bf16[2048,128]{1,0:T(8,128)(2,1)S(1)} %slice.15), channel_id=1, source_target_pairs={{2,0},{4,2},{6,4},{8,6},{10,8},{12,10},{14,12},{16,14},{18,16},{20... | collective-permute-start | bytes 1572872 | tf_op jit(solution)/shard_map/ppermute | solution.py:288
  9.5 4.6 %collective-permute-start = (f32[1,1024]{1,0:T(1,128)S(1)}, f32[1,1024]{1,0:T(1,128)S(1)}, u32[]{:S(2)}, u32[]{:S(2)}) collective-permute-start(f32[1,1024]{1,0:T(1,128)S(1)} %get-tuple-element.28), channel_id=1, source_target_pairs={{0,1},{1,0},{2,3},{3,2},{4,5},{5,4},{6,7},{7,6},{8,9},{9,8},{10,11... | collective-permute-start | bytes 12296 | tf_op jit(solution)/shard_map/ppermute | solution.py:294
  14.2 4.7 %collective-permute-start.4 = (f32[1,1024]{1,0:T(1,128)S(1)}, f32[1,1024]{1,0:T(1,128)S(1)}, u32[]{:S(2)}, u32[]{:S(2)}) collective-permute-start(f32[1,1024]{1,0:T(1,128)S(1)} %add.3.counts_ref), channel_id=1, source_target_pairs={{2,0},{4,2},{6,4},{8,6},{10,8},{12,10},{14,12},{16,14},{18,16},{20... | collective-permute-start | bytes 12296 | tf_op jit(solution)/shard_map/ppermute | solution.py:297
  18.9 34.2 %collective-permute-start.10 = (bf16[2048,128]{1,0:T(8,128)(2,1)S(1)}, bf16[2048,128]{1,0:T(8,128)(2,1)S(1)}, u32[]{:S(2)}, u32[]{:S(2)}) collective-permute-start(bf16[2048,128]{1,0:T(8,128)(2,1)S(1)} %slice.19), channel_id=1, source_target_pairs={{2,0},{4,2},{6,4},{8,6},{10,8},{12,10},{14,12},{16,14},{18,16},{20... | collective-permute-start | bytes 1572872 | tf_op jit(solution)/shard_map/ppermute | solution.py:288
  24.4 32.5 %collective-permute-start.1 = (bf16[512,512]{1,0:T(8,128)(2,1)S(1)}, bf16[512,512]{1,0:T(8,128)(2,1)S(1)}, u32[]{:S(2)}, u32[]{:S(2)}) collective-permute-start(bf16[512,512]{1,0:T(8,128)(2,1)S(1)} %get-tuple-element.30), channel_id=1, source_target_pairs={{0,1},{1,0},{2,3},{3,2},{4,5},{5,4},{6,7},{7,6},{8,9},{9,8},{10,11... | collective-permute-start | bytes 1572872 | tf_op jit(solution)/shard_map/ppermute | solution.py:300
  28.3 28.6 %collective-permute-start.5 = (bf16[384,512]{1,0:T(8,128)(2,1)S(1)}, bf16[384,512]{1,0:T(8,128)(2,1)S(1)}, u32[]{:S(2)}, u32[]{:S(2)}) collective-permute-start(bf16[384,512]{1,0:T(8,128)(2,1)S(1)} %get-tuple-element.34), channel_id=1, source_target_pairs={{0,1},{1,0},{2,3},{3,2},{4,5},{5,4},{6,7},{7,6},{8,9},{9,8},{10,11... | collective-permute-start | bytes 1179656 | tf_op jit(solution)/shard_map/ppermute | solution.py:300
  29.6 27.3 %collective-permute-start.7 = (bf16[256,512]{1,0:T(8,128)(2,1)S(1)}, bf16[256,512]{1,0:T(8,128)(2,1)S(1)}, u32[]{:S(2)}, u32[]{:S(2)}) collective-permute-start(bf16[256,512]{1,0:T(8,128)(2,1)S(1)} %get-tuple-element.39), channel_id=1, source_target_pairs={{0,1},{1,0},{2,3},{3,2},{4,5},{5,4},{6,7},{7,6},{8,9},{9,8},{10,11... | collective-permute-start | bytes 786440 | tf_op jit(solution)/shard_map/ppermute | solution.py:300
  31.4 25.6 %copy-start.1 = (s32[512]{0:T(512)S(1)}, s32[512]{0:T(512)}, u32[]{:S(2)}) copy-start(s32[512]{0:T(512)} %param.3) | copy-start | bytes 6148
  32.8 25.9 %collective-permute-start.9 = (bf16[256,384]{1,0:T(8,128)(2,1)S(1)}, bf16[256,384]{1,0:T(8,128)(2,1)S(1)}, u32[]{:S(2)}, u32[]{:S(2)}) collective-permute-start(bf16[256,384]{1,0:T(8,128)(2,1)S(1)} %get-tuple-element.45), channel_id=1, source_target_pairs={{0,1},{1,0},{2,3},{3,2},{4,5},{5,4},{6,7},{7,6},{8,9},{9,8},{10,11... | collective-permute-start | bytes 589832 | tf_op jit(solution)/shard_map/ppermute | solution.py:300
  53.5 5.2 %collective-permute-start.11 = (bf16[128,128]{1,0:T(8,128)(2,1)S(1)}, bf16[128,128]{1,0:T(8,128)(2,1)S(1)}, u32[]{:S(2)}, u32[]{:S(2)}) collective-permute-start(bf16[128,128]{1,0:T(8,128)(2,1)S(1)} %get-tuple-element.47), channel_id=1, source_target_pairs={{0,1},{2,3},{4,5},{6,7},{8,9},{10,11},{12,13},{14,15},{16,17},{18,... | collective-permute-start | bytes 98312 | tf_op jit(solution)/shard_map/ppermute | solution.py:300

commit v4 on v3

--- a/solution.py
+++ b/solution.py
@@ -10,7 +10,7 @@
 
 
 LANES = 128
-EIGHTHS = (1, 2, 2, 2, 1)
+EIGHTHS = (2, 2, 2, 1, 1)
 VMEM_LIMIT = 20 * 2**20
 variance_floor = 0.01
 
@@ -72,7 +72,7 @@
 def load(haplotypes):
     return pl.pallas_call(
         load_kernel,
-        in_specs=[pl.BlockSpec(memory_space=pl.ANY)],
+        in_specs=[pl.BlockSpec(memory_space=pltpu.HBM)],
         out_specs=[pl.BlockSpec(memory_space=pltpu.VMEM)] * 2,
         out_shape=[
             jax.ShapeDtypeStruct(haplotypes.shape, haplotypes.dtype),
@@ -81,7 +81,7 @@
         scratch_shapes=[pltpu.SemaphoreType.DMA((4,))],
         compiler_params=pltpu.CompilerParams(vmem_limit_bytes=VMEM_LIMIT),
         name="local_counts",
-    )(haplotypes)
+    )(pltpu.with_memory_space_constraint(haplotypes, pltpu.HBM))
 
 
 def standardize_part(raw_ref, counts_ref, first, haplo_total):
@@ -113,28 +113,31 @@
 
 
 def first_kernel(
-    share, haplo_total, raw_0, raw_1, counts_ref, std_ref, before_ref, token_ref, keep_ref, send_ref, later_ref
+    share, haplo_total, raw_0, raw_1, counts_ref, std_ref, low_send_2, before_ref,
+    token_ref, keep_ref, send_ref, later_ref,
 ):
     token_ref[...] = before_ref[...]
-    unit = raw_0.shape[1]
-    later_ref[:, :unit] = standardize_part(raw_0, counts_ref, 0, haplo_total)
-    later_ref[:, unit:] = standardize_part(raw_1, counts_ref, unit, haplo_total)
+    half = raw_0.shape[1]
+    later_ref[:, :half] = standardize_part(raw_0, counts_ref, 0, haplo_total)
+    later_ref[:, half:] = standardize_part(raw_1, counts_ref, half, haplo_total)
     mine = lax.axis_index("samples")
     send_ref[...] = product(later_ref[...], std_ref[:, columns(1 - mine, share)]).astype(jnp.bfloat16)
+
+    @pl.when(mine == 1)
+    def _():
+        send_ref[half:, :half] = low_send_2[...]
+
     keep_ref[...] = product(later_ref[...], std_ref[:, columns(mine, share)])
 
 
 def middle_kernel(
     first, share, haplo_total, raw_ref, counts_ref, std_ref, low_send_1, before_ref,
-    token_ref, keep_ref, send_ref, corner_ref, corner_send,
+    token_ref, keep_ref, send_ref,
 ):
     token_ref[...] = before_ref[...]
     later = standardize_part(raw_ref, counts_ref, first, haplo_total)
     keep = product(later, std_ref[:, share:])
     keep_ref[...] = keep
-    corner = product(later[:, : share - first], std_ref[:, first:share])
-    corner_ref[...] = corner
-    corner_send[...] = corner.astype(jnp.bfloat16)
     mine = lax.axis_index("samples")
 
     @pl.when(mine == 0)
@@ -147,28 +150,9 @@
 
 
 def upper_kernel(
-    first, haplo_total, raw_ref, counts_ref, std_ref, low_send_2, corner_send, before_ref,
-    token_ref, keep_ref, send_ref,
+    first, haplo_total, raw_ref, counts_ref, std_ref, before_ref, token_ref, keep_ref, send_ref
 ):
     token_ref[...] = before_ref[...]
-    later = standardize_part(raw_ref, counts_ref, first, haplo_total)
-    keep = product(later, std_ref[:, first:])
-    keep_ref[...] = keep
-    mine = lax.axis_index("samples")
-
-    @pl.when(mine == 0)
-    def _():
-        send_ref[...] = keep.astype(jnp.bfloat16)
-
-    @pl.when(mine == 1)
-    def _():
-        half, corner = low_send_2.shape[1], corner_send.shape[0]
-        send_ref[:, :half] = low_send_2[...]
-        send_ref[:corner, half:] = corner_send[...]
-        send_ref[corner:, half:] = jnp.zeros_like(send_ref[corner:, half:])
-
-
-def last_kernel(first, haplo_total, raw_ref, counts_ref, std_ref, keep_ref, send_ref):
     later = standardize_part(raw_ref, counts_ref, first, haplo_total)
     keep = product(later, std_ref[:, first:])
     keep_ref[...] = keep
@@ -302,7 +286,7 @@
     tails, tail_pieces = [], []
     token_type = ((8, LANES), f32)
     if samples == 2:
-        half, u, whole = share // 2, unit, slice(None)
+        half, whole = share // 2, slice(None)
         standard, norm, token, high, send, low, low_send_1, low_send_2 = call(
             functools.partial(own_kernel, share, haplo_total, rates),
             [((depth, width), bf16), ((2, share), f32), token_type]
@@ -314,17 +298,18 @@
         got_0 = swap(send)
         token, keep_1, send, _ = call(
             functools.partial(first_kernel, share, haplo_total),
-            [token_type, ((3 * u, share), f32), ((3 * u, share), bf16), ((depth, 3 * u), bf16)],
+            [token_type, ((share, share), f32), ((share, share), bf16), ((depth, share), bf16)],
             raws[0],
             raws[1],
             next_counts,
             standard,
+            low_send_2,
             token,
         )
         got_1 = swap(send)
-        token, keep_2, send, corner, corner_send = call(
+        token, keep_2, send = call(
             functools.partial(middle_kernel, firsts[2], share, haplo_total),
-            [token_type, ((2 * u, share), f32), ((2 * u, share), bf16), ((u, u), f32), ((u, u), bf16)],
+            [token_type, ((half, share), f32), ((half, share), bf16)],
             raws[2],
             next_counts,
             standard,
@@ -332,22 +317,27 @@
             token,
         )
         got_2 = swap(send)
-        token, keep_3, send = call(
-            functools.partial(upper_kernel, firsts[3], haplo_total),
-            [token_type, ((2 * u, 3 * u), f32), ((2 * u, 3 * u), bf16)],
-            raws[3],
-            next_counts,
-            standard,
-            low_send_2,
-            corner_send,
-            token,
-        )
-        got_3 = swap(send)
+        tails = []
+        for c in (3, 4):
+            shape = (sizes[c], width - firsts[c])
+            token, keep, send = call(
+                functools.partial(upper_kernel, firsts[c], haplo_total),
+                [token_type, (shape, f32), (shape, bf16)],
+                raws[c],
+                next_counts,
+                standard,
+                token,
+            )
+            tails += [keep, swap(send, [(0, 1)])]
+        lower, upper = slice(0, half), slice(half, None)
         pieces = [
             (None, 0, (whole, whole), 1, (whole, whole), share, 0),
-            (None, 2, (whole, whole), 3, (whole, whole), width, 0),
-            (0, 4, (slice(half, None), whole), 6, (whole, whole), half, 0),
-            (1, 5, (whole, whole), 6, (whole, whole), width + firsts[2], share),
+            (0, 2, (lower, whole), 3, (lower, whole), width, 0),
+            (0, 2, (upper, upper), 3, (upper, upper), width + half, half),
+            (1, 2, (whole, whole), 3, (whole, whole), width, share),
+            (0, 4, (lower, lower), 3, (upper, lower), 0, 0),
+            (0, 4, (upper, whole), 6, (whole, whole), half, 0),
+            (1, 5, (whole, whole), 6, (whole, whole), width + share, share),
         ]
         (sums,) = call(
             functools.partial(early_kernel, share, haplo_total, pieces),
@@ -361,20 +351,9 @@
             keep_2,
             got_2,
         )
-        keep_4, send = call(
-            functools.partial(last_kernel, firsts[4], haplo_total),
-            [((u, u), f32), ((u, u), bf16)],
-            raws[4],
-            next_counts,
-            standard,
-        )
-        got_4 = swap(send, [(0, 1)])
-        tails = [low, corner, keep_3, got_3, keep_4, got_4]
         tail_pieces = [
-            (0, 0, (slice(0, half), slice(0, half)), 3, (whole, slice(0, half)), 0, 0),
-            (0, 1, (whole, whole), 3, (slice(0, u), slice(half, None)), width + firsts[2], firsts[2]),
-            (1, 2, (whole, whole), 3, (whole, whole), width + firsts[3], firsts[3]),
-            (1, 4, (whole, whole), 5, (whole, whole), width + firsts[4], firsts[4]),
+            (1, 2 * k, (whole, whole), 2 * k + 1, (whole, whole), width + firsts[c], firsts[c])
+            for k, c in enumerate((3, 4))
         ]
     else:
         frequency, inverse_sd = moments(counts, haplo_total)

time: 103 us -> 101 us (0.981)
  waiting for transfers between devices: 25.6 us -> 21.7 us
  starting transfers between devices: 18.4 us -> 20.3 us
  Pallas kernels: 12.7 us -> 13.9 us
  local copies, waits for them, and re-layouts: 2.67 us -> 1.57 us
    ppermute x5, waiting for transfers between devices: 20.1 us -> 16.1 us  [shifted(): lax.ppermute(array[:, firsts[c]:firsts[c] + sizes[c]], 'genome', back)]
    unnamed x4 -> x2, local copies, waits for them, and re-layouts: 2.18 us -> 0.01 us
    ppermute x5, starting transfers between devices: 7.64 us -> 9.53 us  [swap(): return lax.ppermute(send, 'samples', pairs)]
    pallas_call x1, Pallas kernels: 1.15 us -> 2.42 us  [load(): pl.pallas_call(load_kernel, in_specs=[pl.BlockSpec(memory_space=pltpu.HBM...]
    slice x3, local copies, waits for them, and re-layouts: 0.48 us -> 1.57 us  [shifted(): array[:, firsts[c]:firsts[c] + sizes[c]]]
  transfers between devices with their start and end apart: 12 -> 12, of which waited for: 4 -> 4; matrix products, arithmetic and copies ran while one was open for 0% -> 0% of each run, Pallas kernels for 10% -> 12%
where the time goes in v4:
time: 101 us
  blocking collectives  42.5 us (42%)
  waiting for transfers between devices  21.7 us (21%)
  starting transfers between devices  20.3 us (20%)
  Pallas kernels  13.9 us (14%)
  local copies, waits for them, and re-layouts  1.57 us (2%)
    all_to_all x1, blocking collectives, per_device(): lax.all_to_all(last[:, None], ('genome', 'samples'), 0, 0, tiled=True)[:, 0]  42.5 us
    ppermute x5, waiting for transfers between devices, shifted(): lax.ppermute(array[:, firsts[c]:firsts[c] + sizes[c]], 'genome', back)  16.1 us
    pallas_call x8, Pallas kernels, call(): pl.pallas_call(kernel, in_specs=[pl.BlockSpec(memory_space=pltpu.VMEM)] *...  11.4 us
    ppermute x5, starting transfers between devices, swap(): return lax.ppermute(send, 'samples', pairs)  9.53 us
    ppermute x5, starting transfers between devices, shifted(): lax.ppermute(array[:, firsts[c]:firsts[c] + sizes[c]], 'genome', back)  6.45 us
    ppermute x1, waiting for transfers between devices, per_device(): next_counts = lax.ppermute(counts, 'genome', back)  3.4 us
    ppermute x1, starting transfers between devices, per_device(): counts = counts + lax.ppermute(counts, 'samples', [(0, 1), (1, 0)])  3.06 us
    pallas_call x1, Pallas kernels, load(): pl.pallas_call(load_kernel, in_specs=[pl.BlockSpec(memory_space=pltpu.HBM...  2.42 us
  transfers between devices with their start and end apart: 12, of which 4 were waited for; matrix products, arithmetic and copies ran while one was open for 0% of the time, Pallas kernels for 12%

profile of v4, /device:TPU:0, one launch (start us, length us, event | category | flops | bytes accessed | tf_op | source)
XLA Modules:
  0.0 100.7 jit_solution(5604497654392543462)
XLA Ops:
  0.6 1.3 %slice.15 = bf16[2048,256]{1,0:T(8,128)(2,1)S(1)} slice(bf16[2048,1024]{1,0:T(8,128)(2,1)} %hap_hbm.1), slice={[0:2048], [0:256]} | slice | bytes 2097152 | tf_op jit(solution)/shard_map/slice | solution.py:272
  1.9 1.3 %collective-permute-start.2 = (bf16[2048,256]{1,0:T(8,128)(2,1)S(1)}, bf16[2048,256]{1,0:T(8,128)(2,1)S(1)}, u32[]{:S(2)}, u32[]{:S(2)}) collective-permute-start(bf16[2048,256]{1,0:T(8,128)(2,1)S(1)} %slice.15), channel_id=1, source_target_pairs={{2,0},{4,2},{6,4},{8,6},{10,8},{12,10},{14,12},{16,14},{18,16},{20... | collective-permute-start | bytes 3145736 | tf_op jit(solution)/shard_map/ppermute | solution.py:272
  3.2 2.4 %local_counts.1 = (bf16[2048,1024]{1,0:T(8,128)(2,1)S(1)}, f32[1,1024]{1,0:T(1,128)S(1)}) custom-call(bf16[2048,1024]{1,0:T(8,128)(2,1)} %hap_hbm.1), custom_call_target="tpu_custom_call" | custom-call | tf_op jit(solution)/shard_map/local_counts/pallas_call | solution.py:73
  5.7 0.1 fusion.1
  5.8 1.3 %collective-permute-start.3 = (bf16[2048,256]{1,0:T(8,128)(2,1)S(1)}, bf16[2048,256]{1,0:T(8,128)(2,1)S(1)}, u32[]{:S(2)}, u32[]{:S(2)}) collective-permute-start(bf16[2048,256]{1,0:T(8,128)(2,1)S(1)} %get-tuple-element.53), channel_id=1, source_target_pairs={{2,0},{4,2},{6,4},{8,6},{10,8},{12,10},{14,12},{16,14},{18,16},{20... | collective-permute-start | bytes 3145736 | tf_op jit(solution)/shard_map/ppermute | solution.py:272
  7.1 1.3 %collective-permute-start.6 = (bf16[2048,256]{1,0:T(8,128)(2,1)S(1)}, bf16[2048,256]{1,0:T(8,128)(2,1)S(1)}, u32[]{:S(2)}, u32[]{:S(2)}) collective-permute-start(bf16[2048,256]{1,0:T(8,128)(2,1)S(1)} %get-tuple-element.52), channel_id=1, source_target_pairs={{2,0},{4,2},{6,4},{8,6},{10,8},{12,10},{14,12},{16,14},{18,16},{20... | collective-permute-start | bytes 3145736 | tf_op jit(solution)/shard_map/ppermute | solution.py:272
  8.4 0.1 fusion
  8.5 1.3 %collective-permute-start.8 = (bf16[2048,128]{1,0:T(8,128)(2,1)S(1)}, bf16[2048,128]{1,0:T(8,128)(2,1)S(1)}, u32[]{:S(2)}, u32[]{:S(2)}) collective-permute-start(bf16[2048,128]{1,0:T(8,128)(2,1)S(1)} %get-tuple-element.51), channel_id=1, source_target_pairs={{2,0},{4,2},{6,4},{8,6},{10,8},{12,10},{14,12},{16,14},{18,16},{20... | collective-permute-start | bytes 1572872 | tf_op jit(solution)/shard_map/ppermute | solution.py:272
  9.8 3.1 %collective-permute-start = (f32[1,1024]{1,0:T(1,128)S(1)}, f32[1,1024]{1,0:T(1,128)S(1)}, u32[]{:S(2)}, u32[]{:S(2)}) collective-permute-start(f32[1,1024]{1,0:T(1,128)S(1)} %get-tuple-element.27), channel_id=1, source_target_pairs={{0,1},{1,0},{2,3},{3,2},{4,5},{5,4},{6,7},{7,6},{8,9},{9,8},{10,11... | collective-permute-start | bytes 12296 | tf_op jit(solution)/shard_map/ppermute | solution.py:278
  12.9 1.6 %collective-permute-done = f32[1,1024]{1,0:T(1,128)S(1)} collective-permute-done((f32[1,1024]{1,0:T(1,128)S(1)}, f32[1,1024]{1,0:T(1,128)S(1)}, u32[]{:S(2)}, u32[]{:S(2)}) %collective-permute-start) | collective-permute-done | bytes 4128 | tf_op jit(solution)/shard_map/ppermute | solution.py:278
  14.5 1.3 %collective-permute-start.4 = (f32[1,1024]{1,0:T(1,128)S(1)}, f32[1,1024]{1,0:T(1,128)S(1)}, u32[]{:S(2)}, u32[]{:S(2)}) collective-permute-start(f32[1,1024]{1,0:T(1,128)S(1)} %add.3.counts_ref), channel_id=1, source_target_pairs={{2,0},{4,2},{6,4},{8,6},{10,8},{12,10},{14,12},{16,14},{18,16},{20... | collective-permute-start | bytes 12296 | tf_op jit(solution)/shard_map/ppermute | solution.py:281
  15.8 3.4 %collective-permute-done.4.counts_ref = f32[1,1024]{1,0:T(1,128)S(1)} collective-permute-done((f32[1,1024]{1,0:T(1,128)S(1)}, f32[1,1024]{1,0:T(1,128)S(1)}, u32[]{:S(2)}, u32[]{:S(2)}) %collective-permute-start.4) | collective-permute-done | bytes 4128 | tf_op jit(solution)/shard_map/ppermute | solution.py:281
  19.2 1.3 %collective-permute-start.10 = (bf16[2048,128]{1,0:T(8,128)(2,1)S(1)}, bf16[2048,128]{1,0:T(8,128)(2,1)S(1)}, u32[]{:S(2)}, u32[]{:S(2)}) collective-permute-start(bf16[2048,128]{1,0:T(8,128)(2,1)S(1)} %get-tuple-element.50), channel_id=1, source_target_pairs={{2,0},{4,2},{6,4},{8,6},{10,8},{12,10},{14,12},{16,14},{18,16},{20... | collective-permute-start | bytes 1572872 | tf_op jit(solution)/shard_map/ppermute | solution.py:272
  20.5 4.2 %shard_map.41 = (bf16[2048,1024]{1,0:T(8,128)(2,1)S(1)}, f32[2,512]{1,0:T(2,128)S(1)}, f32[8,128]{1,0:T(8,128)S(1)}, f32[512,512]{1,0:T(8,128)S(1)}, bf16[512,51...) custom-call(bf16[2048,1024]{1,0:T(8,128)(2,1)S(1)} %get-tuple-element.2, ...), custom_call_target="tpu_custom_call" | custom-call | tf_op jit(solution)/shard_map/pallas_call | solution.py:34
  24.7 0.0 collective-permute-done.2.raw_0
  24.7 1.8 %collective-permute-start.1 = (bf16[512,512]{1,0:T(8,128)(2,1)S(1)}, bf16[512,512]{1,0:T(8,128)(2,1)S(1)}, u32[]{:S(2)}, u32[]{:S(2)}) collective-permute-start(bf16[512,512]{1,0:T(8,128)(2,1)S(1)} %get-tuple-element.29), channel_id=1, source_target_pairs={{0,1},{1,0},{2,3},{3,2},{4,5},{5,4},{6,7},{7,6},{8,9},{9,8},{10,11... | collective-permute-start | bytes 1572872 | tf_op jit(solution)/shard_map/ppermute | solution.py:284
  26.5 0.0 collective-permute-done.3.raw_1
  26.5 2.7 %shard_map.42 = (f32[8,128]{1,0:T(8,128)S(1)}, f32[512,512]{1,0:T(8,128)S(1)}, bf16[512,512]{1,0:T(8,128)(2,1)S(1)}, bf16[2048,512]{1,0:T(8,128)(2,1)}) custom-call(bf16[2048,256]{1,0:T(8,128)(2,1)S(1)} %collective-permute-done.2.raw_0, bf16[2048,256]{1,0:T(8,128)(2,1)S(1)} %collective-permute-done.3.raw_1, f32[1,1024]{1,0:T(1,128)S(1)} %collective-permute-done.4.counts_ref, ...), custom_call_target="tpu_custom_call" | custom-call | tf_op jit(solution)/shard_map/pallas_call | solution.py:34
  29.2 0.3 collective-permute-start.5
  29.5 0.0 collective-permute-done.6.raw_ref
  29.5 0.8 shard_map.43
  30.3 1.8 %collective-permute-start.7 = (bf16[256,512]{1,0:T(8,128)(2,1)S(1)}, bf16[256,512]{1,0:T(8,128)(2,1)S(1)}, u32[]{:S(2)}, u32[]{:S(2)}) collective-permute-start(bf16[256,512]{1,0:T(8,128)(2,1)S(1)} %get-tuple-element.39), channel_id=1, source_target_pairs={{0,1},{1,0},{2,3},{3,2},{4,5},{5,4},{6,7},{7,6},{8,9},{9,8},{10,11... | collective-permute-start | bytes 786440 | tf_op jit(solution)/shard_map/ppermute | solution.py:284
  32.1 0.0 collective-permute-done.8.raw_ref
  32.1 0.0 copy-start
  32.1 0.4 shard_map.45
  32.5 2.2 %collective-permute-start.9 = (bf16[128,256]{1,0:T(8,128)(2,1)S(1)}, bf16[128,256]{1,0:T(8,128)(2,1)S(1)}, u32[]{:S(2)}, u32[]{:S(2)}) collective-permute-start(bf16[128,256]{1,0:T(8,128)(2,1)S(1)} %get-tuple-element.42), channel_id=1, source_target_pairs={{0,1},{2,3},{4,5},{6,7},{8,9},{10,11},{12,13},{14,15},{16,17},{18,... | collective-permute-start | bytes 196616 | tf_op jit(solution)/shard_map/ppermute | solution.py:284
  34.7 16.1 %collective-permute-done.10.raw_ref = bf16[2048,128]{1,0:T(8,128)(2,1)S(1)} collective-permute-done((bf16[2048,128]{1,0:T(8,128)(2,1)S(1)}, bf16[2048,128]{1,0:T(8,128)(2,1)S(1)}, u32[]{:S(2)}, u32[]{:S(2)}) %collective-permute-start.10) | collective-permute-done | bytes 524320 | tf_op jit(solution)/shard_map/ppermute | solution.py:272
  50.8 0.9 shard_map.46
  51.7 3.4 %collective-permute-start.11 = (bf16[128,128]{1,0:T(8,128)(2,1)S(1)}, bf16[128,128]{1,0:T(8,128)(2,1)S(1)}, u32[]{:S(2)}, u32[]{:S(2)}) collective-permute-start(bf16[128,128]{1,0:T(8,128)(2,1)S(1)} %get-tuple-element.45), channel_id=1, source_target_pairs={{0,1},{2,3},{4,5},{6,7},{8,9},{10,11},{12,13},{14,15},{16,17},{18,... | collective-permute-start | bytes 98312 | tf_op jit(solution)/shard_map/ppermute | solution.py:284
  55.1 0.0 collective-permute-done.1.refs_1_
  55.1 0.0 collective-permute-done.7.refs_6_
  55.1 0.0 collective-permute-done.5.refs_3_
  55.2 0.0 copy-done
  55.2 1.2 %shard_map.44.sums_ref = f32[1,512]{1,0:T(1,128)S(1)} custom-call(s32[1,512]{1,0:T(1,128)S(1)} %bitcast.8, f32[512,512]{1,0:T(8,128)S(1)} %get-tuple-element.28.refs_0_, bf16[512,512]{1,0:T(8,128)(2,1)S(1)} %collective-permute-done.1.refs_1_, f32[512,512]{1,0:T(8,128)S(1)} %get-tuple-element.33.refs_2_, bf16[512,512]{1,0:T(8,128)(2,1)S(1)} %collective-permute-done.5.refs_3_, ...), custom_call_target="tpu_custom_call" | custom-call | tf_op jit(solution)/shard_map/pallas_call | solution.py:34
  56.3 0.5 collective-permute-done.11.refs_3_
  56.9 0.0 collective-permute-done.9.refs_1_
  56.9 0.6 shard_map.47
  57.5 42.5 %all_to_all.5 = f32[32,1,128]{2,1,0:T(1,128)S(1)} all-to-all(f32[32,1,128]{2,1,0:T(1,128)S(1)} %bitcast.7), channel_id=1, replica_groups=mesh['genome'=16,'samples'=2] {'genome','samples'}, dimensions={0} | all-to-all | bytes 32768 | tf_op jit(solution)/shard_map/all_to_all | solution.py:388
  100.0 0.7 shard_map.48
  (1 shorter events, 0.0 us)
Async XLA Ops:
  1.9 22.8 %collective-permute-start.2 = (bf16[2048,256]{1,0:T(8,128)(2,1)S(1)}, bf16[2048,256]{1,0:T(8,128)(2,1)S(1)}, u32[]{:S(2)}, u32[]{:S(2)}) collective-permute-start(bf16[2048,256]{1,0:T(8,128)(2,1)S(1)} %slice.15), channel_id=1, source_target_pairs={{2,0},{4,2},{6,4},{8,6},{10,8},{12,10},{14,12},{16,14},{18,16},{20... | collective-permute-start | bytes 3145736 | tf_op jit(solution)/shard_map/ppermute | solution.py:272
  5.8 20.7 %collective-permute-start.3 = (bf16[2048,256]{1,0:T(8,128)(2,1)S(1)}, bf16[2048,256]{1,0:T(8,128)(2,1)S(1)}, u32[]{:S(2)}, u32[]{:S(2)}) collective-permute-start(bf16[2048,256]{1,0:T(8,128)(2,1)S(1)} %get-tuple-element.53), channel_id=1, source_target_pairs={{2,0},{4,2},{6,4},{8,6},{10,8},{12,10},{14,12},{16,14},{18,16},{20... | collective-permute-start | bytes 3145736 | tf_op jit(solution)/shard_map/ppermute | solution.py:272
  7.1 22.4 %collective-permute-start.6 = (bf16[2048,256]{1,0:T(8,128)(2,1)S(1)}, bf16[2048,256]{1,0:T(8,128)(2,1)S(1)}, u32[]{:S(2)}, u32[]{:S(2)}) collective-permute-start(bf16[2048,256]{1,0:T(8,128)(2,1)S(1)} %get-tuple-element.52), channel_id=1, source_target_pairs={{2,0},{4,2},{6,4},{8,6},{10,8},{12,10},{14,12},{16,14},{18,16},{20... | collective-permute-start | bytes 3145736 | tf_op jit(solution)/shard_map/ppermute | solution.py:272
  8.5 23.6 %collective-permute-start.8 = (bf16[2048,128]{1,0:T(8,128)(2,1)S(1)}, bf16[2048,128]{1,0:T(8,128)(2,1)S(1)}, u32[]{:S(2)}, u32[]{:S(2)}) collective-permute-start(bf16[2048,128]{1,0:T(8,128)(2,1)S(1)} %get-tuple-element.51), channel_id=1, source_target_pairs={{2,0},{4,2},{6,4},{8,6},{10,8},{12,10},{14,12},{16,14},{18,16},{20... | collective-permute-start | bytes 1572872 | tf_op jit(solution)/shard_map/ppermute | solution.py:272
  9.8 4.6 %collective-permute-start = (f32[1,1024]{1,0:T(1,128)S(1)}, f32[1,1024]{1,0:T(1,128)S(1)}, u32[]{:S(2)}, u32[]{:S(2)}) collective-permute-start(f32[1,1024]{1,0:T(1,128)S(1)} %get-tuple-element.27), channel_id=1, source_target_pairs={{0,1},{1,0},{2,3},{3,2},{4,5},{5,4},{6,7},{7,6},{8,9},{9,8},{10,11... | collective-permute-start | bytes 12296 | tf_op jit(solution)/shard_map/ppermute | solution.py:278
  14.5 4.7 %collective-permute-start.4 = (f32[1,1024]{1,0:T(1,128)S(1)}, f32[1,1024]{1,0:T(1,128)S(1)}, u32[]{:S(2)}, u32[]{:S(2)}) collective-permute-start(f32[1,1024]{1,0:T(1,128)S(1)} %add.3.counts_ref), channel_id=1, source_target_pairs={{2,0},{4,2},{6,4},{8,6},{10,8},{12,10},{14,12},{16,14},{18,16},{20... | collective-permute-start | bytes 12296 | tf_op jit(solution)/shard_map/ppermute | solution.py:281
  19.2 31.6 %collective-permute-start.10 = (bf16[2048,128]{1,0:T(8,128)(2,1)S(1)}, bf16[2048,128]{1,0:T(8,128)(2,1)S(1)}, u32[]{:S(2)}, u32[]{:S(2)}) collective-permute-start(bf16[2048,128]{1,0:T(8,128)(2,1)S(1)} %get-tuple-element.50), channel_id=1, source_target_pairs={{2,0},{4,2},{6,4},{8,6},{10,8},{12,10},{14,12},{16,14},{18,16},{20... | collective-permute-start | bytes 1572872 | tf_op jit(solution)/shard_map/ppermute | solution.py:272
  24.7 30.4 %collective-permute-start.1 = (bf16[512,512]{1,0:T(8,128)(2,1)S(1)}, bf16[512,512]{1,0:T(8,128)(2,1)S(1)}, u32[]{:S(2)}, u32[]{:S(2)}) collective-permute-start(bf16[512,512]{1,0:T(8,128)(2,1)S(1)} %get-tuple-element.29), channel_id=1, source_target_pairs={{0,1},{1,0},{2,3},{3,2},{4,5},{5,4},{6,7},{7,6},{8,9},{9,8},{10,11... | collective-permute-start | bytes 1572872 | tf_op jit(solution)/shard_map/ppermute | solution.py:284
  29.2 25.9 %collective-permute-start.5 = (bf16[512,512]{1,0:T(8,128)(2,1)S(1)}, bf16[512,512]{1,0:T(8,128)(2,1)S(1)}, u32[]{:S(2)}, u32[]{:S(2)}) collective-permute-start(bf16[512,512]{1,0:T(8,128)(2,1)S(1)} %get-tuple-element.34), channel_id=1, source_target_pairs={{0,1},{1,0},{2,3},{3,2},{4,5},{5,4},{6,7},{7,6},{8,9},{9,8},{10,11... | collective-permute-start | bytes 1572872 | tf_op jit(solution)/shard_map/ppermute | solution.py:284
  30.3 24.8 %collective-permute-start.7 = (bf16[256,512]{1,0:T(8,128)(2,1)S(1)}, bf16[256,512]{1,0:T(8,128)(2,1)S(1)}, u32[]{:S(2)}, u32[]{:S(2)}) collective-permute-start(bf16[256,512]{1,0:T(8,128)(2,1)S(1)} %get-tuple-element.39), channel_id=1, source_target_pairs={{0,1},{1,0},{2,3},{3,2},{4,5},{5,4},{6,7},{7,6},{8,9},{9,8},{10,11... | collective-permute-start | bytes 786440 | tf_op jit(solution)/shard_map/ppermute | solution.py:284
  32.1 23.0 %copy-start = (s32[512]{0:T(512)S(1)}, s32[512]{0:T(512)}, u32[]{:S(2)}) copy-start(s32[512]{0:T(512)} %param.3) | copy-start | bytes 6148
  32.5 24.4 %collective-permute-start.9 = (bf16[128,256]{1,0:T(8,128)(2,1)S(1)}, bf16[128,256]{1,0:T(8,128)(2,1)S(1)}, u32[]{:S(2)}, u32[]{:S(2)}) collective-permute-start(bf16[128,256]{1,0:T(8,128)(2,1)S(1)} %get-tuple-element.42), channel_id=1, source_target_pairs={{0,1},{2,3},{4,5},{6,7},{8,9},{10,11},{12,13},{14,15},{16,17},{18,... | collective-permute-start | bytes 196616 | tf_op jit(solution)/shard_map/ppermute | solution.py:284
  51.7 5.2 %collective-permute-start.11 = (bf16[128,128]{1,0:T(8,128)(2,1)S(1)}, bf16[128,128]{1,0:T(8,128)(2,1)S(1)}, u32[]{:S(2)}, u32[]{:S(2)}) collective-permute-start(bf16[128,128]{1,0:T(8,128)(2,1)S(1)} %get-tuple-element.45), channel_id=1, source_target_pairs={{0,1},{2,3},{4,5},{6,7},{8,9},{10,11},{12,13},{14,15},{16,17},{18,... | collective-permute-start | bytes 98312 | tf_op jit(solution)/shard_map/ppermute | solution.py:284

commit v5 on v3

--- a/solution.py
+++ b/solution.py
@@ -10,7 +10,7 @@
 
 
 LANES = 128
-EIGHTHS = (1, 2, 2, 2, 1)
+EIGHTHS = (3, 2, 2, 1)
 VMEM_LIMIT = 20 * 2**20
 variance_floor = 0.01
 
@@ -72,7 +72,7 @@
 def load(haplotypes):
     return pl.pallas_call(
         load_kernel,
-        in_specs=[pl.BlockSpec(memory_space=pl.ANY)],
+        in_specs=[pl.BlockSpec(memory_space=pltpu.HBM)],
         out_specs=[pl.BlockSpec(memory_space=pltpu.VMEM)] * 2,
         out_shape=[
             jax.ShapeDtypeStruct(haplotypes.shape, haplotypes.dtype),
@@ -81,7 +81,7 @@
         scratch_shapes=[pltpu.SemaphoreType.DMA((4,))],
         compiler_params=pltpu.CompilerParams(vmem_limit_bytes=VMEM_LIMIT),
         name="local_counts",
-    )(haplotypes)
+    )(pltpu.with_memory_space_constraint(haplotypes, pltpu.HBM))
 
 
 def standardize_part(raw_ref, counts_ref, first, haplo_total):
@@ -113,15 +113,13 @@
 
 
 def first_kernel(
-    share, haplo_total, raw_0, raw_1, counts_ref, std_ref, before_ref, token_ref, keep_ref, send_ref, later_ref
+    share, haplo_total, raw_ref, counts_ref, std_ref, before_ref, token_ref, keep_ref, send_ref
 ):
     token_ref[...] = before_ref[...]
-    unit = raw_0.shape[1]
-    later_ref[:, :unit] = standardize_part(raw_0, counts_ref, 0, haplo_total)
-    later_ref[:, unit:] = standardize_part(raw_1, counts_ref, unit, haplo_total)
-    mine = lax.axis_index("samples")
-    send_ref[...] = product(later_ref[...], std_ref[:, columns(1 - mine, share)]).astype(jnp.bfloat16)
-    keep_ref[...] = product(later_ref[...], std_ref[:, columns(mine, share)])
+    later = standardize_part(raw_ref, counts_ref, 0, haplo_total)
+    mine = lax.axis_index("samples")
+    send_ref[...] = product(later, std_ref[:, columns(1 - mine, share)]).astype(jnp.bfloat16)
+    keep_ref[...] = product(later, std_ref[:, columns(mine, share)])
 
 
 def middle_kernel(
@@ -312,20 +310,19 @@
             counts,
         )
         got_0 = swap(send)
-        token, keep_1, send, _ = call(
+        token, keep_1, send = call(
             functools.partial(first_kernel, share, haplo_total),
-            [token_type, ((3 * u, share), f32), ((3 * u, share), bf16), ((depth, 3 * u), bf16)],
+            [token_type, ((3 * u, share), f32), ((3 * u, share), bf16)],
             raws[0],
-            raws[1],
             next_counts,
             standard,
             token,
         )
         got_1 = swap(send)
         token, keep_2, send, corner, corner_send = call(
-            functools.partial(middle_kernel, firsts[2], share, haplo_total),
+            functools.partial(middle_kernel, firsts[1], share, haplo_total),
             [token_type, ((2 * u, share), f32), ((2 * u, share), bf16), ((u, u), f32), ((u, u), bf16)],
-            raws[2],
+            raws[1],
             next_counts,
             standard,
             low_send_1,
@@ -333,9 +330,9 @@
         )
         got_2 = swap(send)
         token, keep_3, send = call(
-            functools.partial(upper_kernel, firsts[3], haplo_total),
+            functools.partial(upper_kernel, firsts[2], haplo_total),
             [token_type, ((2 * u, 3 * u), f32), ((2 * u, 3 * u), bf16)],
-            raws[3],
+            raws[2],
             next_counts,
             standard,
             low_send_2,
@@ -347,7 +344,7 @@
             (None, 0, (whole, whole), 1, (whole, whole), share, 0),
             (None, 2, (whole, whole), 3, (whole, whole), width, 0),
             (0, 4, (slice(half, None), whole), 6, (whole, whole), half, 0),
-            (1, 5, (whole, whole), 6, (whole, whole), width + firsts[2], share),
+            (1, 5, (whole, whole), 6, (whole, whole), width + firsts[1], share),
         ]
         (sums,) = call(
             functools.partial(early_kernel, share, haplo_total, pieces),
@@ -362,9 +359,9 @@
             got_2,
         )
         keep_4, send = call(
-            functools.partial(last_kernel, firsts[4], haplo_total),
+            functools.partial(last_kernel, firsts[3], haplo_total),
             [((u, u), f32), ((u, u), bf16)],
-            raws[4],
+            raws[3],
             next_counts,
             standard,
         )
@@ -372,9 +369,9 @@
         tails = [low, corner, keep_3, got_3, keep_4, got_4]
         tail_pieces = [
             (0, 0, (slice(0, half), slice(0, half)), 3, (whole, slice(0, half)), 0, 0),
-            (0, 1, (whole, whole), 3, (slice(0, u), slice(half, None)), width + firsts[2], firsts[2]),
-            (1, 2, (whole, whole), 3, (whole, whole), width + firsts[3], firsts[3]),
-            (1, 4, (whole, whole), 5, (whole, whole), width + firsts[4], firsts[4]),
+            (0, 1, (whole, whole), 3, (slice(0, u), slice(half, None)), width + firsts[1], firsts[1]),
+            (1, 2, (whole, whole), 3, (whole, whole), width + firsts[2], firsts[2]),
+            (1, 4, (whole, whole), 5, (whole, whole), width + firsts[3], firsts[3]),
         ]
     else:
         frequency, inverse_sd = moments(counts, haplo_total)

time: 103 us -> 100 us (0.971)
  waiting for transfers between devices: 25.6 us -> 6.12 us
  blocking collectives: 42.9 us -> 59.5 us
  Pallas kernels: 12.7 us -> 13.8 us
    ppermute x5 -> x4, waiting for transfers between devices: 20.1 us -> 0.01 us  [shifted(): lax.ppermute(array[:, firsts[c]:firsts[c] + sizes[c]], 'genome', back)]
    all_to_all x1, blocking collectives: 42.9 us -> 59.5 us  [per_device(): lax.all_to_all(last[:, None], ('genome', 'samples'), 0, 0, tiled=True)[:, 0]]
    ppermute x5, waiting for transfers between devices: 0.67 us -> 4.52 us  [swap(): return lax.ppermute(send, 'samples', pairs)]
    ppermute x1, waiting for transfers between devices: 3.26 us -> 0.01 us  [per_device(): next_counts = lax.ppermute(counts, 'genome', back)]
    unnamed x4 -> x2, local copies, waits for them, and re-layouts: 2.18 us -> 0.01 us
    slice x3, local copies, waits for them, and re-layouts: 0.48 us -> 1.84 us  [shifted(): array[:, firsts[c]:firsts[c] + sizes[c]]]
    ppermute x5 -> x4, starting transfers between devices: 6.45 us -> 5.17 us  [shifted(): lax.ppermute(array[:, firsts[c]:firsts[c] + sizes[c]], 'genome', back)]
    pallas_call x1, Pallas kernels: 1.15 us -> 2.42 us  [load(): pl.pallas_call(load_kernel, in_specs=[pl.BlockSpec(memory_space=pltpu.HBM...]
  transfers between devices with their start and end apart: 12 -> 11, of which waited for: 4 -> 4; matrix products, arithmetic and copies ran while one was open for 0% -> 0% of each run, Pallas kernels for 10% -> 12%
where the time goes in v5:
time: 100 us; the launch traced here: 99.7 us
  blocking collectives  59.5 us (60%)
  starting transfers between devices  17.7 us (18%)
  Pallas kernels  13.8 us (14%)
  waiting for transfers between devices  6.12 us (6%)
  local copies, waits for them, and re-layouts  1.85 us (2%)
    all_to_all x1, blocking collectives, per_device(): lax.all_to_all(last[:, None], ('genome', 'samples'), 0, 0, tiled=True)[:, 0]  59.5 us
    pallas_call x8, Pallas kernels, call(): pl.pallas_call(kernel, in_specs=[pl.BlockSpec(memory_space=pltpu.VMEM)] *...  11.3 us
    ppermute x5, starting transfers between devices, swap(): return lax.ppermute(send, 'samples', pairs)  8.17 us
    ppermute x4, starting transfers between devices, shifted(): lax.ppermute(array[:, firsts[c]:firsts[c] + sizes[c]], 'genome', back)  5.17 us
    ppermute x5, waiting for transfers between devices, swap(): return lax.ppermute(send, 'samples', pairs)  4.52 us
    ppermute x1, starting transfers between devices, per_device(): counts = counts + lax.ppermute(counts, 'samples', [(0, 1), (1, 0)])  3.06 us
    pallas_call x1, Pallas kernels, load(): pl.pallas_call(load_kernel, in_specs=[pl.BlockSpec(memory_space=pltpu.HBM...  2.42 us
  transfers between devices with their start and end apart: 11, of which 4 were waited for; matrix products, arithmetic and copies ran while one was open for 0% of the time, Pallas kernels for 12%

profile of v5, /device:TPU:0, one launch (start us, length us, event | category | flops | bytes accessed | tf_op | source)
XLA Modules:
  0.0 99.7 jit_solution(8105471529429444876)
XLA Ops:
  0.6 1.6 %slice.12 = bf16[2048,384]{1,0:T(8,128)(2,1)S(1)} slice(bf16[2048,1024]{1,0:T(8,128)(2,1)} %hap_hbm.1), slice={[0:2048], [0:384]} | slice | bytes 3145728 | tf_op jit(solution)/shard_map/slice | solution.py:286
  2.2 1.3 %collective-permute-start.2 = (bf16[2048,384]{1,0:T(8,128)(2,1)S(1)}, bf16[2048,384]{1,0:T(8,128)(2,1)S(1)}, u32[]{:S(2)}, u32[]{:S(2)}) collective-permute-start(bf16[2048,384]{1,0:T(8,128)(2,1)S(1)} %slice.12), channel_id=1, source_target_pairs={{2,0},{4,2},{6,4},{8,6},{10,8},{12,10},{14,12},{16,14},{18,16},{20... | collective-permute-start | bytes 4718600 | tf_op jit(solution)/shard_map/ppermute | solution.py:286
  3.5 2.4 %local_counts.1 = (bf16[2048,1024]{1,0:T(8,128)(2,1)S(1)}, f32[1,1024]{1,0:T(1,128)S(1)}) custom-call(bf16[2048,1024]{1,0:T(8,128)(2,1)} %hap_hbm.1), custom_call_target="tpu_custom_call" | custom-call | tf_op jit(solution)/shard_map/local_counts/pallas_call | solution.py:73
  5.9 0.1 fusion
  6.1 1.3 %collective-permute-start.5 = (bf16[2048,256]{1,0:T(8,128)(2,1)S(1)}, bf16[2048,256]{1,0:T(8,128)(2,1)S(1)}, u32[]{:S(2)}, u32[]{:S(2)}) collective-permute-start(bf16[2048,256]{1,0:T(8,128)(2,1)S(1)} %get-tuple-element.53), channel_id=1, source_target_pairs={{2,0},{4,2},{6,4},{8,6},{10,8},{12,10},{14,12},{16,14},{18,16},{20... | collective-permute-start | bytes 3145736 | tf_op jit(solution)/shard_map/ppermute | solution.py:286
  7.4 1.3 %collective-permute-start.7 = (bf16[2048,256]{1,0:T(8,128)(2,1)S(1)}, bf16[2048,256]{1,0:T(8,128)(2,1)S(1)}, u32[]{:S(2)}, u32[]{:S(2)}) collective-permute-start(bf16[2048,256]{1,0:T(8,128)(2,1)S(1)} %get-tuple-element.52), channel_id=1, source_target_pairs={{2,0},{4,2},{6,4},{8,6},{10,8},{12,10},{14,12},{16,14},{18,16},{20... | collective-permute-start | bytes 3145736 | tf_op jit(solution)/shard_map/ppermute | solution.py:286
  8.7 0.1 slice.15
  8.8 1.3 %collective-permute-start.9 = (bf16[2048,128]{1,0:T(8,128)(2,1)S(1)}, bf16[2048,128]{1,0:T(8,128)(2,1)S(1)}, u32[]{:S(2)}, u32[]{:S(2)}) collective-permute-start(bf16[2048,128]{1,0:T(8,128)(2,1)S(1)} %slice.15), channel_id=1, source_target_pairs={{2,0},{4,2},{6,4},{8,6},{10,8},{12,10},{14,12},{16,14},{18,16},{20... | collective-permute-start | bytes 1572872 | tf_op jit(solution)/shard_map/ppermute | solution.py:286
  10.1 3.1 %collective-permute-start = (f32[1,1024]{1,0:T(1,128)S(1)}, f32[1,1024]{1,0:T(1,128)S(1)}, u32[]{:S(2)}, u32[]{:S(2)}) collective-permute-start(f32[1,1024]{1,0:T(1,128)S(1)} %get-tuple-element.28), channel_id=1, source_target_pairs={{0,1},{1,0},{2,3},{3,2},{4,5},{5,4},{6,7},{7,6},{8,9},{9,8},{10,11... | collective-permute-start | bytes 12296 | tf_op jit(solution)/shard_map/ppermute | solution.py:292
  13.2 1.6 %collective-permute-done = f32[1,1024]{1,0:T(1,128)S(1)} collective-permute-done((f32[1,1024]{1,0:T(1,128)S(1)}, f32[1,1024]{1,0:T(1,128)S(1)}, u32[]{:S(2)}, u32[]{:S(2)}) %collective-permute-start) | collective-permute-done | bytes 4128 | tf_op jit(solution)/shard_map/ppermute | solution.py:292
  14.8 1.3 %collective-permute-start.3 = (f32[1,1024]{1,0:T(1,128)S(1)}, f32[1,1024]{1,0:T(1,128)S(1)}, u32[]{:S(2)}, u32[]{:S(2)}) collective-permute-start(f32[1,1024]{1,0:T(1,128)S(1)} %add.3.counts_ref), channel_id=1, source_target_pairs={{2,0},{4,2},{6,4},{8,6},{10,8},{12,10},{14,12},{16,14},{18,16},{20... | collective-permute-start | bytes 12296 | tf_op jit(solution)/shard_map/ppermute | solution.py:295
  16.1 4.2 %shard_map.41 = (bf16[2048,1024]{1,0:T(8,128)(2,1)S(1)}, f32[2,512]{1,0:T(2,128)S(1)}, f32[8,128]{1,0:T(8,128)S(1)}, f32[512,512]{1,0:T(8,128)S(1)}, bf16[512,51...) custom-call(bf16[2048,1024]{1,0:T(8,128)(2,1)S(1)} %get-tuple-element.2, ...), custom_call_target="tpu_custom_call" | custom-call | tf_op jit(solution)/shard_map/pallas_call | solution.py:34
  20.3 0.0 collective-permute-done.3.counts_ref
  20.3 2.1 %collective-permute-start.1 = (bf16[512,512]{1,0:T(8,128)(2,1)S(1)}, bf16[512,512]{1,0:T(8,128)(2,1)S(1)}, u32[]{:S(2)}, u32[]{:S(2)}) collective-permute-start(bf16[512,512]{1,0:T(8,128)(2,1)S(1)} %get-tuple-element.30), channel_id=1, source_target_pairs={{0,1},{1,0},{2,3},{3,2},{4,5},{5,4},{6,7},{7,6},{8,9},{9,8},{10,11... | collective-permute-start | bytes 1572872 | tf_op jit(solution)/shard_map/ppermute | solution.py:298
  22.4 0.0 collective-permute-done.2.raw_ref
  22.4 1.8 %shard_map.42 = (f32[8,128]{1,0:T(8,128)S(1)}, f32[384,512]{1,0:T(8,128)S(1)}, bf16[384,512]{1,0:T(8,128)(2,1)S(1)}) custom-call(bf16[2048,384]{1,0:T(8,128)(2,1)S(1)} %collective-permute-done.2.raw_ref, f32[1,1024]{1,0:T(1,128)S(1)} %collective-permute-done.3.counts_ref, bf16[2048,1024]{1,0:T(8,128)(2,1)S(1)} %get-tuple-element.31.std_ref, ...), custom_call_target="tpu_custom_call" | custom-call | tf_op jit(solution)/shard_map/pallas_call | solution.py:34
  24.2 0.1 collective-permute-start.4
  24.3 0.0 collective-permute-done.5.raw_ref
  24.3 1.0 shard_map.43
  25.3 2.1 %collective-permute-start.6 = (bf16[256,512]{1,0:T(8,128)(2,1)S(1)}, bf16[256,512]{1,0:T(8,128)(2,1)S(1)}, u32[]{:S(2)}, u32[]{:S(2)}) collective-permute-start(bf16[256,512]{1,0:T(8,128)(2,1)S(1)} %get-tuple-element.39), channel_id=1, source_target_pairs={{0,1},{1,0},{2,3},{3,2},{4,5},{5,4},{6,7},{7,6},{8,9},{9,8},{10,11... | collective-permute-start | bytes 786440 | tf_op jit(solution)/shard_map/ppermute | solution.py:298
  27.4 0.0 collective-permute-done.7.raw_ref
  27.4 0.0 copy-start
  27.4 1.4 %shard_map.45 = (f32[8,128]{1,0:T(8,128)}, f32[256,384]{1,0:T(8,128)S(1)}, bf16[256,384]{1,0:T(8,128)(2,1)S(1)}) custom-call(bf16[2048,256]{1,0:T(8,128)(2,1)S(1)} %collective-permute-done.7.raw_ref, f32[1,1024]{1,0:T(1,128)S(1)} %collective-permute-done.3.counts_ref, bf16[2048,1024]{1,0:T(8,128)(2,1)S(1)} %get-tuple-element.31.std_ref, ...), custom_call_target="tpu_custom_call" | custom-call | tf_op jit(solution)/shard_map/pallas_call | solution.py:34
  28.8 0.0 collective-permute-start.8
  28.8 0.0 collective-permute-done.9.raw_ref
  28.8 0.4 shard_map.46
  29.1 3.9 %collective-permute-start.10 = (bf16[128,128]{1,0:T(8,128)(2,1)S(1)}, bf16[128,128]{1,0:T(8,128)(2,1)S(1)}, u32[]{:S(2)}, u32[]{:S(2)}) collective-permute-start(bf16[128,128]{1,0:T(8,128)(2,1)S(1)} %get-tuple-element.47), channel_id=1, source_target_pairs={{0,1},{2,3},{4,5},{6,7},{8,9},{10,11},{12,13},{14,15},{16,17},{18,... | collective-permute-start | bytes 98312 | tf_op jit(solution)/shard_map/ppermute | solution.py:298
  33.1 0.0 collective-permute-done.1.refs_1_
  33.1 3.5 %collective-permute-done.6.refs_6_ = bf16[256,512]{1,0:T(8,128)(2,1)S(1)} collective-permute-done((bf16[256,512]{1,0:T(8,128)(2,1)S(1)}, bf16[256,512]{1,0:T(8,128)(2,1)S(1)}, u32[]{:S(2)}, u32[]{:S(2)}) %collective-permute-start.6) | collective-permute-done | bytes 262176 | tf_op jit(solution)/shard_map/ppermute | solution.py:298
  36.6 0.0 collective-permute-done.4.refs_3_
  36.6 0.0 copy-done
  36.6 1.1 %shard_map.44.sums_ref = f32[1,512]{1,0:T(1,128)S(1)} custom-call(s32[1,512]{1,0:T(1,128)S(1)} %bitcast.8, f32[512,512]{1,0:T(8,128)S(1)} %get-tuple-element.29.refs_0_, bf16[512,512]{1,0:T(8,128)(2,1)S(1)} %collective-permute-done.1.refs_1_, f32[384,512]{1,0:T(8,128)S(1)} %get-tuple-element.33.refs_2_, bf16[384,512]{1,0:T(8,128)(2,1)S(1)} %collective-permute-done.4.refs_3_, ...), custom_call_target="tpu_custom_call" | custom-call | tf_op jit(solution)/shard_map/pallas_call | solution.py:34
  37.6 0.9 collective-permute-done.10.refs_5_
  38.6 0.1 collective-permute-done.8.refs_3_
  38.7 0.8 shard_map.47
  39.5 59.5 %all_to_all.5 = f32[32,1,128]{2,1,0:T(1,128)S(1)} all-to-all(f32[32,1,128]{2,1,0:T(1,128)S(1)} %bitcast.7), channel_id=1, replica_groups=mesh['genome'=16,'samples'=2] {'genome','samples'}, dimensions={0} | all-to-all | bytes 32768 | tf_op jit(solution)/shard_map/all_to_all | solution.py:406
  99.0 0.7 shard_map.48
  (1 shorter events, 0.0 us)
Async XLA Ops:
  2.2 20.2 %collective-permute-start.2 = (bf16[2048,384]{1,0:T(8,128)(2,1)S(1)}, bf16[2048,384]{1,0:T(8,128)(2,1)S(1)}, u32[]{:S(2)}, u32[]{:S(2)}) collective-permute-start(bf16[2048,384]{1,0:T(8,128)(2,1)S(1)} %slice.12), channel_id=1, source_target_pairs={{2,0},{4,2},{6,4},{8,6},{10,8},{12,10},{14,12},{16,14},{18,16},{20... | collective-permute-start | bytes 4718600 | tf_op jit(solution)/shard_map/ppermute | solution.py:286
  6.1 18.2 %collective-permute-start.5 = (bf16[2048,256]{1,0:T(8,128)(2,1)S(1)}, bf16[2048,256]{1,0:T(8,128)(2,1)S(1)}, u32[]{:S(2)}, u32[]{:S(2)}) collective-permute-start(bf16[2048,256]{1,0:T(8,128)(2,1)S(1)} %get-tuple-element.53), channel_id=1, source_target_pairs={{2,0},{4,2},{6,4},{8,6},{10,8},{12,10},{14,12},{16,14},{18,16},{20... | collective-permute-start | bytes 3145736 | tf_op jit(solution)/shard_map/ppermute | solution.py:286
  7.4 20.0 %collective-permute-start.7 = (bf16[2048,256]{1,0:T(8,128)(2,1)S(1)}, bf16[2048,256]{1,0:T(8,128)(2,1)S(1)}, u32[]{:S(2)}, u32[]{:S(2)}) collective-permute-start(bf16[2048,256]{1,0:T(8,128)(2,1)S(1)} %get-tuple-element.52), channel_id=1, source_target_pairs={{2,0},{4,2},{6,4},{8,6},{10,8},{12,10},{14,12},{16,14},{18,16},{20... | collective-permute-start | bytes 3145736 | tf_op jit(solution)/shard_map/ppermute | solution.py:286
  8.8 20.0 %collective-permute-start.9 = (bf16[2048,128]{1,0:T(8,128)(2,1)S(1)}, bf16[2048,128]{1,0:T(8,128)(2,1)S(1)}, u32[]{:S(2)}, u32[]{:S(2)}) collective-permute-start(bf16[2048,128]{1,0:T(8,128)(2,1)S(1)} %slice.15), channel_id=1, source_target_pairs={{2,0},{4,2},{6,4},{8,6},{10,8},{12,10},{14,12},{16,14},{18,16},{20... | collective-permute-start | bytes 1572872 | tf_op jit(solution)/shard_map/ppermute | solution.py:286
  10.1 4.6 %collective-permute-start = (f32[1,1024]{1,0:T(1,128)S(1)}, f32[1,1024]{1,0:T(1,128)S(1)}, u32[]{:S(2)}, u32[]{:S(2)}) collective-permute-start(f32[1,1024]{1,0:T(1,128)S(1)} %get-tuple-element.28), channel_id=1, source_target_pairs={{0,1},{1,0},{2,3},{3,2},{4,5},{5,4},{6,7},{7,6},{8,9},{9,8},{10,11... | collective-permute-start | bytes 12296 | tf_op jit(solution)/shard_map/ppermute | solution.py:292
  14.8 5.5 %collective-permute-start.3 = (f32[1,1024]{1,0:T(1,128)S(1)}, f32[1,1024]{1,0:T(1,128)S(1)}, u32[]{:S(2)}, u32[]{:S(2)}) collective-permute-start(f32[1,1024]{1,0:T(1,128)S(1)} %add.3.counts_ref), channel_id=1, source_target_pairs={{2,0},{4,2},{6,4},{8,6},{10,8},{12,10},{14,12},{16,14},{18,16},{20... | collective-permute-start | bytes 12296 | tf_op jit(solution)/shard_map/ppermute | solution.py:295
  20.3 12.8 %collective-permute-start.1 = (bf16[512,512]{1,0:T(8,128)(2,1)S(1)}, bf16[512,512]{1,0:T(8,128)(2,1)S(1)}, u32[]{:S(2)}, u32[]{:S(2)}) collective-permute-start(bf16[512,512]{1,0:T(8,128)(2,1)S(1)} %get-tuple-element.30), channel_id=1, source_target_pairs={{0,1},{1,0},{2,3},{3,2},{4,5},{5,4},{6,7},{7,6},{8,9},{9,8},{10,11... | collective-permute-start | bytes 1572872 | tf_op jit(solution)/shard_map/ppermute | solution.py:298
  24.2 12.3 %collective-permute-start.4 = (bf16[384,512]{1,0:T(8,128)(2,1)S(1)}, bf16[384,512]{1,0:T(8,128)(2,1)S(1)}, u32[]{:S(2)}, u32[]{:S(2)}) collective-permute-start(bf16[384,512]{1,0:T(8,128)(2,1)S(1)} %get-tuple-element.34), channel_id=1, source_target_pairs={{0,1},{1,0},{2,3},{3,2},{4,5},{5,4},{6,7},{7,6},{8,9},{9,8},{10,11... | collective-permute-start | bytes 1179656 | tf_op jit(solution)/shard_map/ppermute | solution.py:298
  25.3 11.3 %collective-permute-start.6 = (bf16[256,512]{1,0:T(8,128)(2,1)S(1)}, bf16[256,512]{1,0:T(8,128)(2,1)S(1)}, u32[]{:S(2)}, u32[]{:S(2)}) collective-permute-start(bf16[256,512]{1,0:T(8,128)(2,1)S(1)} %get-tuple-element.39), channel_id=1, source_target_pairs={{0,1},{1,0},{2,3},{3,2},{4,5},{5,4},{6,7},{7,6},{8,9},{9,8},{10,11... | collective-permute-start | bytes 786440 | tf_op jit(solution)/shard_map/ppermute | solution.py:298
  27.4 9.2 %copy-start = (s32[512]{0:T(512)S(1)}, s32[512]{0:T(512)}, u32[]{:S(2)}) copy-start(s32[512]{0:T(512)} %param.3) | copy-start | bytes 6148
  28.8 9.9 %collective-permute-start.8 = (bf16[256,384]{1,0:T(8,128)(2,1)S(1)}, bf16[256,384]{1,0:T(8,128)(2,1)S(1)}, u32[]{:S(2)}, u32[]{:S(2)}) collective-permute-start(bf16[256,384]{1,0:T(8,128)(2,1)S(1)} %get-tuple-element.45), channel_id=1, source_target_pairs={{0,1},{1,0},{2,3},{3,2},{4,5},{5,4},{6,7},{7,6},{8,9},{9,8},{10,11... | collective-permute-start | bytes 589832 | tf_op jit(solution)/shard_map/ppermute | solution.py:298
  29.1 9.4 %collective-permute-start.10 = (bf16[128,128]{1,0:T(8,128)(2,1)S(1)}, bf16[128,128]{1,0:T(8,128)(2,1)S(1)}, u32[]{:S(2)}, u32[]{:S(2)}) collective-permute-start(bf16[128,128]{1,0:T(8,128)(2,1)S(1)} %get-tuple-element.47), channel_id=1, source_target_pairs={{0,1},{2,3},{4,5},{6,7},{8,9},{10,11},{12,13},{14,15},{16,17},{18,... | collective-permute-start | bytes 98312 | tf_op jit(solution)/shard_map/ppermute | solution.py:298

commit v6 on v5

--- a/solution.py
+++ b/solution.py
@@ -10,7 +10,7 @@
 
 
 LANES = 128
-EIGHTHS = (3, 2, 2, 1)
+EIGHTHS = (3, 2, 1, 1, 1)
 VMEM_LIMIT = 20 * 2**20
 variance_floor = 0.01
 
@@ -144,10 +144,8 @@
         send_ref[...] = low_send_1[...]
 
 
-def upper_kernel(
-    first, haplo_total, raw_ref, counts_ref, std_ref, low_send_2, corner_send, before_ref,
-    token_ref, keep_ref, send_ref,
-):
+def upper_kernel(first, haplo_total, fills, raw_ref, counts_ref, std_ref, before_ref, *refs):
+    token_ref, keep_ref, send_ref = refs[len(fills) :]
     token_ref[...] = before_ref[...]
     later = standardize_part(raw_ref, counts_ref, first, haplo_total)
     keep = product(later, std_ref[:, first:])
@@ -160,10 +158,8 @@
 
     @pl.when(mine == 1)
     def _():
-        half, corner = low_send_2.shape[1], corner_send.shape[0]
-        send_ref[:, :half] = low_send_2[...]
-        send_ref[:corner, half:] = corner_send[...]
-        send_ref[corner:, half:] = jnp.zeros_like(send_ref[corner:, half:])
+        for ref, rows, at in zip(refs, *zip(*fills)):
+            send_ref[:, at] = ref[rows, :]
 
 
 def last_kernel(first, haplo_total, raw_ref, counts_ref, std_ref, keep_ref, send_ref):
@@ -236,19 +232,23 @@
     lasts = []
     for k, rate in enumerate(rates):
         weight = jnp.where(lag >= 0.0, jnp.exp(jnp.maximum(lag, 0.0) * rate), 0.0)
-        inner = lax.dot_general(
-            stacked,
-            weight,
-            (((1,), (0,)), ((), ())),
-            precision=lax.Precision.HIGHEST,
-            preferred_element_type=jnp.float32,
+        to_end = jnp.exp((LANES - 1.0 - source.astype(jnp.float32)) * rate)
+        inner, ending = (
+            lax.dot_general(
+                stacked,
+                w,
+                (((1,), (0,)), ((), ())),
+                precision=lax.Precision.HIGHEST,
+                preferred_element_type=jnp.float32,
+            )
+            for w in (weight, to_end)
         )
         fall = jnp.exp((lane + 1.0) * rate)
-        carry = jnp.zeros((1, 1), jnp.float32)
+        block_fall = math.exp(LANES * rate)
+        carry = jnp.zeros((1, LANES), jnp.float32)
         for b in range(blocks):
-            here = inner[b : b + 1, :] + carry * fall
-            local_ref[k : k + 1, b * LANES : (b + 1) * LANES] = here
-            carry = here[:, LANES - 1 :]
+            local_ref[k : k + 1, b * LANES : (b + 1) * LANES] = inner[b : b + 1, :] + carry * fall
+            carry = ending[b : b + 1, :] + carry * block_fall
         lasts.append(carry)
     tile_lane = lax.broadcasted_iota(jnp.int32, last_ref.shape, 1)
     last_ref[...] = jnp.where(tile_lane == 0, lasts[0], jnp.where(tile_lane == 1, lasts[1], 0.0))
@@ -329,17 +329,24 @@
             token,
         )
         got_2 = swap(send)
-        token, keep_3, send = call(
-            functools.partial(upper_kernel, firsts[2], haplo_total),
-            [token_type, ((2 * u, 3 * u), f32), ((2 * u, 3 * u), bf16)],
-            raws[2],
-            next_counts,
-            standard,
-            low_send_2,
-            corner_send,
-            token,
-        )
-        got_3 = swap(send)
+        first_unit, second_unit = slice(0, u), slice(u, None)
+        lower, upper = slice(0, half), slice(half, None)
+        tails = [low, corner]
+        for c, fills, extra in (
+            (2, [(first_unit, lower), (whole, upper)], [low_send_2, corner_send]),
+            (3, [(second_unit, lower)], [low_send_2]),
+        ):
+            shape = (u, width - firsts[c])
+            token, keep, send = call(
+                functools.partial(upper_kernel, firsts[c], haplo_total, fills),
+                [token_type, (shape, f32), (shape, bf16)],
+                raws[c],
+                next_counts,
+                standard,
+                token,
+                *extra,
+            )
+            tails += [keep, swap(send)]
         pieces = [
             (None, 0, (whole, whole), 1, (whole, whole), share, 0),
             (None, 2, (whole, whole), 3, (whole, whole), width, 0),
@@ -358,20 +365,21 @@
             keep_2,
             got_2,
         )
-        keep_4, send = call(
-            functools.partial(last_kernel, firsts[3], haplo_total),
+        keep, send = call(
+            functools.partial(last_kernel, firsts[4], haplo_total),
             [((u, u), f32), ((u, u), bf16)],
-            raws[3],
+            raws[4],
             next_counts,
             standard,
         )
-        got_4 = swap(send, [(0, 1)])
-        tails = [low, corner, keep_3, got_3, keep_4, got_4]
+        tails += [keep, swap(send, [(0, 1)])]
         tail_pieces = [
-            (0, 0, (slice(0, half), slice(0, half)), 3, (whole, slice(0, half)), 0, 0),
-            (0, 1, (whole, whole), 3, (slice(0, u), slice(half, None)), width + firsts[1], firsts[1]),
-            (1, 2, (whole, whole), 3, (whole, whole), width + firsts[2], firsts[2]),
-            (1, 4, (whole, whole), 5, (whole, whole), width + firsts[3], firsts[3]),
+            (0, 0, (first_unit, lower), 3, (whole, lower), 0, 0),
+            (0, 0, (slice(u, half), lower), 5, (whole, lower), u, 0),
+            (0, 1, (whole, whole), 3, (whole, upper), width + firsts[1], firsts[1]),
+        ] + [
+            (1, 2 * c - 2, (whole, whole), 2 * c - 1, (whole, whole), width + firsts[c], firsts[c])
+            for c in (2, 3, 4)
         ]
     else:
         frequency, inverse_sd = moments(counts, haplo_total)

time: 100 us -> 101 us (1.010)
  blocking collectives: 59.5 us -> 41.7 us
  waiting for transfers between devices: 6.12 us -> 23 us
  starting transfers between devices: 17.7 us -> 19 us
    all_to_all x1, blocking collectives: 59.5 us -> 41.7 us  [per_device(): lax.all_to_all(last[:, None], ('genome', 'samples'), 0, 0, tiled=True)[:, 0]]
    ppermute x4 -> x5, waiting for transfers between devices: 0.01 us -> 17.3 us  [shifted(): lax.ppermute(array[:, firsts[c]:firsts[c] + sizes[c]], 'genome', back)]
    ppermute x5 -> x6, waiting for transfers between devices: 4.52 us -> 0.66 us  [swap(): return lax.ppermute(send, 'samples', pairs)]
    ppermute x1, waiting for transfers between devices: 0.01 us -> 3.4 us  [per_device(): next_counts = lax.ppermute(counts, 'genome', back)]
    ppermute x4 -> x5, starting transfers between devices: 5.17 us -> 6.45 us  [shifted(): lax.ppermute(array[:, firsts[c]:firsts[c] + sizes[c]], 'genome', back)]
    ppermute x5 -> x6, starting transfers between devices: 8.17 us -> 8.25 us  [swap(): return lax.ppermute(send, 'samples', pairs)]
    pallas_call x8 -> x9, Pallas kernels: 11.3 us -> 11.4 us  [call(): pl.pallas_call(kernel, in_specs=[pl.BlockSpec(memory_space=pltpu.VMEM)] *...]
  transfers between devices with their start and end apart: 11 -> 13, of which waited for: 4 -> 4; matrix products, arithmetic and copies ran while one was open for 0% -> 0% of each run, Pallas kernels for 12% -> 12%
where the time goes in v6:
time: 101 us; the launch traced here: 100 us
  blocking collectives  41.7 us (41%)
  waiting for transfers between devices  23 us (23%)
  starting transfers between devices  19 us (19%)
  Pallas kernels  13.8 us (14%)
  local copies, waits for them, and re-layouts  1.98 us (2%)
    all_to_all x1, blocking collectives, per_device(): lax.all_to_all(last[:, None], ('genome', 'samples'), 0, 0, tiled=True)[:, 0]  41.7 us
    ppermute x5, waiting for transfers between devices, shifted(): lax.ppermute(array[:, firsts[c]:firsts[c] + sizes[c]], 'genome', back)  17.3 us
    pallas_call x9, Pallas kernels, call(): pl.pallas_call(kernel, in_specs=[pl.BlockSpec(memory_space=pltpu.VMEM)] *...  11.4 us
    ppermute x6, starting transfers between devices, swap(): return lax.ppermute(send, 'samples', pairs)  8.25 us
    ppermute x5, starting transfers between devices, shifted(): lax.ppermute(array[:, firsts[c]:firsts[c] + sizes[c]], 'genome', back)  6.45 us
    ppermute x1, waiting for transfers between devices, per_device(): next_counts = lax.ppermute(counts, 'genome', back)  3.4 us
    ppermute x1, starting transfers between devices, per_device(): counts = counts + lax.ppermute(counts, 'samples', [(0, 1), (1, 0)])  3.06 us
    pallas_call x1, Pallas kernels, load(): pl.pallas_call(load_kernel, in_specs=[pl.BlockSpec(memory_space=pltpu.HBM...  2.42 us
  transfers between devices with their start and end apart: 13, of which 4 were waited for; matrix products, arithmetic and copies ran while one was open for 0% of the time, Pallas kernels for 12%

profile of v6, /device:TPU:0, one launch (start us, length us, event | category | flops | bytes accessed | tf_op | source)
XLA Modules:
  0.0 100.3 jit_solution(8213858353712320383)
XLA Ops:
  0.6 1.6 %slice.15 = bf16[2048,384]{1,0:T(8,128)(2,1)S(1)} slice(bf16[2048,1024]{1,0:T(8,128)(2,1)} %hap_hbm.1), slice={[0:2048], [0:384]} | slice | bytes 3145728 | tf_op jit(solution)/shard_map/slice | solution.py:286
  2.2 1.3 %collective-permute-start.2 = (bf16[2048,384]{1,0:T(8,128)(2,1)S(1)}, bf16[2048,384]{1,0:T(8,128)(2,1)S(1)}, u32[]{:S(2)}, u32[]{:S(2)}) collective-permute-start(bf16[2048,384]{1,0:T(8,128)(2,1)S(1)} %slice.15), channel_id=1, source_target_pairs={{2,0},{4,2},{6,4},{8,6},{10,8},{12,10},{14,12},{16,14},{18,16},{20... | collective-permute-start | bytes 4718600 | tf_op jit(solution)/shard_map/ppermute | solution.py:286
  3.5 2.4 %local_counts.1 = (bf16[2048,1024]{1,0:T(8,128)(2,1)S(1)}, f32[1,1024]{1,0:T(1,128)S(1)}) custom-call(bf16[2048,1024]{1,0:T(8,128)(2,1)} %hap_hbm.1), custom_call_target="tpu_custom_call" | custom-call | tf_op jit(solution)/shard_map/local_counts/pallas_call | solution.py:73
  5.9 0.1 slice.16
  6.1 1.3 %collective-permute-start.5 = (bf16[2048,256]{1,0:T(8,128)(2,1)S(1)}, bf16[2048,256]{1,0:T(8,128)(2,1)S(1)}, u32[]{:S(2)}, u32[]{:S(2)}) collective-permute-start(bf16[2048,256]{1,0:T(8,128)(2,1)S(1)} %slice.16), channel_id=1, source_target_pairs={{2,0},{4,2},{6,4},{8,6},{10,8},{12,10},{14,12},{16,14},{18,16},{20... | collective-permute-start | bytes 3145736 | tf_op jit(solution)/shard_map/ppermute | solution.py:286
  7.4 0.3 fusion
  7.6 1.3 %collective-permute-start.7 = (bf16[2048,128]{1,0:T(8,128)(2,1)S(1)}, bf16[2048,128]{1,0:T(8,128)(2,1)S(1)}, u32[]{:S(2)}, u32[]{:S(2)}) collective-permute-start(bf16[2048,128]{1,0:T(8,128)(2,1)S(1)} %get-tuple-element.60), channel_id=1, source_target_pairs={{2,0},{4,2},{6,4},{8,6},{10,8},{12,10},{14,12},{16,14},{18,16},{20... | collective-permute-start | bytes 1572872 | tf_op jit(solution)/shard_map/ppermute | solution.py:286
  8.9 1.3 %collective-permute-start.9 = (bf16[2048,128]{1,0:T(8,128)(2,1)S(1)}, bf16[2048,128]{1,0:T(8,128)(2,1)S(1)}, u32[]{:S(2)}, u32[]{:S(2)}) collective-permute-start(bf16[2048,128]{1,0:T(8,128)(2,1)S(1)} %get-tuple-element.59), channel_id=1, source_target_pairs={{2,0},{4,2},{6,4},{8,6},{10,8},{12,10},{14,12},{16,14},{18,16},{20... | collective-permute-start | bytes 1572872 | tf_op jit(solution)/shard_map/ppermute | solution.py:286
  10.2 3.1 %collective-permute-start = (f32[1,1024]{1,0:T(1,128)S(1)}, f32[1,1024]{1,0:T(1,128)S(1)}, u32[]{:S(2)}, u32[]{:S(2)}) collective-permute-start(f32[1,1024]{1,0:T(1,128)S(1)} %get-tuple-element.31), channel_id=1, source_target_pairs={{0,1},{1,0},{2,3},{3,2},{4,5},{5,4},{6,7},{7,6},{8,9},{9,8},{10,11... | collective-permute-start | bytes 12296 | tf_op jit(solution)/shard_map/ppermute | solution.py:292
  13.3 1.6 %collective-permute-done = f32[1,1024]{1,0:T(1,128)S(1)} collective-permute-done((f32[1,1024]{1,0:T(1,128)S(1)}, f32[1,1024]{1,0:T(1,128)S(1)}, u32[]{:S(2)}, u32[]{:S(2)}) %collective-permute-start) | collective-permute-done | bytes 4128 | tf_op jit(solution)/shard_map/ppermute | solution.py:292
  14.9 1.3 %collective-permute-start.3 = (f32[1,1024]{1,0:T(1,128)S(1)}, f32[1,1024]{1,0:T(1,128)S(1)}, u32[]{:S(2)}, u32[]{:S(2)}) collective-permute-start(f32[1,1024]{1,0:T(1,128)S(1)} %add.3.counts_ref), channel_id=1, source_target_pairs={{2,0},{4,2},{6,4},{8,6},{10,8},{12,10},{14,12},{16,14},{18,16},{20... | collective-permute-start | bytes 12296 | tf_op jit(solution)/shard_map/ppermute | solution.py:295
  16.2 3.4 %collective-permute-done.3.counts_ref = f32[1,1024]{1,0:T(1,128)S(1)} collective-permute-done((f32[1,1024]{1,0:T(1,128)S(1)}, f32[1,1024]{1,0:T(1,128)S(1)}, u32[]{:S(2)}, u32[]{:S(2)}) %collective-permute-start.3) | collective-permute-done | bytes 4128 | tf_op jit(solution)/shard_map/ppermute | solution.py:295
  19.6 1.3 %collective-permute-start.11 = (bf16[2048,128]{1,0:T(8,128)(2,1)S(1)}, bf16[2048,128]{1,0:T(8,128)(2,1)S(1)}, u32[]{:S(2)}, u32[]{:S(2)}) collective-permute-start(bf16[2048,128]{1,0:T(8,128)(2,1)S(1)} %get-tuple-element.58), channel_id=1, source_target_pairs={{2,0},{4,2},{6,4},{8,6},{10,8},{12,10},{14,12},{16,14},{18,16},{20... | collective-permute-start | bytes 1572872 | tf_op jit(solution)/shard_map/ppermute | solution.py:286
  20.9 4.2 %shard_map.41 = (bf16[2048,1024]{1,0:T(8,128)(2,1)S(1)}, f32[2,512]{1,0:T(2,128)S(1)}, f32[8,128]{1,0:T(8,128)S(1)}, f32[512,512]{1,0:T(8,128)S(1)}, bf16[512,51...) custom-call(bf16[2048,1024]{1,0:T(8,128)(2,1)S(1)} %get-tuple-element.3, ...), custom_call_target="tpu_custom_call" | custom-call | tf_op jit(solution)/shard_map/pallas_call | solution.py:34
  25.1 0.0 collective-permute-done.2.raw_ref
  25.1 1.8 %collective-permute-start.1 = (bf16[512,512]{1,0:T(8,128)(2,1)S(1)}, bf16[512,512]{1,0:T(8,128)(2,1)S(1)}, u32[]{:S(2)}, u32[]{:S(2)}) collective-permute-start(bf16[512,512]{1,0:T(8,128)(2,1)S(1)} %get-tuple-element.33), channel_id=1, source_target_pairs={{0,1},{1,0},{2,3},{3,2},{4,5},{5,4},{6,7},{7,6},{8,9},{9,8},{10,11... | collective-permute-start | bytes 1572872 | tf_op jit(solution)/shard_map/ppermute | solution.py:298
  26.9 1.8 %shard_map.42 = (f32[8,128]{1,0:T(8,128)S(1)}, f32[384,512]{1,0:T(8,128)S(1)}, bf16[384,512]{1,0:T(8,128)(2,1)S(1)}) custom-call(bf16[2048,384]{1,0:T(8,128)(2,1)S(1)} %collective-permute-done.2.raw_ref, f32[1,1024]{1,0:T(1,128)S(1)} %collective-permute-done.3.counts_ref, bf16[2048,1024]{1,0:T(8,128)(2,1)S(1)} %get-tuple-element.34.std_ref, ...), custom_call_target="tpu_custom_call" | custom-call | tf_op jit(solution)/shard_map/pallas_call | solution.py:34
  28.8 0.0 collective-permute-done.5.raw_ref
  28.8 0.3 collective-permute-start.4
  29.1 1.0 shard_map.43
  30.1 0.0 collective-permute-done.7.raw_ref
  30.1 1.8 %collective-permute-start.6 = (bf16[256,512]{1,0:T(8,128)(2,1)S(1)}, bf16[256,512]{1,0:T(8,128)(2,1)S(1)}, u32[]{:S(2)}, u32[]{:S(2)}) collective-permute-start(bf16[256,512]{1,0:T(8,128)(2,1)S(1)} %get-tuple-element.42), channel_id=1, source_target_pairs={{0,1},{1,0},{2,3},{3,2},{4,5},{5,4},{6,7},{7,6},{8,9},{9,8},{10,11... | collective-permute-start | bytes 786440 | tf_op jit(solution)/shard_map/ppermute | solution.py:298
  31.9 0.5 shard_map.45
  32.4 0.0 collective-permute-done.9.raw_ref
  32.4 0.4 collective-permute-start.8
  32.8 0.0 copy-start
  32.8 1.0 shard_map.46
  33.8 17.3 %collective-permute-done.11.raw_ref = bf16[2048,128]{1,0:T(8,128)(2,1)S(1)} collective-permute-done((bf16[2048,128]{1,0:T(8,128)(2,1)S(1)}, bf16[2048,128]{1,0:T(8,128)(2,1)S(1)}, u32[]{:S(2)}, u32[]{:S(2)}) %collective-permute-start.11) | collective-permute-done | bytes 524320 | tf_op jit(solution)/shard_map/ppermute | solution.py:286
  51.1 1.5 %collective-permute-start.10 = (bf16[128,256]{1,0:T(8,128)(2,1)S(1)}, bf16[128,256]{1,0:T(8,128)(2,1)S(1)}, u32[]{:S(2)}, u32[]{:S(2)}) collective-permute-start(bf16[128,256]{1,0:T(8,128)(2,1)S(1)} %get-tuple-element.51), channel_id=1, source_target_pairs={{0,1},{1,0},{2,3},{3,2},{4,5},{5,4},{6,7},{7,6},{8,9},{9,8},{10,11... | collective-permute-start | bytes 196616 | tf_op jit(solution)/shard_map/ppermute | solution.py:298
  52.6 0.4 shard_map.47
  53.0 0.0 collective-permute-done.1.refs_1_
  53.0 2.4 %collective-permute-start.12 = (bf16[128,128]{1,0:T(8,128)(2,1)S(1)}, bf16[128,128]{1,0:T(8,128)(2,1)S(1)}, u32[]{:S(2)}, u32[]{:S(2)}) collective-permute-start(bf16[128,128]{1,0:T(8,128)(2,1)S(1)} %get-tuple-element.53), channel_id=1, source_target_pairs={{0,1},{2,3},{4,5},{6,7},{8,9},{10,11},{12,13},{14,15},{16,17},{18,... | collective-permute-start | bytes 98312 | tf_op jit(solution)/shard_map/ppermute | solution.py:298
  55.4 0.0 collective-permute-done.6.refs_6_
  55.4 0.0 collective-permute-done.4.refs_3_
  55.4 0.0 copy-done
  55.4 1.1 %shard_map.44.sums_ref = f32[1,512]{1,0:T(1,128)S(1)} custom-call(s32[1,512]{1,0:T(1,128)S(1)} %bitcast.8, f32[512,512]{1,0:T(8,128)S(1)} %get-tuple-element.32.refs_0_, bf16[512,512]{1,0:T(8,128)(2,1)S(1)} %collective-permute-done.1.refs_1_, f32[384,512]{1,0:T(8,128)S(1)} %get-tuple-element.36.refs_2_, bf16[384,512]{1,0:T(8,128)(2,1)S(1)} %collective-permute-done.4.refs_3_, ...), custom_call_target="tpu_custom_call" | custom-call | tf_op jit(solution)/shard_map/pallas_call | solution.py:34
  56.5 0.7 collective-permute-done.12.refs_7_
  57.2 0.0 collective-permute-done.10.refs_5_
  57.2 0.0 collective-permute-done.8.refs_3_
  57.2 0.8 shard_map.48
  58.0 41.7 %all_to_all.5 = f32[32,1,128]{2,1,0:T(1,128)S(1)} all-to-all(f32[32,1,128]{2,1,0:T(1,128)S(1)} %bitcast.7), channel_id=1, replica_groups=mesh['genome'=16,'samples'=2] {'genome','samples'}, dimensions={0} | all-to-all | bytes 32768 | tf_op jit(solution)/shard_map/all_to_all | solution.py:414
  99.6 0.7 shard_map.49
  (1 shorter events, 0.0 us)
Async XLA Ops:
  2.2 22.9 %collective-permute-start.2 = (bf16[2048,384]{1,0:T(8,128)(2,1)S(1)}, bf16[2048,384]{1,0:T(8,128)(2,1)S(1)}, u32[]{:S(2)}, u32[]{:S(2)}) collective-permute-start(bf16[2048,384]{1,0:T(8,128)(2,1)S(1)} %slice.15), channel_id=1, source_target_pairs={{2,0},{4,2},{6,4},{8,6},{10,8},{12,10},{14,12},{16,14},{18,16},{20... | collective-permute-start | bytes 4718600 | tf_op jit(solution)/shard_map/ppermute | solution.py:286
  6.1 22.7 %collective-permute-start.5 = (bf16[2048,256]{1,0:T(8,128)(2,1)S(1)}, bf16[2048,256]{1,0:T(8,128)(2,1)S(1)}, u32[]{:S(2)}, u32[]{:S(2)}) collective-permute-start(bf16[2048,256]{1,0:T(8,128)(2,1)S(1)} %slice.16), channel_id=1, source_target_pairs={{2,0},{4,2},{6,4},{8,6},{10,8},{12,10},{14,12},{16,14},{18,16},{20... | collective-permute-start | bytes 3145736 | tf_op jit(solution)/shard_map/ppermute | solution.py:286
  7.6 22.5 %collective-permute-start.7 = (bf16[2048,128]{1,0:T(8,128)(2,1)S(1)}, bf16[2048,128]{1,0:T(8,128)(2,1)S(1)}, u32[]{:S(2)}, u32[]{:S(2)}) collective-permute-start(bf16[2048,128]{1,0:T(8,128)(2,1)S(1)} %get-tuple-element.60), channel_id=1, source_target_pairs={{2,0},{4,2},{6,4},{8,6},{10,8},{12,10},{14,12},{16,14},{18,16},{20... | collective-permute-start | bytes 1572872 | tf_op jit(solution)/shard_map/ppermute | solution.py:286
  8.9 23.5 %collective-permute-start.9 = (bf16[2048,128]{1,0:T(8,128)(2,1)S(1)}, bf16[2048,128]{1,0:T(8,128)(2,1)S(1)}, u32[]{:S(2)}, u32[]{:S(2)}) collective-permute-start(bf16[2048,128]{1,0:T(8,128)(2,1)S(1)} %get-tuple-element.59), channel_id=1, source_target_pairs={{2,0},{4,2},{6,4},{8,6},{10,8},{12,10},{14,12},{16,14},{18,16},{20... | collective-permute-start | bytes 1572872 | tf_op jit(solution)/shard_map/ppermute | solution.py:286
  10.2 4.6 %collective-permute-start = (f32[1,1024]{1,0:T(1,128)S(1)}, f32[1,1024]{1,0:T(1,128)S(1)}, u32[]{:S(2)}, u32[]{:S(2)}) collective-permute-start(f32[1,1024]{1,0:T(1,128)S(1)} %get-tuple-element.31), channel_id=1, source_target_pairs={{0,1},{1,0},{2,3},{3,2},{4,5},{5,4},{6,7},{7,6},{8,9},{9,8},{10,11... | collective-permute-start | bytes 12296 | tf_op jit(solution)/shard_map/ppermute | solution.py:292
  14.9 4.7 %collective-permute-start.3 = (f32[1,1024]{1,0:T(1,128)S(1)}, f32[1,1024]{1,0:T(1,128)S(1)}, u32[]{:S(2)}, u32[]{:S(2)}) collective-permute-start(f32[1,1024]{1,0:T(1,128)S(1)} %add.3.counts_ref), channel_id=1, source_target_pairs={{2,0},{4,2},{6,4},{8,6},{10,8},{12,10},{14,12},{16,14},{18,16},{20... | collective-permute-start | bytes 12296 | tf_op jit(solution)/shard_map/ppermute | solution.py:295
  19.6 31.5 %collective-permute-start.11 = (bf16[2048,128]{1,0:T(8,128)(2,1)S(1)}, bf16[2048,128]{1,0:T(8,128)(2,1)S(1)}, u32[]{:S(2)}, u32[]{:S(2)}) collective-permute-start(bf16[2048,128]{1,0:T(8,128)(2,1)S(1)} %get-tuple-element.58), channel_id=1, source_target_pairs={{2,0},{4,2},{6,4},{8,6},{10,8},{12,10},{14,12},{16,14},{18,16},{20... | collective-permute-start | bytes 1572872 | tf_op jit(solution)/shard_map/ppermute | solution.py:286
  25.1 27.9 %collective-permute-start.1 = (bf16[512,512]{1,0:T(8,128)(2,1)S(1)}, bf16[512,512]{1,0:T(8,128)(2,1)S(1)}, u32[]{:S(2)}, u32[]{:S(2)}) collective-permute-start(bf16[512,512]{1,0:T(8,128)(2,1)S(1)} %get-tuple-element.33), channel_id=1, source_target_pairs={{0,1},{1,0},{2,3},{3,2},{4,5},{5,4},{6,7},{7,6},{8,9},{9,8},{10,11... | collective-permute-start | bytes 1572872 | tf_op jit(solution)/shard_map/ppermute | solution.py:298
  28.8 26.6 %collective-permute-start.4 = (bf16[384,512]{1,0:T(8,128)(2,1)S(1)}, bf16[384,512]{1,0:T(8,128)(2,1)S(1)}, u32[]{:S(2)}, u32[]{:S(2)}) collective-permute-start(bf16[384,512]{1,0:T(8,128)(2,1)S(1)} %get-tuple-element.37), channel_id=1, source_target_pairs={{0,1},{1,0},{2,3},{3,2},{4,5},{5,4},{6,7},{7,6},{8,9},{9,8},{10,11... | collective-permute-start | bytes 1179656 | tf_op jit(solution)/shard_map/ppermute | solution.py:298
  30.1 25.3 %collective-permute-start.6 = (bf16[256,512]{1,0:T(8,128)(2,1)S(1)}, bf16[256,512]{1,0:T(8,128)(2,1)S(1)}, u32[]{:S(2)}, u32[]{:S(2)}) collective-permute-start(bf16[256,512]{1,0:T(8,128)(2,1)S(1)} %get-tuple-element.42), channel_id=1, source_target_pairs={{0,1},{1,0},{2,3},{3,2},{4,5},{5,4},{6,7},{7,6},{8,9},{9,8},{10,11... | collective-permute-start | bytes 786440 | tf_op jit(solution)/shard_map/ppermute | solution.py:298
  32.4 24.7 %collective-permute-start.8 = (bf16[128,384]{1,0:T(8,128)(2,1)S(1)}, bf16[128,384]{1,0:T(8,128)(2,1)S(1)}, u32[]{:S(2)}, u32[]{:S(2)}) collective-permute-start(bf16[128,384]{1,0:T(8,128)(2,1)S(1)} %get-tuple-element.48), channel_id=1, source_target_pairs={{0,1},{1,0},{2,3},{3,2},{4,5},{5,4},{6,7},{7,6},{8,9},{9,8},{10,11... | collective-permute-start | bytes 294920 | tf_op jit(solution)/shard_map/ppermute | solution.py:298
  32.8 22.6 %copy-start = (s32[512]{0:T(512)S(1)}, s32[512]{0:T(512)}, u32[]{:S(2)}) copy-start(s32[512]{0:T(512)} %param.3) | copy-start | bytes 6148
  51.1 6.1 %collective-permute-start.10 = (bf16[128,256]{1,0:T(8,128)(2,1)S(1)}, bf16[128,256]{1,0:T(8,128)(2,1)S(1)}, u32[]{:S(2)}, u32[]{:S(2)}) collective-permute-start(bf16[128,256]{1,0:T(8,128)(2,1)S(1)} %get-tuple-element.51), channel_id=1, source_target_pairs={{0,1},{1,0},{2,3},{3,2},{4,5},{5,4},{6,7},{7,6},{8,9},{9,8},{10,11... | collective-permute-start | bytes 196616 | tf_op jit(solution)/shard_map/ppermute | solution.py:298
  53.0 4.2 %collective-permute-start.12 = (bf16[128,128]{1,0:T(8,128)(2,1)S(1)}, bf16[128,128]{1,0:T(8,128)(2,1)S(1)}, u32[]{:S(2)}, u32[]{:S(2)}) collective-permute-start(bf16[128,128]{1,0:T(8,128)(2,1)S(1)} %get-tuple-element.53), channel_id=1, source_target_pairs={{0,1},{2,3},{4,5},{6,7},{8,9},{10,11},{12,13},{14,15},{16,17},{18,... | collective-permute-start | bytes 98312 | tf_op jit(solution)/shard_map/ppermute | solution.py:298

commit v7 on v6

--- a/solution.py
+++ b/solution.py
@@ -294,8 +294,8 @@
         counts = lax.psum(counts, "samples")
     next_counts = lax.ppermute(counts, "genome", back)
 
-    def swap(send, pairs=((0, 1), (1, 0))):
-        return lax.ppermute(send, "samples", pairs)
+    def swap(send):
+        return lax.ppermute(send, "samples", [(0, 1), (1, 0)])
 
     tails, tail_pieces = [], []
     token_type = ((8, LANES), f32)
@@ -372,7 +372,7 @@
             next_counts,
             standard,
         )
-        tails += [keep, swap(send, [(0, 1)])]
+        tails += [keep, swap(send)]
         tail_pieces = [
             (0, 0, (first_unit, lower), 3, (whole, lower), 0, 0),
             (0, 0, (slice(u, half), lower), 5, (whole, lower), u, 0),

time: 101 us -> 101 us (level)
  waiting for transfers between devices: 23 us -> 25 us
  starting transfers between devices: 19 us -> 17.2 us
    ppermute x6, waiting for transfers between devices: 0.66 us -> 2.68 us  [swap(): return lax.ppermute(send, 'samples', [(0, 1), (1, 0)])]
    ppermute x6, starting transfers between devices: 8.25 us -> 6.41 us  [swap(): return lax.ppermute(send, 'samples', [(0, 1), (1, 0)])]
where the time goes in v7:
time: 101 us; the launch traced here: 100 us
  blocking collectives  41.5 us (41%)
  waiting for transfers between devices  25 us (25%)
  starting transfers between devices  17.2 us (17%)
  Pallas kernels  13.8 us (14%)
  local copies, waits for them, and re-layouts  1.98 us (2%)
    all_to_all x1, blocking collectives, per_device(): lax.all_to_all(last[:, None], ('genome', 'samples'), 0, 0, tiled=True)[:, 0]  41.5 us
    ppermute x5, waiting for transfers between devices, shifted(): lax.ppermute(array[:, firsts[c]:firsts[c] + sizes[c]], 'genome', back)  17.3 us
    pallas_call x9, Pallas kernels, call(): pl.pallas_call(kernel, in_specs=[pl.BlockSpec(memory_space=pltpu.VMEM)] *...  11.4 us
    ppermute x5, starting transfers between devices, shifted(): lax.ppermute(array[:, firsts[c]:firsts[c] + sizes[c]], 'genome', back)  6.45 us
    ppermute x6, starting transfers between devices, swap(): return lax.ppermute(send, 'samples', [(0, 1), (1, 0)])  6.41 us
    ppermute x1, waiting for transfers between devices, per_device(): next_counts = lax.ppermute(counts, 'genome', back)  3.4 us
    ppermute x1, starting transfers between devices, per_device(): counts = counts + lax.ppermute(counts, 'samples', [(0, 1), (1, 0)])  3.06 us
    ppermute x6, waiting for transfers between devices, swap(): return lax.ppermute(send, 'samples', [(0, 1), (1, 0)])  2.68 us
  transfers between devices with their start and end apart: 13, of which 4 were waited for; matrix products, arithmetic and copies ran while one was open for 0% of the time, Pallas kernels for 12%

profile of v7, /device:TPU:0, one launch (start us, length us, event | category | flops | bytes accessed | tf_op | source)
XLA Modules:
  0.0 100.3 jit_solution(3575156908619503141)
XLA Ops:
  0.6 1.6 %slice.15 = bf16[2048,384]{1,0:T(8,128)(2,1)S(1)} slice(bf16[2048,1024]{1,0:T(8,128)(2,1)} %hap_hbm.1), slice={[0:2048], [0:384]} | slice | bytes 3145728 | tf_op jit(solution)/shard_map/slice | solution.py:286
  2.2 1.3 %collective-permute-start.2 = (bf16[2048,384]{1,0:T(8,128)(2,1)S(1)}, bf16[2048,384]{1,0:T(8,128)(2,1)S(1)}, u32[]{:S(2)}, u32[]{:S(2)}) collective-permute-start(bf16[2048,384]{1,0:T(8,128)(2,1)S(1)} %slice.15), channel_id=1, source_target_pairs={{2,0},{4,2},{6,4},{8,6},{10,8},{12,10},{14,12},{16,14},{18,16},{20... | collective-permute-start | bytes 4718600 | tf_op jit(solution)/shard_map/ppermute | solution.py:286
  3.5 2.4 %local_counts.1 = (bf16[2048,1024]{1,0:T(8,128)(2,1)S(1)}, f32[1,1024]{1,0:T(1,128)S(1)}) custom-call(bf16[2048,1024]{1,0:T(8,128)(2,1)} %hap_hbm.1), custom_call_target="tpu_custom_call" | custom-call | tf_op jit(solution)/shard_map/local_counts/pallas_call | solution.py:73
  5.9 0.1 slice.16
  6.1 1.3 %collective-permute-start.5 = (bf16[2048,256]{1,0:T(8,128)(2,1)S(1)}, bf16[2048,256]{1,0:T(8,128)(2,1)S(1)}, u32[]{:S(2)}, u32[]{:S(2)}) collective-permute-start(bf16[2048,256]{1,0:T(8,128)(2,1)S(1)} %slice.16), channel_id=1, source_target_pairs={{2,0},{4,2},{6,4},{8,6},{10,8},{12,10},{14,12},{16,14},{18,16},{20... | collective-permute-start | bytes 3145736 | tf_op jit(solution)/shard_map/ppermute | solution.py:286
  7.4 0.3 fusion
  7.6 1.3 %collective-permute-start.7 = (bf16[2048,128]{1,0:T(8,128)(2,1)S(1)}, bf16[2048,128]{1,0:T(8,128)(2,1)S(1)}, u32[]{:S(2)}, u32[]{:S(2)}) collective-permute-start(bf16[2048,128]{1,0:T(8,128)(2,1)S(1)} %get-tuple-element.60), channel_id=1, source_target_pairs={{2,0},{4,2},{6,4},{8,6},{10,8},{12,10},{14,12},{16,14},{18,16},{20... | collective-permute-start | bytes 1572872 | tf_op jit(solution)/shard_map/ppermute | solution.py:286
  8.9 1.3 %collective-permute-start.9 = (bf16[2048,128]{1,0:T(8,128)(2,1)S(1)}, bf16[2048,128]{1,0:T(8,128)(2,1)S(1)}, u32[]{:S(2)}, u32[]{:S(2)}) collective-permute-start(bf16[2048,128]{1,0:T(8,128)(2,1)S(1)} %get-tuple-element.59), channel_id=1, source_target_pairs={{2,0},{4,2},{6,4},{8,6},{10,8},{12,10},{14,12},{16,14},{18,16},{20... | collective-permute-start | bytes 1572872 | tf_op jit(solution)/shard_map/ppermute | solution.py:286
  10.2 3.1 %collective-permute-start = (f32[1,1024]{1,0:T(1,128)S(1)}, f32[1,1024]{1,0:T(1,128)S(1)}, u32[]{:S(2)}, u32[]{:S(2)}) collective-permute-start(f32[1,1024]{1,0:T(1,128)S(1)} %get-tuple-element.31), channel_id=1, source_target_pairs={{0,1},{1,0},{2,3},{3,2},{4,5},{5,4},{6,7},{7,6},{8,9},{9,8},{10,11... | collective-permute-start | bytes 12296 | tf_op jit(solution)/shard_map/ppermute | solution.py:292
  13.3 1.6 %collective-permute-done = f32[1,1024]{1,0:T(1,128)S(1)} collective-permute-done((f32[1,1024]{1,0:T(1,128)S(1)}, f32[1,1024]{1,0:T(1,128)S(1)}, u32[]{:S(2)}, u32[]{:S(2)}) %collective-permute-start) | collective-permute-done | bytes 4128 | tf_op jit(solution)/shard_map/ppermute | solution.py:292
  14.9 1.3 %collective-permute-start.3 = (f32[1,1024]{1,0:T(1,128)S(1)}, f32[1,1024]{1,0:T(1,128)S(1)}, u32[]{:S(2)}, u32[]{:S(2)}) collective-permute-start(f32[1,1024]{1,0:T(1,128)S(1)} %add.3.counts_ref), channel_id=1, source_target_pairs={{2,0},{4,2},{6,4},{8,6},{10,8},{12,10},{14,12},{16,14},{18,16},{20... | collective-permute-start | bytes 12296 | tf_op jit(solution)/shard_map/ppermute | solution.py:295
  16.2 3.4 %collective-permute-done.3.counts_ref = f32[1,1024]{1,0:T(1,128)S(1)} collective-permute-done((f32[1,1024]{1,0:T(1,128)S(1)}, f32[1,1024]{1,0:T(1,128)S(1)}, u32[]{:S(2)}, u32[]{:S(2)}) %collective-permute-start.3) | collective-permute-done | bytes 4128 | tf_op jit(solution)/shard_map/ppermute | solution.py:295
  19.6 1.3 %collective-permute-start.11 = (bf16[2048,128]{1,0:T(8,128)(2,1)S(1)}, bf16[2048,128]{1,0:T(8,128)(2,1)S(1)}, u32[]{:S(2)}, u32[]{:S(2)}) collective-permute-start(bf16[2048,128]{1,0:T(8,128)(2,1)S(1)} %get-tuple-element.58), channel_id=1, source_target_pairs={{2,0},{4,2},{6,4},{8,6},{10,8},{12,10},{14,12},{16,14},{18,16},{20... | collective-permute-start | bytes 1572872 | tf_op jit(solution)/shard_map/ppermute | solution.py:286
  20.9 4.2 %shard_map.41 = (bf16[2048,1024]{1,0:T(8,128)(2,1)S(1)}, f32[2,512]{1,0:T(2,128)S(1)}, f32[8,128]{1,0:T(8,128)S(1)}, f32[512,512]{1,0:T(8,128)S(1)}, bf16[512,51...) custom-call(bf16[2048,1024]{1,0:T(8,128)(2,1)S(1)} %get-tuple-element.3, ...), custom_call_target="tpu_custom_call" | custom-call | tf_op jit(solution)/shard_map/pallas_call | solution.py:34
  25.1 0.0 collective-permute-done.2.raw_ref
  25.1 1.8 %collective-permute-start.1 = (bf16[512,512]{1,0:T(8,128)(2,1)S(1)}, bf16[512,512]{1,0:T(8,128)(2,1)S(1)}, u32[]{:S(2)}, u32[]{:S(2)}) collective-permute-start(bf16[512,512]{1,0:T(8,128)(2,1)S(1)} %get-tuple-element.33), channel_id=1, source_target_pairs={{0,1},{1,0},{2,3},{3,2},{4,5},{5,4},{6,7},{7,6},{8,9},{9,8},{10,11... | collective-permute-start | bytes 1572872 | tf_op jit(solution)/shard_map/ppermute | solution.py:298
  26.9 1.8 %shard_map.42 = (f32[8,128]{1,0:T(8,128)S(1)}, f32[384,512]{1,0:T(8,128)S(1)}, bf16[384,512]{1,0:T(8,128)(2,1)S(1)}) custom-call(bf16[2048,384]{1,0:T(8,128)(2,1)S(1)} %collective-permute-done.2.raw_ref, f32[1,1024]{1,0:T(1,128)S(1)} %collective-permute-done.3.counts_ref, bf16[2048,1024]{1,0:T(8,128)(2,1)S(1)} %get-tuple-element.34.std_ref, ...), custom_call_target="tpu_custom_call" | custom-call | tf_op jit(solution)/shard_map/pallas_call | solution.py:34
  28.8 0.0 collective-permute-done.5.raw_ref
  28.8 0.3 collective-permute-start.4
  29.1 1.0 shard_map.43
  30.1 0.0 collective-permute-done.7.raw_ref
  30.1 1.8 %collective-permute-start.6 = (bf16[256,512]{1,0:T(8,128)(2,1)S(1)}, bf16[256,512]{1,0:T(8,128)(2,1)S(1)}, u32[]{:S(2)}, u32[]{:S(2)}) collective-permute-start(bf16[256,512]{1,0:T(8,128)(2,1)S(1)} %get-tuple-element.42), channel_id=1, source_target_pairs={{0,1},{1,0},{2,3},{3,2},{4,5},{5,4},{6,7},{7,6},{8,9},{9,8},{10,11... | collective-permute-start | bytes 786440 | tf_op jit(solution)/shard_map/ppermute | solution.py:298
  31.9 0.5 shard_map.45
  32.4 0.0 collective-permute-done.9.raw_ref
  32.4 0.4 collective-permute-start.8
  32.8 0.0 copy-start
  32.8 1.0 shard_map.46
  33.8 17.3 %collective-permute-done.11.raw_ref = bf16[2048,128]{1,0:T(8,128)(2,1)S(1)} collective-permute-done((bf16[2048,128]{1,0:T(8,128)(2,1)S(1)}, bf16[2048,128]{1,0:T(8,128)(2,1)S(1)}, u32[]{:S(2)}, u32[]{:S(2)}) %collective-permute-start.11) | collective-permute-done | bytes 524320 | tf_op jit(solution)/shard_map/ppermute | solution.py:286
  51.1 1.5 %collective-permute-start.10 = (bf16[128,256]{1,0:T(8,128)(2,1)S(1)}, bf16[128,256]{1,0:T(8,128)(2,1)S(1)}, u32[]{:S(2)}, u32[]{:S(2)}) collective-permute-start(bf16[128,256]{1,0:T(8,128)(2,1)S(1)} %get-tuple-element.51), channel_id=1, source_target_pairs={{0,1},{1,0},{2,3},{3,2},{4,5},{5,4},{6,7},{7,6},{8,9},{9,8},{10,11... | collective-permute-start | bytes 196616 | tf_op jit(solution)/shard_map/ppermute | solution.py:298
  52.6 0.4 shard_map.47
  53.0 0.0 collective-permute-done.1.refs_1_
  53.0 0.6 collective-permute-start.12
  53.6 0.0 collective-permute-done.6.refs_6_
  53.6 0.0 collective-permute-done.4.refs_3_
  53.6 0.0 copy-done
  53.6 1.1 %shard_map.44.sums_ref = f32[1,512]{1,0:T(1,128)S(1)} custom-call(s32[1,512]{1,0:T(1,128)S(1)} %bitcast.8, f32[512,512]{1,0:T(8,128)S(1)} %get-tuple-element.32.refs_0_, bf16[512,512]{1,0:T(8,128)(2,1)S(1)} %collective-permute-done.1.refs_1_, f32[384,512]{1,0:T(8,128)S(1)} %get-tuple-element.36.refs_2_, bf16[384,512]{1,0:T(8,128)(2,1)S(1)} %collective-permute-done.4.refs_3_, ...), custom_call_target="tpu_custom_call" | custom-call | tf_op jit(solution)/shard_map/pallas_call | solution.py:34
  54.7 2.7 %collective-permute-done.12.refs_7_ = bf16[128,128]{1,0:T(8,128)(2,1)S(1)} collective-permute-done((bf16[128,128]{1,0:T(8,128)(2,1)S(1)}, bf16[128,128]{1,0:T(8,128)(2,1)S(1)}, u32[]{:S(2)}, u32[]{:S(2)}) %collective-permute-start.12) | collective-permute-done | bytes 32800 | tf_op jit(solution)/shard_map/ppermute | solution.py:298
  57.3 0.0 collective-permute-done.10.refs_5_
  57.3 0.0 collective-permute-done.8.refs_3_
  57.3 0.8 shard_map.48
  58.1 41.5 %all_to_all.5 = f32[32,1,128]{2,1,0:T(1,128)S(1)} all-to-all(f32[32,1,128]{2,1,0:T(1,128)S(1)} %bitcast.7), channel_id=1, replica_groups=mesh['genome'=16,'samples'=2] {'genome','samples'}, dimensions={0} | all-to-all | bytes 32768 | tf_op jit(solution)/shard_map/all_to_all | solution.py:414
  99.6 0.7 shard_map.49
  (1 shorter events, 0.0 us)
Async XLA Ops:
  2.2 22.9 %collective-permute-start.2 = (bf16[2048,384]{1,0:T(8,128)(2,1)S(1)}, bf16[2048,384]{1,0:T(8,128)(2,1)S(1)}, u32[]{:S(2)}, u32[]{:S(2)}) collective-permute-start(bf16[2048,384]{1,0:T(8,128)(2,1)S(1)} %slice.15), channel_id=1, source_target_pairs={{2,0},{4,2},{6,4},{8,6},{10,8},{12,10},{14,12},{16,14},{18,16},{20... | collective-permute-start | bytes 4718600 | tf_op jit(solution)/shard_map/ppermute | solution.py:286
  6.1 22.7 %collective-permute-start.5 = (bf16[2048,256]{1,0:T(8,128)(2,1)S(1)}, bf16[2048,256]{1,0:T(8,128)(2,1)S(1)}, u32[]{:S(2)}, u32[]{:S(2)}) collective-permute-start(bf16[2048,256]{1,0:T(8,128)(2,1)S(1)} %slice.16), channel_id=1, source_target_pairs={{2,0},{4,2},{6,4},{8,6},{10,8},{12,10},{14,12},{16,14},{18,16},{20... | collective-permute-start | bytes 3145736 | tf_op jit(solution)/shard_map/ppermute | solution.py:286
  7.6 22.5 %collective-permute-start.7 = (bf16[2048,128]{1,0:T(8,128)(2,1)S(1)}, bf16[2048,128]{1,0:T(8,128)(2,1)S(1)}, u32[]{:S(2)}, u32[]{:S(2)}) collective-permute-start(bf16[2048,128]{1,0:T(8,128)(2,1)S(1)} %get-tuple-element.60), channel_id=1, source_target_pairs={{2,0},{4,2},{6,4},{8,6},{10,8},{12,10},{14,12},{16,14},{18,16},{20... | collective-permute-start | bytes 1572872 | tf_op jit(solution)/shard_map/ppermute | solution.py:286
  8.9 23.5 %collective-permute-start.9 = (bf16[2048,128]{1,0:T(8,128)(2,1)S(1)}, bf16[2048,128]{1,0:T(8,128)(2,1)S(1)}, u32[]{:S(2)}, u32[]{:S(2)}) collective-permute-start(bf16[2048,128]{1,0:T(8,128)(2,1)S(1)} %get-tuple-element.59), channel_id=1, source_target_pairs={{2,0},{4,2},{6,4},{8,6},{10,8},{12,10},{14,12},{16,14},{18,16},{20... | collective-permute-start | bytes 1572872 | tf_op jit(solution)/shard_map/ppermute | solution.py:286
  10.2 4.6 %collective-permute-start = (f32[1,1024]{1,0:T(1,128)S(1)}, f32[1,1024]{1,0:T(1,128)S(1)}, u32[]{:S(2)}, u32[]{:S(2)}) collective-permute-start(f32[1,1024]{1,0:T(1,128)S(1)} %get-tuple-element.31), channel_id=1, source_target_pairs={{0,1},{1,0},{2,3},{3,2},{4,5},{5,4},{6,7},{7,6},{8,9},{9,8},{10,11... | collective-permute-start | bytes 12296 | tf_op jit(solution)/shard_map/ppermute | solution.py:292
  14.9 4.7 %collective-permute-start.3 = (f32[1,1024]{1,0:T(1,128)S(1)}, f32[1,1024]{1,0:T(1,128)S(1)}, u32[]{:S(2)}, u32[]{:S(2)}) collective-permute-start(f32[1,1024]{1,0:T(1,128)S(1)} %add.3.counts_ref), channel_id=1, source_target_pairs={{2,0},{4,2},{6,4},{8,6},{10,8},{12,10},{14,12},{16,14},{18,16},{20... | collective-permute-start | bytes 12296 | tf_op jit(solution)/shard_map/ppermute | solution.py:295
  19.6 31.5 %collective-permute-start.11 = (bf16[2048,128]{1,0:T(8,128)(2,1)S(1)}, bf16[2048,128]{1,0:T(8,128)(2,1)S(1)}, u32[]{:S(2)}, u32[]{:S(2)}) collective-permute-start(bf16[2048,128]{1,0:T(8,128)(2,1)S(1)} %get-tuple-element.58), channel_id=1, source_target_pairs={{2,0},{4,2},{6,4},{8,6},{10,8},{12,10},{14,12},{16,14},{18,16},{20... | collective-permute-start | bytes 1572872 | tf_op jit(solution)/shard_map/ppermute | solution.py:286
  25.1 27.9 %collective-permute-start.1 = (bf16[512,512]{1,0:T(8,128)(2,1)S(1)}, bf16[512,512]{1,0:T(8,128)(2,1)S(1)}, u32[]{:S(2)}, u32[]{:S(2)}) collective-permute-start(bf16[512,512]{1,0:T(8,128)(2,1)S(1)} %get-tuple-element.33), channel_id=1, source_target_pairs={{0,1},{1,0},{2,3},{3,2},{4,5},{5,4},{6,7},{7,6},{8,9},{9,8},{10,11... | collective-permute-start | bytes 1572872 | tf_op jit(solution)/shard_map/ppermute | solution.py:298
  28.8 24.8 %collective-permute-start.4 = (bf16[384,512]{1,0:T(8,128)(2,1)S(1)}, bf16[384,512]{1,0:T(8,128)(2,1)S(1)}, u32[]{:S(2)}, u32[]{:S(2)}) collective-permute-start(bf16[384,512]{1,0:T(8,128)(2,1)S(1)} %get-tuple-element.37), channel_id=1, source_target_pairs={{0,1},{1,0},{2,3},{3,2},{4,5},{5,4},{6,7},{7,6},{8,9},{9,8},{10,11... | collective-permute-start | bytes 1179656 | tf_op jit(solution)/shard_map/ppermute | solution.py:298
  30.1 23.4 %collective-permute-start.6 = (bf16[256,512]{1,0:T(8,128)(2,1)S(1)}, bf16[256,512]{1,0:T(8,128)(2,1)S(1)}, u32[]{:S(2)}, u32[]{:S(2)}) collective-permute-start(bf16[256,512]{1,0:T(8,128)(2,1)S(1)} %get-tuple-element.42), channel_id=1, source_target_pairs={{0,1},{1,0},{2,3},{3,2},{4,5},{5,4},{6,7},{7,6},{8,9},{9,8},{10,11... | collective-permute-start | bytes 786440 | tf_op jit(solution)/shard_map/ppermute | solution.py:298
  32.4 24.9 %collective-permute-start.8 = (bf16[128,384]{1,0:T(8,128)(2,1)S(1)}, bf16[128,384]{1,0:T(8,128)(2,1)S(1)}, u32[]{:S(2)}, u32[]{:S(2)}) collective-permute-start(bf16[128,384]{1,0:T(8,128)(2,1)S(1)} %get-tuple-element.48), channel_id=1, source_target_pairs={{0,1},{1,0},{2,3},{3,2},{4,5},{5,4},{6,7},{7,6},{8,9},{9,8},{10,11... | collective-permute-start | bytes 294920 | tf_op jit(solution)/shard_map/ppermute | solution.py:298
  32.8 20.8 %copy-start = (s32[512]{0:T(512)S(1)}, s32[512]{0:T(512)}, u32[]{:S(2)}) copy-start(s32[512]{0:T(512)} %param.3) | copy-start | bytes 6148
  51.1 6.2 %collective-permute-start.10 = (bf16[128,256]{1,0:T(8,128)(2,1)S(1)}, bf16[128,256]{1,0:T(8,128)(2,1)S(1)}, u32[]{:S(2)}, u32[]{:S(2)}) collective-permute-start(bf16[128,256]{1,0:T(8,128)(2,1)S(1)} %get-tuple-element.51), channel_id=1, source_target_pairs={{0,1},{1,0},{2,3},{3,2},{4,5},{5,4},{6,7},{7,6},{8,9},{9,8},{10,11... | collective-permute-start | bytes 196616 | tf_op jit(solution)/shard_map/ppermute | solution.py:298
  53.0 4.3 %collective-permute-start.12 = (bf16[128,128]{1,0:T(8,128)(2,1)S(1)}, bf16[128,128]{1,0:T(8,128)(2,1)S(1)}, u32[]{:S(2)}, u32[]{:S(2)}) collective-permute-start(bf16[128,128]{1,0:T(8,128)(2,1)S(1)} %get-tuple-element.53), channel_id=1, source_target_pairs={{0,1},{1,0},{2,3},{3,2},{4,5},{5,4},{6,7},{7,6},{8,9},{9,8},{10,11... | collective-permute-start | bytes 98312 | tf_op jit(solution)/shard_map/ppermute | solution.py:298

commit v8 on v7

--- a/solution.py
+++ b/solution.py
@@ -91,7 +91,8 @@
 
 def own_kernel(
     share, haplo_total, rates, hap_ref, counts_ref,
-    std_ref, norm_ref, token_ref, high_ref, send_ref, low_ref, low_send_1, low_send_2,
+    std_ref, norm_ref, decay_ref, peer_ref, token_ref,
+    high_ref, send_ref, low_ref, low_send_1, low_send_2,
 ):
     token_ref[...] = jnp.zeros_like(token_ref)
     std_ref[...] = standardize_part(hap_ref, counts_ref, 0, haplo_total)
@@ -107,9 +108,28 @@
     low_ref[:half, :half] = low
     low_send_2[...] = low.astype(jnp.bfloat16)
     me = lax.axis_index("genome") * lax.axis_size("samples") + mine
-    position = (me * share + lax.broadcasted_iota(jnp.int32, (1, share), 1)).astype(jnp.float32) + 1.0
+    step = lax.broadcasted_iota(jnp.int32, (1, share), 1)
+    position = (me * share + step).astype(jnp.float32) + 1.0
+    source = lax.broadcasted_iota(jnp.int32, (LANES, LANES), 0)
+    target = lax.broadcasted_iota(jnp.int32, (LANES, LANES), 1)
+    lag = (target - source).astype(jnp.float32)
+    to_end = (LANES - 1 - source).astype(jnp.float32)
+    peer = lax.broadcasted_iota(jnp.int32, peer_ref.shape, 0)
+    peer_lane = lax.broadcasted_iota(jnp.int32, peer_ref.shape, 1)
+    gap = jnp.maximum((me - 1 - peer) * share, 0).astype(jnp.float32)
+    peer_weight = jnp.zeros(peer_ref.shape, jnp.float32)
     for k, rate in enumerate(rates):
-        norm_ref[k : k + 1, :] = math.expm1(rate) / expm1(position * rate)
+        norm = math.expm1(rate) / expm1(position * rate)
+        norm_ref[k : k + 1, :] = norm
+        norm_ref[2 + k : 3 + k, :] = norm * jnp.exp((step.astype(jnp.float32) + 1.0) * rate)
+        at = 2 * k * LANES
+        decay_ref[:, at : at + LANES] = jnp.where(
+            lag >= 0.0, jnp.exp(jnp.maximum(lag, 0.0) * rate), 0.0
+        )
+        decay_ref[:, at + LANES : at + 2 * LANES] = jnp.exp(to_end * rate)
+        used = (peer < me) & (peer_lane == k)
+        peer_weight = peer_weight + jnp.where(used, jnp.exp(gap * rate), 0.0)
+    peer_ref[...] = peer_weight
 
 
 def first_kernel(
@@ -209,7 +229,7 @@
     return (math.log(0.5) / (4 * share), math.log(0.1) / variants)
 
 
-def tail_kernel(share, haplo_total, pieces, rates, ends_ref, sums_ref, *refs):
+def tail_kernel(share, haplo_total, pieces, rates, ends_ref, sums_ref, decay_ref, *refs):
     score_ref, local_ref, last_ref, total_ref = refs[-4:]
     mine = lax.axis_index("samples")
     ends = local_ends(ends_ref, share)
@@ -225,24 +245,18 @@
         + ([jnp.zeros(((-blocks) % 8, LANES), jnp.float32)] if blocks % 8 else []),
         axis=0,
     )
-    source = lax.broadcasted_iota(jnp.int32, (LANES, LANES), 0)
-    target = lax.broadcasted_iota(jnp.int32, (LANES, LANES), 1)
-    lag = (target - source).astype(jnp.float32)
     lane = lax.broadcasted_iota(jnp.int32, (1, LANES), 1).astype(jnp.float32)
+    within = lax.dot_general(
+        stacked,
+        decay_ref[...],
+        (((1,), (0,)), ((), ())),
+        precision=lax.Precision.HIGHEST,
+        preferred_element_type=jnp.float32,
+    )
     lasts = []
     for k, rate in enumerate(rates):
-        weight = jnp.where(lag >= 0.0, jnp.exp(jnp.maximum(lag, 0.0) * rate), 0.0)
-        to_end = jnp.exp((LANES - 1.0 - source.astype(jnp.float32)) * rate)
-        inner, ending = (
-            lax.dot_general(
-                stacked,
-                w,
-                (((1,), (0,)), ((), ())),
-                precision=lax.Precision.HIGHEST,
-                preferred_element_type=jnp.float32,
-            )
-            for w in (weight, to_end)
-        )
+        at = 2 * k * LANES
+        inner, ending = within[:, at : at + LANES], within[:, at + LANES : at + 2 * LANES]
         fall = jnp.exp((lane + 1.0) * rate)
         block_fall = math.exp(LANES * rate)
         carry = jnp.zeros((1, LANES), jnp.float32)
@@ -254,18 +268,33 @@
     last_ref[...] = jnp.where(tile_lane == 0, lasts[0], jnp.where(tile_lane == 1, lasts[1], 0.0))
 
 
-def finish_kernel(rates, local_ref, table_ref, norm_ref, profile_ref):
-    share = local_ref.shape[1]
-    peers = table_ref.shape[0]
-    me = lax.axis_index("genome") * lax.axis_size("samples") + lax.axis_index("samples")
-    peer = lax.broadcasted_iota(jnp.int32, (peers, LANES), 0)
-    gap = ((me - 1 - peer) * share).astype(jnp.float32)
-    step = lax.broadcasted_iota(jnp.int32, (1, share), 1).astype(jnp.float32)
-    for k, rate in enumerate(rates):
-        weight = jnp.where(peer < me, jnp.exp(jnp.maximum(gap, 0.0) * rate), 0.0)
-        incoming = jnp.sum(weight * table_ref[...], axis=0, keepdims=True)[:, k : k + 1]
-        smoothed = local_ref[k : k + 1, :] + incoming * jnp.exp((step + 1.0) * rate)
-        profile_ref[k : k + 1, :] = smoothed * norm_ref[k : k + 1, :]
+def finish_kernel(local_ref, table_ref, norm_ref, peer_ref, profile_ref):
+    incoming = jnp.sum(peer_ref[...] * table_ref[...], axis=0, keepdims=True)
+    for k in range(2):
+        profile_ref[k : k + 1, :] = (
+            local_ref[k : k + 1, :] * norm_ref[k : k + 1, :]
+            + incoming[:, k : k + 1] * norm_ref[2 + k : 3 + k, :]
+        )
+
+
+def peer_constants(rates, share, peers, me):
+    f32 = jnp.float32
+    log_rates = jnp.array(rates, f32)[:, None]
+    step = jnp.arange(share, dtype=jnp.int32)
+    position = (me * share + step).astype(f32)[None] + 1.0
+    norm = jnp.expm1(log_rates) / jnp.expm1(position * log_rates)
+    fall = jnp.exp((step.astype(f32)[None] + 1.0) * log_rates)
+    lane = jnp.arange(LANES, dtype=f32)
+    lag = lane[None] - lane[:, None]
+    decays = []
+    for rate in rates:
+        decays.append(jnp.where(lag >= 0.0, jnp.exp(jnp.maximum(lag, 0.0) * rate), 0.0))
+        decays.append(jnp.broadcast_to(jnp.exp((LANES - 1.0 - lane[:, None]) * rate), lag.shape))
+    peer = jnp.arange(peers, dtype=jnp.int32)
+    gap = jnp.maximum((me - 1 - peer) * share, 0).astype(f32)
+    weight = jnp.where(peer[None] < me, jnp.exp(gap[None] * log_rates), 0.0).T
+    weight = jnp.pad(weight, ((0, 0), (0, LANES - len(rates))))
+    return jnp.concatenate([norm, norm * fall]), jnp.concatenate(decays, axis=1), weight
 
 
 def per_device(haplotypes, window_ends):
@@ -301,9 +330,10 @@
     token_type = ((8, LANES), f32)
     if samples == 2:
         half, u, whole = share // 2, unit, slice(None)
-        standard, norm, token, high, send, low, low_send_1, low_send_2 = call(
+        standard, norm, decay, peer, token, high, send, low, low_send_1, low_send_2 = call(
             functools.partial(own_kernel, share, haplo_total, rates),
-            [((depth, width), bf16), ((2, share), f32), token_type]
+            [((depth, width), bf16), ((4, share), f32), ((LANES, 4 * LANES), f32)]
+            + [((genome * samples, LANES), f32), token_type]
             + [((share, share), f32), ((share, share), bf16), ((share, share), f32)]
             + [((half, share), bf16), ((half, half), bf16)],
             haplotypes,
@@ -393,9 +423,7 @@
             tiled=True,
         )
         me = lax.axis_index("genome") * samples + lax.axis_index("samples")
-        position = (me * share + jnp.arange(share, dtype=jnp.int32)).astype(f32) + 1.0
-        log_rates = jnp.array(rates, f32)[:, None]
-        norm = jnp.expm1(log_rates) / jnp.expm1(position[None] * log_rates)
+        norm, decay, peer = peer_constants(rates, share, genome * samples, me)
         sums = window_sums(
             total,
             haplo_total,
@@ -409,12 +437,11 @@
         [((1, share), f32), ((2, share), f32), ((genome * samples, LANES), f32), ((1, share), f32)],
         ends,
         sums,
+        decay,
         *tails,
     )
     table = lax.all_to_all(last[:, None], ("genome", "samples"), 0, 0, tiled=True)[:, 0]
-    (profile,) = call(
-        functools.partial(finish_kernel, rates), [((2, share), f32)], local, table, norm
-    )
+    (profile,) = call(finish_kernel, [((2, share), f32)], local, table, norm, peer)
     return score[0], profile
 
 

time: 101 us -> 101 us (level)
  no operation moved by 1% of the time
where the time goes in v8:
time: 101 us; the launch traced here: 100 us
  blocking collectives  41.5 us (41%)
  waiting for transfers between devices  25.1 us (25%)
  starting transfers between devices  17.2 us (17%)
  Pallas kernels  13.7 us (14%)
  local copies, waits for them, and re-layouts  1.98 us (2%)
    all_to_all x1, blocking collectives, per_device(): lax.all_to_all(last[:, None], ('genome', 'samples'), 0, 0, tiled=True)[:, 0]  41.5 us
    ppermute x5, waiting for transfers between devices, shifted(): lax.ppermute(array[:, firsts[c]:firsts[c] + sizes[c]], 'genome', back)  17.4 us
    pallas_call x9, Pallas kernels, call(): pl.pallas_call(kernel, in_specs=[pl.BlockSpec(memory_space=pltpu.VMEM)] *...  11.3 us
    ppermute x5, starting transfers between devices, shifted(): lax.ppermute(array[:, firsts[c]:firsts[c] + sizes[c]], 'genome', back)  6.45 us
    ppermute x6, starting transfers between devices, swap(): return lax.ppermute(send, 'samples', [(0, 1), (1, 0)])  6.41 us
    ppermute x1, waiting for transfers between devices, per_device(): next_counts = lax.ppermute(counts, 'genome', back)  3.4 us
    ppermute x1, starting transfers between devices, per_device(): counts = counts + lax.ppermute(counts, 'samples', [(0, 1), (1, 0)])  3.06 us
    ppermute x6, waiting for transfers between devices, swap(): return lax.ppermute(send, 'samples', [(0, 1), (1, 0)])  2.69 us
  transfers between devices with their start and end apart: 13, of which 4 were waited for; matrix products, arithmetic and copies ran while one was open for 0% of the time, Pallas kernels for 12%

profile of v8, /device:TPU:0, one launch (start us, length us, event | category | flops | bytes accessed | tf_op | source)
XLA Modules:
  0.0 100.3 jit_solution(15993405844391009798)
XLA Ops:
  0.6 1.6 %slice.15 = bf16[2048,384]{1,0:T(8,128)(2,1)S(1)} slice(bf16[2048,1024]{1,0:T(8,128)(2,1)} %hap_hbm.1), slice={[0:2048], [0:384]} | slice | bytes 3145728 | tf_op jit(solution)/shard_map/slice | solution.py:315
  2.2 1.3 %collective-permute-start.2 = (bf16[2048,384]{1,0:T(8,128)(2,1)S(1)}, bf16[2048,384]{1,0:T(8,128)(2,1)S(1)}, u32[]{:S(2)}, u32[]{:S(2)}) collective-permute-start(bf16[2048,384]{1,0:T(8,128)(2,1)S(1)} %slice.15), channel_id=1, source_target_pairs={{2,0},{4,2},{6,4},{8,6},{10,8},{12,10},{14,12},{16,14},{18,16},{20... | collective-permute-start | bytes 4718600 | tf_op jit(solution)/shard_map/ppermute | solution.py:315
  3.5 2.4 %local_counts.1 = (bf16[2048,1024]{1,0:T(8,128)(2,1)S(1)}, f32[1,1024]{1,0:T(1,128)S(1)}) custom-call(bf16[2048,1024]{1,0:T(8,128)(2,1)} %hap_hbm.1), custom_call_target="tpu_custom_call" | custom-call | tf_op jit(solution)/shard_map/local_counts/pallas_call | solution.py:73
  5.9 0.1 slice.16
  6.1 1.3 %collective-permute-start.5 = (bf16[2048,256]{1,0:T(8,128)(2,1)S(1)}, bf16[2048,256]{1,0:T(8,128)(2,1)S(1)}, u32[]{:S(2)}, u32[]{:S(2)}) collective-permute-start(bf16[2048,256]{1,0:T(8,128)(2,1)S(1)} %slice.16), channel_id=1, source_target_pairs={{2,0},{4,2},{6,4},{8,6},{10,8},{12,10},{14,12},{16,14},{18,16},{20... | collective-permute-start | bytes 3145736 | tf_op jit(solution)/shard_map/ppermute | solution.py:315
  7.4 0.3 fusion
  7.6 1.3 %collective-permute-start.7 = (bf16[2048,128]{1,0:T(8,128)(2,1)S(1)}, bf16[2048,128]{1,0:T(8,128)(2,1)S(1)}, u32[]{:S(2)}, u32[]{:S(2)}) collective-permute-start(bf16[2048,128]{1,0:T(8,128)(2,1)S(1)} %get-tuple-element.64), channel_id=1, source_target_pairs={{2,0},{4,2},{6,4},{8,6},{10,8},{12,10},{14,12},{16,14},{18,16},{20... | collective-permute-start | bytes 1572872 | tf_op jit(solution)/shard_map/ppermute | solution.py:315
  8.9 1.3 %collective-permute-start.9 = (bf16[2048,128]{1,0:T(8,128)(2,1)S(1)}, bf16[2048,128]{1,0:T(8,128)(2,1)S(1)}, u32[]{:S(2)}, u32[]{:S(2)}) collective-permute-start(bf16[2048,128]{1,0:T(8,128)(2,1)S(1)} %get-tuple-element.63), channel_id=1, source_target_pairs={{2,0},{4,2},{6,4},{8,6},{10,8},{12,10},{14,12},{16,14},{18,16},{20... | collective-permute-start | bytes 1572872 | tf_op jit(solution)/shard_map/ppermute | solution.py:315
  10.2 3.1 %collective-permute-start = (f32[1,1024]{1,0:T(1,128)S(1)}, f32[1,1024]{1,0:T(1,128)S(1)}, u32[]{:S(2)}, u32[]{:S(2)}) collective-permute-start(f32[1,1024]{1,0:T(1,128)S(1)} %get-tuple-element.33), channel_id=1, source_target_pairs={{0,1},{1,0},{2,3},{3,2},{4,5},{5,4},{6,7},{7,6},{8,9},{9,8},{10,11... | collective-permute-start | bytes 12296 | tf_op jit(solution)/shard_map/ppermute | solution.py:321
  13.3 1.6 %collective-permute-done = f32[1,1024]{1,0:T(1,128)S(1)} collective-permute-done((f32[1,1024]{1,0:T(1,128)S(1)}, f32[1,1024]{1,0:T(1,128)S(1)}, u32[]{:S(2)}, u32[]{:S(2)}) %collective-permute-start) | collective-permute-done | bytes 4128 | tf_op jit(solution)/shard_map/ppermute | solution.py:321
  14.9 1.3 %collective-permute-start.3 = (f32[1,1024]{1,0:T(1,128)S(1)}, f32[1,1024]{1,0:T(1,128)S(1)}, u32[]{:S(2)}, u32[]{:S(2)}) collective-permute-start(f32[1,1024]{1,0:T(1,128)S(1)} %add.3.counts_ref), channel_id=1, source_target_pairs={{2,0},{4,2},{6,4},{8,6},{10,8},{12,10},{14,12},{16,14},{18,16},{20... | collective-permute-start | bytes 12296 | tf_op jit(solution)/shard_map/ppermute | solution.py:324
  16.2 3.4 %collective-permute-done.3.counts_ref = f32[1,1024]{1,0:T(1,128)S(1)} collective-permute-done((f32[1,1024]{1,0:T(1,128)S(1)}, f32[1,1024]{1,0:T(1,128)S(1)}, u32[]{:S(2)}, u32[]{:S(2)}) %collective-permute-start.3) | collective-permute-done | bytes 4128 | tf_op jit(solution)/shard_map/ppermute | solution.py:324
  19.6 1.3 %collective-permute-start.11 = (bf16[2048,128]{1,0:T(8,128)(2,1)S(1)}, bf16[2048,128]{1,0:T(8,128)(2,1)S(1)}, u32[]{:S(2)}, u32[]{:S(2)}) collective-permute-start(bf16[2048,128]{1,0:T(8,128)(2,1)S(1)} %get-tuple-element.62), channel_id=1, source_target_pairs={{2,0},{4,2},{6,4},{8,6},{10,8},{12,10},{14,12},{16,14},{18,16},{20... | collective-permute-start | bytes 1572872 | tf_op jit(solution)/shard_map/ppermute | solution.py:315
  20.9 4.2 %shard_map.41 = (bf16[2048,1024]{1,0:T(8,128)(2,1)S(1)}, f32[4,512]{1,0:T(4,128)S(1)}, f32[128,512]{1,0:T(8,128)S(1)}, f32[32,128]{1,0:T(8,128)S(1)}, f32[8,128]...) custom-call(bf16[2048,1024]{1,0:T(8,128)(2,1)S(1)} %get-tuple-elemen, ...), custom_call_target="tpu_custom_call" | custom-call | tf_op jit(solution)/shard_map/pallas_call | solution.py:34
  25.1 0.0 collective-permute-done.2.raw_ref
  25.1 1.8 %collective-permute-start.1 = (bf16[512,512]{1,0:T(8,128)(2,1)S(1)}, bf16[512,512]{1,0:T(8,128)(2,1)S(1)}, u32[]{:S(2)}, u32[]{:S(2)}) collective-permute-start(bf16[512,512]{1,0:T(8,128)(2,1)S(1)} %get-tuple-element.35), channel_id=1, source_target_pairs={{0,1},{1,0},{2,3},{3,2},{4,5},{5,4},{6,7},{7,6},{8,9},{9,8},{10,11... | collective-permute-start | bytes 1572872 | tf_op jit(solution)/shard_map/ppermute | solution.py:327
  26.9 1.8 %shard_map.42 = (f32[8,128]{1,0:T(8,128)S(1)}, f32[384,512]{1,0:T(8,128)S(1)}, bf16[384,512]{1,0:T(8,128)(2,1)S(1)}) custom-call(bf16[2048,384]{1,0:T(8,128)(2,1)S(1)} %collective-permute-done.2.raw_ref, f32[1,1024]{1,0:T(1,128)S(1)} %collective-permute-done.3.counts_ref, bf16[2048,1024]{1,0:T(8,128)(2,1)S(1)} %get-tuple-element.36.std_ref, ...), custom_call_target="tpu_custom_call" | custom-call | tf_op jit(solution)/shard_map/pallas_call | solution.py:34
  28.8 0.0 collective-permute-done.5.raw_ref
  28.8 0.3 collective-permute-start.4
  29.1 0.9 shard_map.43
  30.1 0.0 collective-permute-done.7.raw_ref
  30.1 1.8 %collective-permute-start.6 = (bf16[256,512]{1,0:T(8,128)(2,1)S(1)}, bf16[256,512]{1,0:T(8,128)(2,1)S(1)}, u32[]{:S(2)}, u32[]{:S(2)}) collective-permute-start(bf16[256,512]{1,0:T(8,128)(2,1)S(1)} %get-tuple-element.44), channel_id=1, source_target_pairs={{0,1},{1,0},{2,3},{3,2},{4,5},{5,4},{6,7},{7,6},{8,9},{9,8},{10,11... | collective-permute-start | bytes 786440 | tf_op jit(solution)/shard_map/ppermute | solution.py:327
  31.9 0.5 shard_map.45
  32.4 0.0 collective-permute-done.9.raw_ref
  32.4 0.3 collective-permute-start.8
  32.7 0.0 copy-start
  32.7 1.0 shard_map.46
  33.7 17.4 %collective-permute-done.11.raw_ref = bf16[2048,128]{1,0:T(8,128)(2,1)S(1)} collective-permute-done((bf16[2048,128]{1,0:T(8,128)(2,1)S(1)}, bf16[2048,128]{1,0:T(8,128)(2,1)S(1)}, u32[]{:S(2)}, u32[]{:S(2)}) %collective-permute-start.11) | collective-permute-done | bytes 524320 | tf_op jit(solution)/shard_map/ppermute | solution.py:315
  51.1 1.5 %collective-permute-start.10 = (bf16[128,256]{1,0:T(8,128)(2,1)S(1)}, bf16[128,256]{1,0:T(8,128)(2,1)S(1)}, u32[]{:S(2)}, u32[]{:S(2)}) collective-permute-start(bf16[128,256]{1,0:T(8,128)(2,1)S(1)} %get-tuple-element.54), channel_id=1, source_target_pairs={{0,1},{1,0},{2,3},{3,2},{4,5},{5,4},{6,7},{7,6},{8,9},{9,8},{10,11... | collective-permute-start | bytes 196616 | tf_op jit(solution)/shard_map/ppermute | solution.py:327
  52.6 0.4 shard_map.47
  53.0 0.0 collective-permute-done.1.refs_1_
  53.0 0.6 collective-permute-start.12
  53.6 0.0 collective-permute-done.6.refs_6_
  53.6 0.0 collective-permute-done.4.refs_3_
  53.6 0.0 copy-done
  53.6 1.0 %shard_map.44.sums_ref = f32[1,512]{1,0:T(1,128)S(1)} custom-call(s32[1,512]{1,0:T(1,128)S(1)} %bitcast.8, f32[512,512]{1,0:T(8,128)S(1)} %get-tuple-element.34.refs_0_, bf16[512,512]{1,0:T(8,128)(2,1)S(1)} %collective-permute-done.1.refs_1_, f32[384,512]{1,0:T(8,128)S(1)} %get-tuple-element.38.refs_2_, bf16[384,512]{1,0:T(8,128)(2,1)S(1)} %collective-permute-done.4.refs_3_, ...), custom_call_target="tpu_custom_call" | custom-call | tf_op jit(solution)/shard_map/pallas_call | solution.py:34
  54.6 2.7 %collective-permute-done.12.refs_7_ = bf16[128,128]{1,0:T(8,128)(2,1)S(1)} collective-permute-done((bf16[128,128]{1,0:T(8,128)(2,1)S(1)}, bf16[128,128]{1,0:T(8,128)(2,1)S(1)}, u32[]{:S(2)}, u32[]{:S(2)}) %collective-permute-start.12) | collective-permute-done | bytes 32800 | tf_op jit(solution)/shard_map/ppermute | solution.py:327
  57.3 0.0 collective-permute-done.10.refs_5_
  57.3 0.0 collective-permute-done.8.refs_3_
  57.3 0.8 shard_map.48
  58.1 41.5 %all_to_all.5 = f32[32,1,128]{2,1,0:T(1,128)S(1)} all-to-all(f32[32,1,128]{2,1,0:T(1,128)S(1)} %bitcast.7), channel_id=1, replica_groups=mesh['genome'=16,'samples'=2] {'genome','samples'}, dimensions={0} | all-to-all | bytes 32768 | tf_op jit(solution)/shard_map/all_to_all | solution.py:443
  99.6 0.7 shard_map.49
  (1 shorter events, 0.0 us)
Async XLA Ops:
  2.2 22.9 %collective-permute-start.2 = (bf16[2048,384]{1,0:T(8,128)(2,1)S(1)}, bf16[2048,384]{1,0:T(8,128)(2,1)S(1)}, u32[]{:S(2)}, u32[]{:S(2)}) collective-permute-start(bf16[2048,384]{1,0:T(8,128)(2,1)S(1)} %slice.15), channel_id=1, source_target_pairs={{2,0},{4,2},{6,4},{8,6},{10,8},{12,10},{14,12},{16,14},{18,16},{20... | collective-permute-start | bytes 4718600 | tf_op jit(solution)/shard_map/ppermute | solution.py:315
  6.1 22.7 %collective-permute-start.5 = (bf16[2048,256]{1,0:T(8,128)(2,1)S(1)}, bf16[2048,256]{1,0:T(8,128)(2,1)S(1)}, u32[]{:S(2)}, u32[]{:S(2)}) collective-permute-start(bf16[2048,256]{1,0:T(8,128)(2,1)S(1)} %slice.16), channel_id=1, source_target_pairs={{2,0},{4,2},{6,4},{8,6},{10,8},{12,10},{14,12},{16,14},{18,16},{20... | collective-permute-start | bytes 3145736 | tf_op jit(solution)/shard_map/ppermute | solution.py:315
  7.6 22.4 %collective-permute-start.7 = (bf16[2048,128]{1,0:T(8,128)(2,1)S(1)}, bf16[2048,128]{1,0:T(8,128)(2,1)S(1)}, u32[]{:S(2)}, u32[]{:S(2)}) collective-permute-start(bf16[2048,128]{1,0:T(8,128)(2,1)S(1)} %get-tuple-element.64), channel_id=1, source_target_pairs={{2,0},{4,2},{6,4},{8,6},{10,8},{12,10},{14,12},{16,14},{18,16},{20... | collective-permute-start | bytes 1572872 | tf_op jit(solution)/shard_map/ppermute | solution.py:315
  8.9 23.5 %collective-permute-start.9 = (bf16[2048,128]{1,0:T(8,128)(2,1)S(1)}, bf16[2048,128]{1,0:T(8,128)(2,1)S(1)}, u32[]{:S(2)}, u32[]{:S(2)}) collective-permute-start(bf16[2048,128]{1,0:T(8,128)(2,1)S(1)} %get-tuple-element.63), channel_id=1, source_target_pairs={{2,0},{4,2},{6,4},{8,6},{10,8},{12,10},{14,12},{16,14},{18,16},{20... | collective-permute-start | bytes 1572872 | tf_op jit(solution)/shard_map/ppermute | solution.py:315
  10.2 4.6 %collective-permute-start = (f32[1,1024]{1,0:T(1,128)S(1)}, f32[1,1024]{1,0:T(1,128)S(1)}, u32[]{:S(2)}, u32[]{:S(2)}) collective-permute-start(f32[1,1024]{1,0:T(1,128)S(1)} %get-tuple-element.33), channel_id=1, source_target_pairs={{0,1},{1,0},{2,3},{3,2},{4,5},{5,4},{6,7},{7,6},{8,9},{9,8},{10,11... | collective-permute-start | bytes 12296 | tf_op jit(solution)/shard_map/ppermute | solution.py:321
  14.9 4.7 %collective-permute-start.3 = (f32[1,1024]{1,0:T(1,128)S(1)}, f32[1,1024]{1,0:T(1,128)S(1)}, u32[]{:S(2)}, u32[]{:S(2)}) collective-permute-start(f32[1,1024]{1,0:T(1,128)S(1)} %add.3.counts_ref), channel_id=1, source_target_pairs={{2,0},{4,2},{6,4},{8,6},{10,8},{12,10},{14,12},{16,14},{18,16},{20... | collective-permute-start | bytes 12296 | tf_op jit(solution)/shard_map/ppermute | solution.py:324
  19.6 31.5 %collective-permute-start.11 = (bf16[2048,128]{1,0:T(8,128)(2,1)S(1)}, bf16[2048,128]{1,0:T(8,128)(2,1)S(1)}, u32[]{:S(2)}, u32[]{:S(2)}) collective-permute-start(bf16[2048,128]{1,0:T(8,128)(2,1)S(1)} %get-tuple-element.62), channel_id=1, source_target_pairs={{2,0},{4,2},{6,4},{8,6},{10,8},{12,10},{14,12},{16,14},{18,16},{20... | collective-permute-start | bytes 1572872 | tf_op jit(solution)/shard_map/ppermute | solution.py:315
  25.1 27.9 %collective-permute-start.1 = (bf16[512,512]{1,0:T(8,128)(2,1)S(1)}, bf16[512,512]{1,0:T(8,128)(2,1)S(1)}, u32[]{:S(2)}, u32[]{:S(2)}) collective-permute-start(bf16[512,512]{1,0:T(8,128)(2,1)S(1)} %get-tuple-element.35), channel_id=1, source_target_pairs={{0,1},{1,0},{2,3},{3,2},{4,5},{5,4},{6,7},{7,6},{8,9},{9,8},{10,11... | collective-permute-start | bytes 1572872 | tf_op jit(solution)/shard_map/ppermute | solution.py:327
  28.8 24.8 %collective-permute-start.4 = (bf16[384,512]{1,0:T(8,128)(2,1)S(1)}, bf16[384,512]{1,0:T(8,128)(2,1)S(1)}, u32[]{:S(2)}, u32[]{:S(2)}) collective-permute-start(bf16[384,512]{1,0:T(8,128)(2,1)S(1)} %get-tuple-element.39), channel_id=1, source_target_pairs={{0,1},{1,0},{2,3},{3,2},{4,5},{5,4},{6,7},{7,6},{8,9},{9,8},{10,11... | collective-permute-start | bytes 1179656 | tf_op jit(solution)/shard_map/ppermute | solution.py:327
  30.1 23.5 %collective-permute-start.6 = (bf16[256,512]{1,0:T(8,128)(2,1)S(1)}, bf16[256,512]{1,0:T(8,128)(2,1)S(1)}, u32[]{:S(2)}, u32[]{:S(2)}) collective-permute-start(bf16[256,512]{1,0:T(8,128)(2,1)S(1)} %get-tuple-element.44), channel_id=1, source_target_pairs={{0,1},{1,0},{2,3},{3,2},{4,5},{5,4},{6,7},{7,6},{8,9},{9,8},{10,11... | collective-permute-start | bytes 786440 | tf_op jit(solution)/shard_map/ppermute | solution.py:327
  32.4 24.9 %collective-permute-start.8 = (bf16[128,384]{1,0:T(8,128)(2,1)S(1)}, bf16[128,384]{1,0:T(8,128)(2,1)S(1)}, u32[]{:S(2)}, u32[]{:S(2)}) collective-permute-start(bf16[128,384]{1,0:T(8,128)(2,1)S(1)} %get-tuple-element.51), channel_id=1, source_target_pairs={{0,1},{1,0},{2,3},{3,2},{4,5},{5,4},{6,7},{7,6},{8,9},{9,8},{10,11... | collective-permute-start | bytes 294920 | tf_op jit(solution)/shard_map/ppermute | solution.py:327
  32.7 20.8 %copy-start = (s32[512]{0:T(512)S(1)}, s32[512]{0:T(512)}, u32[]{:S(2)}) copy-start(s32[512]{0:T(512)} %param.3) | copy-start | bytes 6148
  51.1 6.2 %collective-permute-start.10 = (bf16[128,256]{1,0:T(8,128)(2,1)S(1)}, bf16[128,256]{1,0:T(8,128)(2,1)S(1)}, u32[]{:S(2)}, u32[]{:S(2)}) collective-permute-start(bf16[128,256]{1,0:T(8,128)(2,1)S(1)} %get-tuple-element.54), channel_id=1, source_target_pairs={{0,1},{1,0},{2,3},{3,2},{4,5},{5,4},{6,7},{7,6},{8,9},{9,8},{10,11... | collective-permute-start | bytes 196616 | tf_op jit(solution)/shard_map/ppermute | solution.py:327
  53.0 4.3 %collective-permute-start.12 = (bf16[128,128]{1,0:T(8,128)(2,1)S(1)}, bf16[128,128]{1,0:T(8,128)(2,1)S(1)}, u32[]{:S(2)}, u32[]{:S(2)}) collective-permute-start(bf16[128,128]{1,0:T(8,128)(2,1)S(1)} %get-tuple-element.56), channel_id=1, source_target_pairs={{0,1},{1,0},{2,3},{3,2},{4,5},{5,4},{6,7},{7,6},{8,9},{9,8},{10,11... | collective-permute-start | bytes 98312 | tf_op jit(solution)/shard_map/ppermute | solution.py:327

commit v9 on v8

--- a/solution.py
+++ b/solution.py
@@ -67,6 +67,35 @@
         copy.wait()
         block = hap_ref[k * rows : (k + 1) * rows, :].astype(jnp.float32)
         out_ref[...] += jnp.sum(block, axis=0, keepdims=True)
+
+
+def cut_kernel(first, hap_hbm, out_ref, arrived):
+    parts = arrived.shape[0]
+    rows, size = out_ref.shape[0] // parts, out_ref.shape[1]
+    copies = [
+        pltpu.make_async_copy(
+            hap_hbm.at[pl.ds(k * rows, rows), pl.ds(first, size)],
+            out_ref.at[pl.ds(k * rows, rows)],
+            arrived.at[k],
+        )
+        for k in range(parts)
+    ]
+    for copy in copies:
+        copy.start()
+    for copy in copies:
+        copy.wait()
+
+
+def cut(haplotypes, first, size):
+    return pl.pallas_call(
+        functools.partial(cut_kernel, first),
+        in_specs=[pl.BlockSpec(memory_space=pltpu.HBM)],
+        out_specs=pl.BlockSpec(memory_space=pltpu.VMEM),
+        out_shape=jax.ShapeDtypeStruct((haplotypes.shape[0], size), haplotypes.dtype),
+        scratch_shapes=[pltpu.SemaphoreType.DMA((4,))],
+        compiler_params=pltpu.CompilerParams(vmem_limit_bytes=VMEM_LIMIT),
+        name="cut",
+    )(pltpu.with_memory_space_constraint(haplotypes, pltpu.HBM))
 
 
 def load(haplotypes):
@@ -304,7 +333,7 @@
     share = width // samples
     haplo_total = float(depth * samples)
     rates = rates_of(share, width * genome)
-    back = [(i + 1, i) for i in range(genome - 1)]
+    back = [((i + 1) % genome, i) for i in range(genome)]
     ends = window_ends[None]
     f32, bf16 = jnp.float32, jnp.bfloat16
     unit = width // 8
@@ -314,7 +343,8 @@
     def shifted(array, c):
         return lax.ppermute(array[:, firsts[c] : firsts[c] + sizes[c]], "genome", back)
 
-    raws = [shifted(haplotypes, 0)]
+    opening = cut(haplotypes, 0, sizes[0])
+    raws = [lax.ppermute(opening, "genome", back)]
     haplotypes, counts = load(haplotypes)
     raws += [shifted(haplotypes, c) for c in range(1, len(EIGHTHS))]
     if samples == 2:

time: 101 us -> 97.2 us (0.962)
  blocking collectives: 41.5 us -> 10.7 us
  waiting for transfers between devices: 25.1 us -> 49.6 us
  starting transfers between devices: 17.2 us -> 20.4 us
  local copies, waits for them, and re-layouts: 1.98 us -> 0.41 us
  Pallas kernels: 13.7 us -> 15.1 us
    all_to_all x1, blocking collectives: 41.5 us -> 10.7 us  [per_device(): lax.all_to_all(last[:, None], ('genome', 'samples'), 0, 0, tiled=True)[:, 0]]
    ppermute x1, waiting for transfers between devices: 3.4 us -> 32.6 us  [per_device(): next_counts = lax.ppermute(counts, 'genome', back)]
    ppermute x5 -> x4, waiting for transfers between devices: 17.4 us -> 0.01 us  [shifted(): lax.ppermute(array[:, firsts[c]:firsts[c] + sizes[c]], 'genome', back)]
    ppermute x6, waiting for transfers between devices: 2.69 us -> 15 us  [swap(): return lax.ppermute(send, 'samples', [(0, 1), (1, 0)])]
    ppermute x0 -> x1, starting transfers between devices: none -> 5.5 us  [per_device(): raws = [lax.ppermute(opening, 'genome', back)]]
    slice x3 -> x2, local copies, waits for them, and re-layouts: 1.98 us -> 0.41 us  [shifted(): array[:, firsts[c]:firsts[c] + sizes[c]]]
    ppermute x1, starting transfers between devices: 3.06 us -> 1.52 us  [per_device(): counts = counts + lax.ppermute(counts, 'samples', [(0, 1), (1, 0)])]
    pallas_call x0 -> x1, Pallas kernels: none -> 1.4 us  [cut(): pl.pallas_call(functools.partial(cut_kernel, first), in_specs=[pl.BlockSp...]
  transfers between devices with their start and end apart: 13 -> 13, of which waited for: 4 -> 5; matrix products, arithmetic and copies ran while one was open for 0% -> 0% of each run, Pallas kernels for 12% -> 13%
where the time goes in v9:
time: 97.2 us; the launch traced here: 97.1 us
  waiting for transfers between devices  49.6 us (51%)
  starting transfers between devices  20.4 us (21%)
  Pallas kernels  15.1 us (16%)
  blocking collectives  10.7 us (11%)
    ppermute x1, waiting for transfers between devices, per_device(): next_counts = lax.ppermute(counts, 'genome', back)  32.6 us
    ppermute x6, waiting for transfers between devices, swap(): return lax.ppermute(send, 'samples', [(0, 1), (1, 0)])  15 us
    pallas_call x9, Pallas kernels, call(): pl.pallas_call(kernel, in_specs=[pl.BlockSpec(memory_space=pltpu.VMEM)] *...  11.3 us
    all_to_all x1, blocking collectives, per_device(): lax.all_to_all(last[:, None], ('genome', 'samples'), 0, 0, tiled=True)[:, 0]  10.7 us
    ppermute x6, starting transfers between devices, swap(): return lax.ppermute(send, 'samples', [(0, 1), (1, 0)])  7.39 us
    ppermute x4, starting transfers between devices, shifted(): lax.ppermute(array[:, firsts[c]:firsts[c] + sizes[c]], 'genome', back)  6.03 us
    ppermute x1, starting transfers between devices, per_device(): raws = [lax.ppermute(opening, 'genome', back)]  5.5 us
    pallas_call x1, Pallas kernels, load(): pl.pallas_call(load_kernel, in_specs=[pl.BlockSpec(memory_space=pltpu.HBM...  2.41 us
  transfers between devices with their start and end apart: 13, of which 5 were waited for; matrix products, arithmetic and copies ran while one was open for 0% of the time, Pallas kernels for 13%

profile of v9, /device:TPU:0, one launch (start us, length us, event | category | flops | bytes accessed | tf_op | source)
XLA Modules:
  0.0 97.1 jit_solution(8245946419192942703)
XLA Ops:
  0.6 1.4 %cut.1 = bf16[2048,384]{1,0:T(8,128)(2,1)S(1)} custom-call(bf16[2048,1024]{1,0:T(8,128)(2,1)} %hap_hbm.3), custom_call_target="tpu_custom_call" | custom-call | tf_op jit(solution)/shard_map/cut/pallas_call | solution.py:90
  2.0 5.5 %collective-permute-start.2 = (bf16[2048,384]{1,0:T(8,128)(2,1)S(1)}, bf16[2048,384]{1,0:T(8,128)(2,1)S(1)}, u32[]{:S(2)}, u32[]{:S(2)}) collective-permute-start(bf16[2048,384]{1,0:T(8,128)(2,1)S(1)} %cut.1), channel_id=1, source_target_pairs={{2,0},{4,2},{6,4},{8,6},{10,8},{12,10},{14,12},{16,14},{18,16},{20... | collective-permute-start | bytes 4718600 | tf_op jit(solution)/shard_map/ppermute | solution.py:347
  7.5 2.4 %local_counts.1 = (bf16[2048,1024]{1,0:T(8,128)(2,1)S(1)}, f32[1,1024]{1,0:T(1,128)S(1)}) custom-call(bf16[2048,1024]{1,0:T(8,128)(2,1)} %hap_hbm.3), custom_call_target="tpu_custom_call" | custom-call | tf_op jit(solution)/shard_map/local_counts/pallas_call | solution.py:102
  10.0 0.1 slice.12
  10.1 0.7 collective-permute-start.5
  10.8 0.3 fusion
  11.1 0.1 collective-permute-start.7
  11.2 0.6 collective-permute-start.9
  11.8 1.5 %collective-permute-start = (f32[1,1024]{1,0:T(1,128)S(1)}, f32[1,1024]{1,0:T(1,128)S(1)}, u32[]{:S(2)}, u32[]{:S(2)}) collective-permute-start(f32[1,1024]{1,0:T(1,128)S(1)} %get-tuple-element.33), channel_id=1, source_target_pairs={{0,1},{1,0},{2,3},{3,2},{4,5},{5,4},{6,7},{7,6},{8,9},{9,8},{10,11... | collective-permute-start | bytes 12296 | tf_op jit(solution)/shard_map/ppermute | solution.py:351
  13.3 2.1 %collective-permute-done = f32[1,1024]{1,0:T(1,128)S(1)} collective-permute-done((f32[1,1024]{1,0:T(1,128)S(1)}, f32[1,1024]{1,0:T(1,128)S(1)}, u32[]{:S(2)}, u32[]{:S(2)}) %collective-permute-start) | collective-permute-done | bytes 4128 | tf_op jit(solution)/shard_map/ppermute | solution.py:351
  15.4 0.0 collective-permute-start.3
  15.4 32.6 %collective-permute-done.3.counts_ref = f32[1,1024]{1,0:T(1,128)S(1)} collective-permute-done((f32[1,1024]{1,0:T(1,128)S(1)}, f32[1,1024]{1,0:T(1,128)S(1)}, u32[]{:S(2)}, u32[]{:S(2)}) %collective-permute-start.3) | collective-permute-done | bytes 4128 | tf_op jit(solution)/shard_map/ppermute | solution.py:354
  48.0 4.6 %collective-permute-start.11 = (bf16[2048,128]{1,0:T(8,128)(2,1)S(1)}, bf16[2048,128]{1,0:T(8,128)(2,1)S(1)}, u32[]{:S(2)}, u32[]{:S(2)}) collective-permute-start(bf16[2048,128]{1,0:T(8,128)(2,1)S(1)} %get-tuple-element.62), channel_id=1, source_target_pairs={{2,0},{4,2},{6,4},{8,6},{10,8},{12,10},{14,12},{16,14},{18,16},{20... | collective-permute-start | bytes 1572872 | tf_op jit(solution)/shard_map/ppermute | solution.py:344
  52.6 4.2 %shard_map.41 = (bf16[2048,1024]{1,0:T(8,128)(2,1)S(1)}, f32[4,512]{1,0:T(4,128)S(1)}, f32[128,512]{1,0:T(8,128)S(1)}, f32[32,128]{1,0:T(8,128)S(1)}, f32[8,128]...) custom-call(bf16[2048,1024]{1,0:T(8,128)(2,1)S(1)} %get-tuple-elemen, ...), custom_call_target="tpu_custom_call" | custom-call | tf_op jit(solution)/shard_map/pallas_call | solution.py:34
  56.8 0.0 collective-permute-done.2.raw_ref
  56.8 1.6 %collective-permute-start.1 = (bf16[512,512]{1,0:T(8,128)(2,1)S(1)}, bf16[512,512]{1,0:T(8,128)(2,1)S(1)}, u32[]{:S(2)}, u32[]{:S(2)}) collective-permute-start(bf16[512,512]{1,0:T(8,128)(2,1)S(1)} %get-tuple-element.35), channel_id=1, source_target_pairs={{0,1},{1,0},{2,3},{3,2},{4,5},{5,4},{6,7},{7,6},{8,9},{9,8},{10,11... | collective-permute-start | bytes 1572872 | tf_op jit(solution)/shard_map/ppermute | solution.py:357
  58.4 1.8 %shard_map.42 = (f32[8,128]{1,0:T(8,128)S(1)}, f32[384,512]{1,0:T(8,128)S(1)}, bf16[384,512]{1,0:T(8,128)(2,1)S(1)}) custom-call(bf16[2048,384]{1,0:T(8,128)(2,1)S(1)} %collective-permute-done.2.raw_ref, f32[1,1024]{1,0:T(1,128)S(1)} %collective-permute-done.3.counts_ref, bf16[2048,1024]{1,0:T(8,128)(2,1)S(1)} %get-tuple-element.36.std_ref, ...), custom_call_target="tpu_custom_call" | custom-call | tf_op jit(solution)/shard_map/pallas_call | solution.py:34
  60.3 0.0 collective-permute-done.5.raw_ref
  60.3 0.5 collective-permute-start.4
  60.8 0.9 shard_map.43
  61.8 0.0 collective-permute-done.7.raw_ref
  61.8 1.6 %collective-permute-start.6 = (bf16[256,512]{1,0:T(8,128)(2,1)S(1)}, bf16[256,512]{1,0:T(8,128)(2,1)S(1)}, u32[]{:S(2)}, u32[]{:S(2)}) collective-permute-start(bf16[256,512]{1,0:T(8,128)(2,1)S(1)} %get-tuple-element.44), channel_id=1, source_target_pairs={{0,1},{1,0},{2,3},{3,2},{4,5},{5,4},{6,7},{7,6},{8,9},{9,8},{10,11... | collective-permute-start | bytes 786440 | tf_op jit(solution)/shard_map/ppermute | solution.py:357
  63.4 0.5 shard_map.45
  63.9 0.0 collective-permute-done.9.raw_ref
  63.9 0.5 collective-permute-start.8
  64.4 0.0 copy-start
  64.4 1.0 shard_map.46
  65.4 0.0 collective-permute-done.11.raw_ref
  65.4 1.5 %collective-permute-start.10 = (bf16[128,256]{1,0:T(8,128)(2,1)S(1)}, bf16[128,256]{1,0:T(8,128)(2,1)S(1)}, u32[]{:S(2)}, u32[]{:S(2)}) collective-permute-start(bf16[128,256]{1,0:T(8,128)(2,1)S(1)} %get-tuple-element.54), channel_id=1, source_target_pairs={{0,1},{1,0},{2,3},{3,2},{4,5},{5,4},{6,7},{7,6},{8,9},{9,8},{10,11... | collective-permute-start | bytes 196616 | tf_op jit(solution)/shard_map/ppermute | solution.py:357
  66.9 0.4 shard_map.47
  67.3 4.4 %collective-permute-done.1.refs_1_ = bf16[512,512]{1,0:T(8,128)(2,1)S(1)} collective-permute-done((bf16[512,512]{1,0:T(8,128)(2,1)S(1)}, bf16[512,512]{1,0:T(8,128)(2,1)S(1)}, u32[]{:S(2)}, u32[]{:S(2)}) %collective-permute-start.1) | collective-permute-done | bytes 524320 | tf_op jit(solution)/shard_map/ppermute | solution.py:357
  71.7 1.5 %collective-permute-start.12 = (bf16[128,128]{1,0:T(8,128)(2,1)S(1)}, bf16[128,128]{1,0:T(8,128)(2,1)S(1)}, u32[]{:S(2)}, u32[]{:S(2)}) collective-permute-start(bf16[128,128]{1,0:T(8,128)(2,1)S(1)} %get-tuple-element.56), channel_id=1, source_target_pairs={{0,1},{1,0},{2,3},{3,2},{4,5},{5,4},{6,7},{7,6},{8,9},{9,8},{10,11... | collective-permute-start | bytes 98312 | tf_op jit(solution)/shard_map/ppermute | solution.py:357
  73.2 9.6 %collective-permute-done.6.refs_6_ = bf16[256,512]{1,0:T(8,128)(2,1)S(1)} collective-permute-done((bf16[256,512]{1,0:T(8,128)(2,1)S(1)}, bf16[256,512]{1,0:T(8,128)(2,1)S(1)}, u32[]{:S(2)}, u32[]{:S(2)}) %collective-permute-start.6) | collective-permute-done | bytes 262176 | tf_op jit(solution)/shard_map/ppermute | solution.py:357
  82.8 0.0 collective-permute-done.4.refs_3_
  82.8 0.0 copy-done
  82.8 1.0 %shard_map.44.sums_ref = f32[1,512]{1,0:T(1,128)S(1)} custom-call(s32[1,512]{1,0:T(1,128)S(1)} %bitcast.8, f32[512,512]{1,0:T(8,128)S(1)} %get-tuple-element.34.refs_0_, bf16[512,512]{1,0:T(8,128)(2,1)S(1)} %collective-permute-done.1.refs_1_, f32[384,512]{1,0:T(8,128)S(1)} %get-tuple-element.38.refs_2_, bf16[384,512]{1,0:T(8,128)(2,1)S(1)} %collective-permute-done.4.refs_3_, ...), custom_call_target="tpu_custom_call" | custom-call | tf_op jit(solution)/shard_map/pallas_call | solution.py:34
  83.8 1.1 %collective-permute-done.12.refs_7_ = bf16[128,128]{1,0:T(8,128)(2,1)S(1)} collective-permute-done((bf16[128,128]{1,0:T(8,128)(2,1)S(1)}, bf16[128,128]{1,0:T(8,128)(2,1)S(1)}, u32[]{:S(2)}, u32[]{:S(2)}) %collective-permute-start.12) | collective-permute-done | bytes 32800 | tf_op jit(solution)/shard_map/ppermute | solution.py:357
  84.9 0.0 collective-permute-done.10.refs_5_
  84.9 0.0 collective-permute-done.8.refs_3_
  84.9 0.8 shard_map.48
  85.7 10.7 %all_to_all.5 = f32[32,1,128]{2,1,0:T(1,128)S(1)} all-to-all(f32[32,1,128]{2,1,0:T(1,128)S(1)} %bitcast.7), channel_id=1, replica_groups=mesh['genome'=16,'samples'=2] {'genome','samples'}, dimensions={0} | all-to-all | bytes 32768 | tf_op jit(solution)/shard_map/all_to_all | solution.py:473
  96.4 0.7 shard_map.49
  (1 shorter events, 0.0 us)
Async XLA Ops:
  2.0 54.8 %collective-permute-start.2 = (bf16[2048,384]{1,0:T(8,128)(2,1)S(1)}, bf16[2048,384]{1,0:T(8,128)(2,1)S(1)}, u32[]{:S(2)}, u32[]{:S(2)}) collective-permute-start(bf16[2048,384]{1,0:T(8,128)(2,1)S(1)} %cut.1), channel_id=1, source_target_pairs={{2,0},{4,2},{6,4},{8,6},{10,8},{12,10},{14,12},{16,14},{18,16},{20... | collective-permute-start | bytes 4718600 | tf_op jit(solution)/shard_map/ppermute | solution.py:347
  10.1 50.2 %collective-permute-start.5 = (bf16[2048,256]{1,0:T(8,128)(2,1)S(1)}, bf16[2048,256]{1,0:T(8,128)(2,1)S(1)}, u32[]{:S(2)}, u32[]{:S(2)}) collective-permute-start(bf16[2048,256]{1,0:T(8,128)(2,1)S(1)} %slice.12), channel_id=1, source_target_pairs={{2,0},{4,2},{6,4},{8,6},{10,8},{12,10},{14,12},{16,14},{18,16},{20... | collective-permute-start | bytes 3145736 | tf_op jit(solution)/shard_map/ppermute | solution.py:344
  11.1 50.7 %collective-permute-start.7 = (bf16[2048,128]{1,0:T(8,128)(2,1)S(1)}, bf16[2048,128]{1,0:T(8,128)(2,1)S(1)}, u32[]{:S(2)}, u32[]{:S(2)}) collective-permute-start(bf16[2048,128]{1,0:T(8,128)(2,1)S(1)} %get-tuple-element.64), channel_id=1, source_target_pairs={{2,0},{4,2},{6,4},{8,6},{10,8},{12,10},{14,12},{16,14},{18,16},{20... | collective-permute-start | bytes 1572872 | tf_op jit(solution)/shard_map/ppermute | solution.py:344
  11.2 52.7 %collective-permute-start.9 = (bf16[2048,128]{1,0:T(8,128)(2,1)S(1)}, bf16[2048,128]{1,0:T(8,128)(2,1)S(1)}, u32[]{:S(2)}, u32[]{:S(2)}) collective-permute-start(bf16[2048,128]{1,0:T(8,128)(2,1)S(1)} %get-tuple-element.63), channel_id=1, source_target_pairs={{2,0},{4,2},{6,4},{8,6},{10,8},{12,10},{14,12},{16,14},{18,16},{20... | collective-permute-start | bytes 1572872 | tf_op jit(solution)/shard_map/ppermute | solution.py:344
  11.8 3.6 %collective-permute-start = (f32[1,1024]{1,0:T(1,128)S(1)}, f32[1,1024]{1,0:T(1,128)S(1)}, u32[]{:S(2)}, u32[]{:S(2)}) collective-permute-start(f32[1,1024]{1,0:T(1,128)S(1)} %get-tuple-element.33), channel_id=1, source_target_pairs={{0,1},{1,0},{2,3},{3,2},{4,5},{5,4},{6,7},{7,6},{8,9},{9,8},{10,11... | collective-permute-start | bytes 12296 | tf_op jit(solution)/shard_map/ppermute | solution.py:351
  15.4 32.6 %collective-permute-start.3 = (f32[1,1024]{1,0:T(1,128)S(1)}, f32[1,1024]{1,0:T(1,128)S(1)}, u32[]{:S(2)}, u32[]{:S(2)}) collective-permute-start(f32[1,1024]{1,0:T(1,128)S(1)} %add.3.counts_ref), channel_id=1, source_target_pairs={{2,0},{4,2},{6,4},{8,6},{10,8},{12,10},{14,12},{16,14},{18,16},{20... | collective-permute-start | bytes 12296 | tf_op jit(solution)/shard_map/ppermute | solution.py:354
  48.0 17.4 %collective-permute-start.11 = (bf16[2048,128]{1,0:T(8,128)(2,1)S(1)}, bf16[2048,128]{1,0:T(8,128)(2,1)S(1)}, u32[]{:S(2)}, u32[]{:S(2)}) collective-permute-start(bf16[2048,128]{1,0:T(8,128)(2,1)S(1)} %get-tuple-element.62), channel_id=1, source_target_pairs={{2,0},{4,2},{6,4},{8,6},{10,8},{12,10},{14,12},{16,14},{18,16},{20... | collective-permute-start | bytes 1572872 | tf_op jit(solution)/shard_map/ppermute | solution.py:344
  56.8 14.9 %collective-permute-start.1 = (bf16[512,512]{1,0:T(8,128)(2,1)S(1)}, bf16[512,512]{1,0:T(8,128)(2,1)S(1)}, u32[]{:S(2)}, u32[]{:S(2)}) collective-permute-start(bf16[512,512]{1,0:T(8,128)(2,1)S(1)} %get-tuple-element.35), channel_id=1, source_target_pairs={{0,1},{1,0},{2,3},{3,2},{4,5},{5,4},{6,7},{7,6},{8,9},{9,8},{10,11... | collective-permute-start | bytes 1572872 | tf_op jit(solution)/shard_map/ppermute | solution.py:357
  60.3 22.5 %collective-permute-start.4 = (bf16[384,512]{1,0:T(8,128)(2,1)S(1)}, bf16[384,512]{1,0:T(8,128)(2,1)S(1)}, u32[]{:S(2)}, u32[]{:S(2)}) collective-permute-start(bf16[384,512]{1,0:T(8,128)(2,1)S(1)} %get-tuple-element.39), channel_id=1, source_target_pairs={{0,1},{1,0},{2,3},{3,2},{4,5},{5,4},{6,7},{7,6},{8,9},{9,8},{10,11... | collective-permute-start | bytes 1179656 | tf_op jit(solution)/shard_map/ppermute | solution.py:357
  61.8 21.0 %collective-permute-start.6 = (bf16[256,512]{1,0:T(8,128)(2,1)S(1)}, bf16[256,512]{1,0:T(8,128)(2,1)S(1)}, u32[]{:S(2)}, u32[]{:S(2)}) collective-permute-start(bf16[256,512]{1,0:T(8,128)(2,1)S(1)} %get-tuple-element.44), channel_id=1, source_target_pairs={{0,1},{1,0},{2,3},{3,2},{4,5},{5,4},{6,7},{7,6},{8,9},{9,8},{10,11... | collective-permute-start | bytes 786440 | tf_op jit(solution)/shard_map/ppermute | solution.py:357
  63.9 21.0 %collective-permute-start.8 = (bf16[128,384]{1,0:T(8,128)(2,1)S(1)}, bf16[128,384]{1,0:T(8,128)(2,1)S(1)}, u32[]{:S(2)}, u32[]{:S(2)}) collective-permute-start(bf16[128,384]{1,0:T(8,128)(2,1)S(1)} %get-tuple-element.51), channel_id=1, source_target_pairs={{0,1},{1,0},{2,3},{3,2},{4,5},{5,4},{6,7},{7,6},{8,9},{9,8},{10,11... | collective-permute-start | bytes 294920 | tf_op jit(solution)/shard_map/ppermute | solution.py:357
  64.4 18.3 %copy-start = (s32[512]{0:T(512)S(1)}, s32[512]{0:T(512)}, u32[]{:S(2)}) copy-start(s32[512]{0:T(512)} %param.3) | copy-start | bytes 6148
  65.4 19.5 %collective-permute-start.10 = (bf16[128,256]{1,0:T(8,128)(2,1)S(1)}, bf16[128,256]{1,0:T(8,128)(2,1)S(1)}, u32[]{:S(2)}, u32[]{:S(2)}) collective-permute-start(bf16[128,256]{1,0:T(8,128)(2,1)S(1)} %get-tuple-element.54), channel_id=1, source_target_pairs={{0,1},{1,0},{2,3},{3,2},{4,5},{5,4},{6,7},{7,6},{8,9},{9,8},{10,11... | collective-permute-start | bytes 196616 | tf_op jit(solution)/shard_map/ppermute | solution.py:357
  71.7 13.2 %collective-permute-start.12 = (bf16[128,128]{1,0:T(8,128)(2,1)S(1)}, bf16[128,128]{1,0:T(8,128)(2,1)S(1)}, u32[]{:S(2)}, u32[]{:S(2)}) collective-permute-start(bf16[128,128]{1,0:T(8,128)(2,1)S(1)} %get-tuple-element.56), channel_id=1, source_target_pairs={{0,1},{1,0},{2,3},{3,2},{4,5},{5,4},{6,7},{7,6},{8,9},{9,8},{10,11... | collective-permute-start | bytes 98312 | tf_op jit(solution)/shard_map/ppermute | solution.py:357
